TPU v7x, 256 devices: a whole 4x4x8 slice. The times are simulated.
256 devices in a mesh: row: 8 (over x, core), col: 32 (over y, z).
Axes of the slice: x: 4, y: 4, z: 8, core: 2. Of those that a mesh axis runs over, the one named last changes fastest.
Arguments:
- pooled: bfloat16 [16384, 1152], P(('row', 'col')), may hold values from -32 to 32
- hidden: bfloat16 [16384, 4304], P(('row', 'col')), may hold values from -6 to 6
- text: bfloat16 [16384, 1152], P(('row', 'col')), may hold values from -12 to 12
- weight: float32 [1152, 4304], P('col', 'row'), may hold values from -0.09375 to 0.09375
- row_moment: float32 [1152], P('col'), may hold values from 1e-07 to 1e-05
- col_moment: float32 [4304], P('row'), may hold values from 1e-07 to 1e-05
- log_scale: float32 [], replicated, may hold values from 4.2 to 4.8
- bias: float32 [], replicated, may hold values from -16 to -12
Outputs:
- update: float32 [1152, 4304], P('col', 'row')
- new_row: float32 [1152], P('col')
- new_col: float32 [4304], P('row')
- loss: float32 [], replicated
All inputs are finite; a program needn't handle non-finite values.
Results may differ from a plain program's by a relative error of at most 0.004.
Values may be sent and summed in bfloat16 or wider, within the bound.
No kernel may reach another device: no remote copies, remote signals or barrier semaphores. Data moves between devices by JAX's collectives and lax.ppermute only.
A program may use at most 128 MiB of HBM per device.

v0:
```python
import functools
import itertools

import jax
import jax.numpy as jnp
from jax import lax
from jax.experimental import pallas as pl
from jax.experimental.pallas import tpu as pltpu
from jax.sharding import Mesh
from jax.sharding import PartitionSpec as P


D = 1152
FF = 4304
AXES = ("x", "k", "y", "z")
SIZES = {"x": 4, "k": 2, "y": 4, "z": 8}
ROW = ("x", "k")
COL = ("y", "z")
EPSILON = 1e-06
DECAY_RATE = 0.8
CLIP_LEVEL = 1.0
FLOOR_VALUE = 1e-30
BF16 = jnp.bfloat16
F32 = jnp.float32


def shift(value, **by):
    names = tuple(a for a in AXES if a in by)
    sizes = [SIZES[a] for a in names]

    def linear(place):
        index = 0
        for p, n in zip(place, sizes):
            index = index * n + p
        return index

    pairs = [
        (linear(p), linear([(c + by[a]) % SIZES[a] for c, a in zip(p, names)]))
        for p in itertools.product(*[range(n) for n in sizes])
    ]
    return lax.ppermute(value, names, pairs)


def exchange(pieces, axes):
    return lax.all_to_all(pieces, axes, split_axis=0, concat_axis=0, tiled=True)


def everywhere(array, axes):
    return exchange(jnp.broadcast_to(array, (lax.axis_size(axes), *array.shape)), axes)


def after(values, *others):
    return lax.optimization_barrier((values, others))[0]


def rolled(pieces, by, count):
    twice = jnp.concatenate([pieces, pieces])
    return lax.dynamic_slice_in_dim(twice, by & (count - 1), count, 0)


def ring_step(up, down, axis):
    return shift(up, **{axis: 1}), shift(down, **{axis: -1})


def project_kernel(h0, h1, h2, h3, own, other, part, *hid):
    at = pl.program_id(0)
    total = None
    for kk in range(2):
        rows = jnp.concatenate([h[0, kk] for h in (h0, h1, h2, h3)], axis=0)
        for s in range(4):

            @pl.when(at == s)
            def _(s=s, rows=rows):
                hid[s][kk] = rows

        piece = lax.dot_general(
            rows, (own, other)[kk][0], (((1,), (1,)), ((), ())), preferred_element_type=F32
        )
        total = piece if total is None else total + piece

    @pl.when(at == 0)
    def _():
        part[...] = total

    @pl.when(at > 0)
    def _():
        part[...] += total


def project(hid_y, own, other):
    count, _, tokens, units = hid_y[0].shape
    features = own.shape[1]
    weights = pl.BlockSpec((1, features, units), lambda i: (i, 0, 0))
    rows = (2, 4 * tokens, units)
    return pl.pallas_call(
        project_kernel,
        grid=(count,),
        in_specs=[pl.BlockSpec((1, 2, tokens, units), lambda i: (i, 0, 0, 0))] * 4
        + [weights] * 2,
        out_specs=[pl.BlockSpec((4 * tokens, features), lambda i: (0, 0))]
        + [pl.BlockSpec(rows, lambda i: (0, 0, 0))] * 4,
        out_shape=[jax.ShapeDtypeStruct((4 * tokens, features), F32)]
        + [jax.ShapeDtypeStruct(rows, BF16)] * 4,
        cost_estimate=pl.CostEstimate(
            flops=2 * count * 2 * 4 * tokens * units * features,
            bytes_accessed=8000000,
            transcendentals=0,
        ),
        compiler_params=pltpu.CompilerParams(dimension_semantics=("arbitrary",)),
    )(*hid_y, own, other)


def gradient_kernel(*refs):
    grads, hid, outs = refs[:4], refs[4:8], refs[8:]
    totals = [None, None]
    for s in range(4):
        turned = grads[s][...].T
        for kk in range(2):
            piece = jnp.dot(
                turned, hid[s][kk if s == 0 else 1 - kk], preferred_element_type=F32
            )
            totals[kk] = piece if totals[kk] is None else totals[kk] + piece
    for kk in range(2):
        outs[kk][...] = totals[kk]


def gradients(grads, hid):
    features, units = grads[0].shape[1], hid[0].shape[2]
    return pl.pallas_call(
        gradient_kernel,
        out_shape=[jax.ShapeDtypeStruct((features, units), F32)] * 2,
        cost_estimate=pl.CostEstimate(
            flops=16 * grads[0].size * units, bytes_accessed=4000000, transcendentals=0
        ),
    )(*grads, *hid)


def joined(pieces):
    rows = sum(p.shape[0] for p in pieces)
    whole = jnp.zeros((rows, *pieces[0].shape[1:]), pieces[0].dtype)
    at = 0
    for piece in pieces:
        whole = lax.dynamic_update_slice_in_dim(whole, piece, at, 0)
        at += piece.shape[0]
    return whole


def pair_kernel(scalars, images, texts, *refs, first, tokens, batch_total):
    if first:
        part, loss = refs
    else:
        before, part, sent, loss = refs
    at = pl.program_id(0)
    block = texts[...]
    logits = (
        scalars[0]
        * lax.dot_general(
            images[...], block, (((1,), (1,)), ((), ())), preferred_element_type=F32
        )
        + scalars[1]
    )
    if first:
        rows = lax.broadcasted_iota(jnp.int32, logits.shape, 0)
        cols = lax.broadcasted_iota(jnp.int32, logits.shape, 1) + at * logits.shape[1]
        positive = (rows == cols) & (rows < tokens)
        logits = jnp.where(positive, -logits, logits)
    small = jnp.exp(-jnp.abs(logits))
    inverse = 1.0 / (1.0 + small)
    slope = jnp.where(logits >= 0, inverse, small * inverse) / batch_total
    if first:
        slope = jnp.where(positive, -slope, slope)
    added = jnp.dot(slope.astype(BF16), block, preferred_element_type=F32)
    losses = jnp.sum(jnp.maximum(logits, 0.0) + jnp.log1p(small), axis=0, keepdims=True)

    @pl.when(at == 0)
    def _():
        loss[...] = losses
        part[...] = added if first else added + before[...]

    @pl.when(at > 0)
    def _():
        loss[...] += losses
        part[...] += added

    if not first:

        @pl.when(at == pl.num_programs(0) - 1)
        def _():
            scaled = scalars[0] * part[...]
            part[...] = scaled
            sent[...] = scaled.astype(BF16)


def pair_tiles(scalars, images, texts, before, tokens, batch_total):
    first = before is None
    count, width = images.shape
    block = 256
    whole = pl.BlockSpec((count, width), lambda i: (0, 0))
    outs = [jax.ShapeDtypeStruct((count, width), F32)]
    if not first:
        outs.append(jax.ShapeDtypeStruct((count, width), BF16))
    outs.append(jax.ShapeDtypeStruct((1, block), F32))
    pairs = count * texts.shape[0]
    return pl.pallas_call(
        functools.partial(
            pair_kernel, first=first, tokens=tokens, batch_total=batch_total
        ),
        grid=(texts.shape[0] // block,),
        in_specs=[
            pl.BlockSpec(memory_space=pltpu.SMEM),
            whole,
            pl.BlockSpec((block, width), lambda i: (i, 0)),
        ]
        + ([] if first else [whole]),
        out_specs=[whole] * (len(outs) - 1) + [pl.BlockSpec((1, block), lambda i: (0, 0))],
        out_shape=outs,
        cost_estimate=pl.CostEstimate(
            flops=4 * pairs * width, bytes_accessed=2 * texts.size, transcendentals=3 * pairs
        ),
        compiler_params=pltpu.CompilerParams(dimension_semantics=("arbitrary",)),
    )(scalars, images, texts, *([] if first else [before]))


def step(pooled, hidden, text, weight, row_moment, col_moment, log_scale, bias):
    tokens = pooled.shape[0]
    batch_total = tokens * 256
    slice_ff = weight.shape[1]
    k_place = lax.axis_index("k")

    quarter = D // 4
    x_place = lax.axis_index("x")
    y_place = lax.axis_index("y")
    half_ff = slice_ff

    text_float = text.astype(F32)
    text_units = (
        text_float / jnp.sqrt(jnp.sum(text_float * text_float, axis=1, keepdims=True) + EPSILON)
    ).astype(BF16)
    texts_y = joined([text_units] + [shift(text_units, k=1, y=s) for s in (1, 2, 3)])

    by_slice = jnp.moveaxis(hidden.reshape(tokens, 8, half_ff), 1, 0).reshape(
        4, 2, tokens, half_ff
    )
    by_slice = jnp.where(k_place == 0, by_slice, by_slice[:, ::-1])
    hid_mine = rolled(by_slice, x_place, 4)
    hid_y = [hid_mine] + [shift(hid_mine, y=-s) for s in (1, 2, 3)]

    up, down = ring_step(texts_y, texts_y, "z")
    ring_pieces = [texts_y, up, down]

    weight_z = everywhere(weight.astype(BF16), "z").reshape(quarter, half_ff)
    weight_own = [weight_z] + [shift(weight_z, x=-s) for s in (1, 2, 3)]
    weight_own = joined([w[None] for w in weight_own])
    weight_other = shift(after(weight_own, up, down), k=1)
    up, down = ring_step(up, down, "z")
    ring_pieces += [up, down]
    mixed_part, *hid_all = project(hid_y, weight_own, weight_other)
    mixed_part = mixed_part.reshape(4, tokens, quarter)

    by_y = (2, 4, tokens, half_ff)
    hid_x = [hid_all[0]] + [
        shift(hid_all[s].reshape(by_y), x=s, k=1).reshape(hid_all[s].shape)
        for s in (1, 2, 3)
    ]
    arrived = exchange(rolled(mixed_part, -y_place, 4), "y")
    mixed = pooled.astype(F32) + jnp.moveaxis(arrived, 0, 1).reshape(tokens, D)
    length = jnp.sqrt(jnp.sum(mixed * mixed, axis=1, keepdims=True) + EPSILON)
    unit = mixed / length
    images = unit.astype(BF16)
    up, down = ring_step(*after((up, down), mixed_part), "z")
    ring_pieces += [up, down]
    half = texts_y.shape[0] // 2
    ring_pieces += ring_step(*after((up[:half], down[half:]), images), "z")

    logit_scale = jnp.exp(log_scale)
    image_rows = joined([images] + [shift(images, x=s) for s in (1, 2, 3)])
    texts_own = jnp.concatenate(ring_pieces[:-2] + after(ring_pieces[-2:], image_rows))
    texts_other = shift(texts_own, k=1)
    scalars = jnp.stack([logit_scale, bias])
    part_a, loss_a = pair_tiles(scalars, image_rows, texts_own, None, tokens, batch_total)
    part, part_sent, loss_b = pair_tiles(
        scalars, image_rows, texts_other, part_a, tokens, batch_total
    )
    unit_grad = part[:tokens] + sum(
        shift(part_sent[s * tokens : (s + 1) * tokens], x=-s).astype(F32) for s in (1, 2, 3)
    )
    mixed_grad = (
        (unit_grad - unit * jnp.sum(unit * unit_grad, axis=1, keepdims=True)) / length
    ).astype(BF16)

    quarters = jnp.moveaxis(mixed_grad.reshape(tokens, 4, quarter), 1, 0)
    quarters = rolled(quarters, y_place, 4)
    grad_y = [quarters[0]] + [shift(quarters[s], y=s) for s in (1, 2, 3)]
    grad_mine = joined([grad_y[-s] for s in range(4)])
    grad_x = [grad_mine] + [shift(grad_mine, x=s, k=1) for s in (1, 2, 3)]
    both = gradients(grad_x, hid_x)
    chip_grad = both[0] + shift(both[1], k=1)
    arrived_grad = exchange(chip_grad.astype(BF16).reshape(8, D // 32, slice_ff), "z")
    gradient = jnp.sum(arrived_grad.astype(F32), axis=0)

    squared = gradient * gradient + FLOOR_VALUE
    row_message = jnp.concatenate([jnp.sum(squared, axis=1), jnp.sum(loss_a + loss_b).reshape(1)])
    row_total = jnp.sum(everywhere(row_message[None], ROW), axis=(0, 1))
    loss_row = row_total[-1]
    new_row = DECAY_RATE * row_moment + (1.0 - DECAY_RATE) * row_total[:-1] / FF
    scaled = jnp.sum(gradient * gradient / new_row[:, None], axis=0)
    col_message = jnp.stack(
        [jnp.sum(squared, axis=0), scaled, jnp.full((slice_ff,), loss_row)]
    )
    col_total = jnp.sum(everywhere(col_message, COL), axis=0)
    new_col = DECAY_RATE * col_moment + (1.0 - DECAY_RATE) * col_total[0] / D
    loss = col_total[2, 0] / batch_total
    ours = jnp.sum(col_total[1] / new_col)
    update_total = jnp.sum(everywhere(jnp.full((1, 128), ours), ROW), axis=(0, 1))[0]
    update_rms = jnp.sqrt(update_total / (D * FF))
    raw_update = gradient / jnp.sqrt(new_row[:, None] * new_col[None, :])
    update = raw_update / jnp.maximum(1.0, update_rms / CLIP_LEVEL)
    return (update, new_row, new_col, loss)


def solution(mesh):
    finer = Mesh(mesh.devices.reshape(4, 2, 4, 8), AXES)
    return jax.shard_map(
        step,
        mesh=finer,
        in_specs=(
            P(AXES, None),
            P(AXES, None),
            P(AXES, None),
            P(COL, ROW),
            P(COL),
            P(ROW),
            P(),
            P(),
        ),
        out_specs=(P(COL, ROW), P(COL), P(ROW), P()),
        check_vma=False,
    )
```

profile of v0, /device:TPU:2, one launch (start us, length us, event | category | flops | bytes accessed | tf_op | source)
XLA Modules:
  0.0 280.4 jit_solution(14950336000531771789)
XLA Ops:
  2.3 8.5 %all-to-all-start = ((bf16[8,36,538]{2,1,0:T(8,128)(2,1)}), bf16[8,36,538]{2,1,0:T(8,128)(2,1)S(1)}, u32[]{:S(2)}, u32[]{:S(2)}) async-start(bf16[8,36,538]{2,1,0:T(8,128)(2,1)} %broadcast_in_dim.12), calls=%async_computation | async-start | bytes 819200 | tf_op jit(solution)/shard_map/all_to_all | solution.py:45
  10.8 1.0 fusion.2
  13.7 3.5 %collective-permute-start.7 = (bf16[64,1152]{1,0:T(8,128)(2,1)S(1)}, bf16[64,1152]{1,0:T(8,128)(2,1)S(1)}, u32[]{:S(2)}, u32[]{:S(2)}) collective-permute-start(bf16[64,1152]{1,0:T(8,128)(2,1)S(1)} %fusion.3), channel_id=1, source_target_pairs={{0,48},{8,56},{16,32},{24,40},{32,16},{40,24},{48,0},{56,8},{1,49}... | collective-permute-start | bytes 442376 | tf_op jit(solution)/shard_map/ppermute | solution.py:41
  17.7 2.2 collective-permute-done.6
  20.0 5.9 %all-to-all-done = bf16[8,36,538]{2,1,0:T(8,128)(2,1)S(1)} async-done(((bf16[8,36,538]{2,1,0:T(8,128)(2,1)}), bf16[8,36,538]{2,1,0:T(8,128)(2,1)S(1)}, u32[]{:S(2)}, u32[]{:S(2)}) %all-to-all-start) | async-done | bytes 309920 | tf_op jit(solution)/shard_map/all_to_all | solution.py:45
  26.6 2.5 collective-permute-start.4
  29.8 2.7 collective-permute-start.10
  32.4 1.8 collective-permute-start.5
  34.5 2.2 collective-permute-done.3
  37.7 7.0 %collective-permute-done.4 = bf16[288,538]{1,0:T(8,128)(2,1)} collective-permute-done((bf16[288,538]{1,0:T(8,128)(2,1)S(1)}, bf16[288,538]{1,0:T(8,128)(2,1)}, u32[]{:S(2)}, u32[]{:S(2)}) %collective-permute-start.4) | collective-permute-done | bytes 309920 | tf_op jit(solution)/shard_map/ppermute | solution.py:41
  44.7 1.0 bitcast_dynamic-update-slice_fusion.1
  45.7 1.0 bitcast_dynamic-update-slice_fusion.own
  47.7 2.0 reshape.74
  50.2 3.1 %collective-permute-start = (bf16[4,2,64,538]{3,2,1,0:T(8,128)(2,1)S(1)}, bf16[4,2,64,538]{3,2,1,0:T(8,128)(2,1)}, u32[]{:S(2)}, u32[]{:S(2)}) collective-permute-start(bf16[4,2,64,538]{3,2,1,0:T(8,128)(2,1)S(1)} %fusion.h0), channel_id=1, source_target_pairs={{0,24},{8,0},{16,8},{24,16},{1,25},{9,1},{17,9},{25,17},{2,26},{10... | collective-permute-start | bytes 1652744 | tf_op jit(solution)/shard_map/ppermute | solution.py:41
  55.8 2.0 constant_dynamic-update-slice_fusion.7
  58.6 22.6 %collective-permute-done.h1 = bf16[4,2,64,538]{3,2,1,0:T(8,128)(2,1)} collective-permute-done((bf16[4,2,64,538]{3,2,1,0:T(8,128)(2,1)S(1)}, bf16[4,2,64,538]{3,2,1,0:T(8,128)(2,1)}, u32[]{:S(2)}, u32[]{:S(2)}) %collective-permute-start) | collective-permute-done | bytes 550944 | tf_op jit(solution)/shard_map/ppermute | solution.py:41
  81.6 3.4 %collective-permute-done.2.h3 = bf16[4,2,64,538]{3,2,1,0:T(8,128)(2,1)} collective-permute-done((bf16[4,2,64,538]{3,2,1,0:T(8,128)(2,1)S(1)}, bf16[4,2,64,538]{3,2,1,0:T(8,128)(2,1)}, u32[]{:S(2)}, u32[]{:S(2)}) %collective-permute-start.2) | collective-permute-done | bytes 550944 | tf_op jit(solution)/shard_map/ppermute | solution.py:41
  85.0 6.8 %shard_map.111 = (f32[256,288]{1,0:T(8,128)}, bf16[2,256,538]{2,1,0:T(8,128)(2,1)}, bf16[2,256,538]{2,1,0:T(8,128)(2,1)}, bf16[2,256,538]{2,1,0:T(8,128)(2,1)}, bf16[2,256,538]{2,1,0:T(8,128)(2,1)}) custom-call(bf16[4,2,64,538]{3,2,1,0:T(8,128)(2,1)} %copy-done.1, bf16[4,2,64,538]{3,2,1,0:T(8,128)(2,1)} %collective-permute-done.h1, ...), custom_call_target="tpu_custom_call" | custom-call | flops 634650624 | bytes 8000000 | tf_op jit(solution)/shard_map/pallas_call | solution.py:95
  91.8 1.8 fusion.1
  93.6 3.5 %all-to-all-start.1 = ((f32[4,64,288]{2,1,0:T(8,128)}), f32[4,64,288]{2,1,0:T(8,128)S(1)}, u32[]{:S(2)}, u32[]{:S(2)}) async-start(f32[4,64,288]{2,1,0:T(8,128)} %fusion.1), calls=%async_computation.1 | async-start | bytes 786432 | tf_op jit(solution)/shard_map/all_to_all | solution.py:45
  97.1 1.9 constant_dynamic-update-slice_fusion.5
  99.0 6.6 %all-to-all-done.1 = f32[4,64,288]{2,1,0:T(8,128)S(1)} async-done(((f32[4,64,288]{2,1,0:T(8,128)}), f32[4,64,288]{2,1,0:T(8,128)S(1)}, u32[]{:S(2)}, u32[]{:S(2)}) %all-to-all-start.1) | async-done | bytes 294944 | tf_op jit(solution)/shard_map/all_to_all | solution.py:45
  106.4 1.5 collective-permute-start.12
  107.8 2.0 constant_dynamic-update-slice_fusion.4
  109.8 3.2 %collective-permute-start.18 = (bf16[256,1152]{1,0:T(8,128)(2,1)}, bf16[256,1152]{1,0:T(8,128)(2,1)S(1)}, u32[]{:S(2)}, u32[]{:S(2)}) collective-permute-start(bf16[256,1152]{1,0:T(8,128)(2,1)} %collective-permute-done.16), channel_id=1, source_target_pairs={{0,7},{1,0},{2,1},{3,2},{4,3},{5,4},{6,5},{7,6},{8,15},{9,8},{10,9... | collective-permute-start | bytes 1769480 | tf_op jit(solution)/shard_map/ppermute | solution.py:41
  113.1 3.7 %collective-permute-start.13 = (bf16[64,1152]{1,0:T(8,128)(2,1)S(1)}, bf16[64,1152]{1,0:T(8,128)(2,1)S(1)}, u32[]{:S(2)}, u32[]{:S(2)}) collective-permute-start(bf16[64,1152]{1,0:T(8,128)(2,1)S(1)} %fusion.7), channel_id=1, source_target_pairs={{0,128},{64,192},{128,0},{192,64},{1,129},{65,193},{129,1},{193,65... | collective-permute-start | bytes 442376 | tf_op jit(solution)/shard_map/ppermute | solution.py:41
  116.8 1.0 collective-permute-start.14
  117.9 2.9 %collective-permute-done.13 = bf16[64,1152]{1,0:T(8,128)(2,1)S(1)} collective-permute-done((bf16[64,1152]{1,0:T(8,128)(2,1)S(1)}, bf16[64,1152]{1,0:T(8,128)(2,1)S(1)}, u32[]{:S(2)}, u32[]{:S(2)}) %collective-permute-start.13) | collective-permute-done | bytes 147488 | tf_op jit(solution)/shard_map/ppermute | solution.py:41
  120.8 1.5 collective-permute-done.14
  122.3 3.0 %collective-permute-done.17 = bf16[256,1152]{1,0:T(8,128)(2,1)S(1)} collective-permute-done((bf16[256,1152]{1,0:T(8,128)(2,1)}, bf16[256,1152]{1,0:T(8,128)(2,1)S(1)}, u32[]{:S(2)}, u32[]{:S(2)}) %collective-permute-start.17) | collective-permute-done | bytes 589856 | tf_op jit(solution)/shard_map/ppermute | solution.py:41
  125.5 3.2 %collective-permute-start.20 = (bf16[128,1152]{1,0:T(8,128)(2,1)S(1)}, bf16[128,1152]{1,0:T(8,128)(2,1)S(1)}, u32[]{:S(2)}, u32[]{:S(2)}) collective-permute-start(bf16[128,1152]{1,0:T(8,128)(2,1)S(1)} %slice.65), channel_id=1, source_target_pairs={{0,7},{1,0},{2,1},{3,2},{4,3},{5,4},{6,5},{7,6},{8,15},{9,8},{10,9... | collective-permute-start | bytes 884744 | tf_op jit(solution)/shard_map/ppermute | solution.py:41
  130.5 3.2 %collective-permute-done.19 = bf16[128,1152]{1,0:T(8,128)(2,1)S(1)} collective-permute-done((bf16[128,1152]{1,0:T(8,128)(2,1)S(1)}, bf16[128,1152]{1,0:T(8,128)(2,1)S(1)}, u32[]{:S(2)}, u32[]{:S(2)}) %collective-permute-start.19) | collective-permute-done | bytes 294944 | tf_op jit(solution)/shard_map/ppermute | solution.py:41
  137.1 11.8 %shard_map.112 = (f32[256,1152]{1,0:T(8,128)}, f32[1,256]{1,0:T(1,128)}) custom-call(f32[2]{0:T(128)} %pad_maximum_fusion.scalars, bf16[256,1152]{1,0:T(8,128)(2,1)} %copy-done.9, bf16[2048,1152]{1,0:T(8,128)(2,1)} %constant_dynamic-update-slice_fusion.texts), custom_call_target="tpu_custom_call" | custom-call | flops 2415919104 | bytes 4718592 | tf_op jit(solution)/shard_map/pallas_call | solution.py:204
  149.0 12.6 %shard_map.113 = (f32[256,1152]{1,0:T(8,128)}, bf16[256,1152]{1,0:T(8,128)(2,1)}, f32[1,256]{1,0:T(1,128)}) custom-call(f32[2]{0:T(128)} %pad_maximum_fusion.scalars, bf16[256,1152]{1,0:T(8,128)(2,1)} %copy-done.9, bf16[2048,1152]{1,0:T(8,128)(2,1)} %collective-permute-done.21.texts, f32[256,1152]{1,0:T(8,128)} %get-tuple-element.31.refs_0_), custom_call_target="tpu_custom_call" | custom-call | flops 2415919104 | bytes 4718592 | tf_op jit(solution)/shard_map/pallas_call | solution.py:204
  161.6 1.1 fusion.8
  162.7 2.7 collective-permute-start.24
  165.4 1.6 collective-permute-start.23
  167.0 2.0 collective-permute-start.22
  169.0 2.8 %collective-permute-start.32 = (bf16[2,4,64,538]{3,2,1,0:T(8,128)(2,1)}, bf16[2,4,64,538]{3,2,1,0:T(8,128)(2,1)S(1)}, u32[]{:S(2)}, u32[]{:S(2)}) collective-permute-start(bf16[2,4,64,538]{3,2,1,0:T(8,128)(2,1)} %bitcast.49), channel_id=1, source_target_pairs={{0,160},{32,128},{64,224},{96,192},{128,32},{160,0},{192,96},{224,... | collective-permute-start | bytes 1652744 | tf_op jit(solution)/shard_map/ppermute | solution.py:41
  171.9 1.8 collective-permute-done.23
  173.6 3.2 %collective-permute-done.22 = bf16[64,1152]{1,0:T(8,128)(2,1)S(1)} collective-permute-done((bf16[64,1152]{1,0:T(8,128)(2,1)S(1)}, bf16[64,1152]{1,0:T(8,128)(2,1)S(1)}, u32[]{:S(2)}, u32[]{:S(2)}) %collective-permute-start.22) | collective-permute-done | bytes 147488 | tf_op jit(solution)/shard_map/ppermute | solution.py:41
  176.9 1.2 multiply_reduce_fusion
  178.0 1.1 divide_convert_fusion
  179.6 1.2 collective-permute-start.25
  180.8 1.6 collective-permute-start.26
  182.4 1.3 collective-permute-done.25
  184.3 2.4 collective-permute-done.26
  186.8 2.3 collective-permute-done.27
  189.2 1.8 collective-permute-start.29
  191.0 8.9 %collective-permute-done.31 = bf16[2,4,64,538]{3,2,1,0:T(8,128)(2,1)S(1)} collective-permute-done((bf16[2,4,64,538]{3,2,1,0:T(8,128)(2,1)}, bf16[2,4,64,538]{3,2,1,0:T(8,128)(2,1)S(1)}, u32[]{:S(2)}, u32[]{:S(2)}) %collective-permute-start.31) | collective-permute-done | bytes 550944 | tf_op jit(solution)/shard_map/ppermute | solution.py:41
  199.9 4.0 %collective-permute-done.33 = bf16[2,4,64,538]{3,2,1,0:T(8,128)(2,1)S(1)} collective-permute-done((bf16[2,4,64,538]{3,2,1,0:T(8,128)(2,1)}, bf16[2,4,64,538]{3,2,1,0:T(8,128)(2,1)S(1)}, u32[]{:S(2)}, u32[]{:S(2)}) %collective-permute-start.33) | collective-permute-done | bytes 550944 | tf_op jit(solution)/shard_map/ppermute | solution.py:41
  203.9 1.5 collective-permute-done.28.refs_1_
  205.4 2.4 collective-permute-done.29.refs_2_
  207.8 4.3 %collective-permute-done.30.refs_3_ = bf16[256,288]{1,0:T(8,128)(2,1)S(1)} collective-permute-done((bf16[256,288]{1,0:T(8,128)(2,1)S(1)}, bf16[256,288]{1,0:T(8,128)(2,1)S(1)}, u32[]{:S(2)}, u32[]{:S(2)}) %collective-permute-start.30) | collective-permute-done | bytes 147488 | tf_op jit(solution)/shard_map/ppermute | solution.py:41
  212.8 4.1 %shard_map.114 = (f32[288,538]{1,0:T(8,128)}, f32[288,538]{1,0:T(8,128)}) custom-call(bf16[256,288]{1,0:T(8,128)(2,1)} %copy-done.3, bf16[256,288]{1,0:T(8,128)(2,1)} %copy-done.10, bf16[256,288]{1,0:T(8,128)(2,1)} %copy-done.11, bf16[256,288]{1,0:T(8,128)(2,1)} %copy-done.12, bf16[2,256,538]{2,1,0:T(8,128)(2,1)} %get-tuple-element.34.refs_4_, ...), custom_call_target="tpu_custom_call" | custom-call | flops 634650624 | bytes 4000000 | tf_op jit(solution)/shard_map/pallas_call | solution.py:129
  217.1 2.3 collective-permute-done.34
  219.4 1.2 add_convert_fusion
  221.4 4.2 %all-to-all-start.2 = ((bf16[8,36,538]{2,1,0:T(8,128)(2,1)}), bf16[8,36,538]{2,1,0:T(8,128)(2,1)S(1)}, u32[]{:S(2)}, u32[]{:S(2)}) async-start(bf16[8,36,538]{2,1,0:T(8,128)(2,1)} %reshape.86), calls=%async_computation.2 | async-start | bytes 819200 | tf_op jit(solution)/shard_map/all_to_all | solution.py:45
  226.2 14.7 %all-to-all-done.2 = bf16[8,36,538]{2,1,0:T(8,128)(2,1)S(1)} async-done(((bf16[8,36,538]{2,1,0:T(8,128)(2,1)}), bf16[8,36,538]{2,1,0:T(8,128)(2,1)S(1)}, u32[]{:S(2)}, u32[]{:S(2)}) %all-to-all-start.2) | async-done | bytes 309920 | tf_op jit(solution)/shard_map/all_to_all | solution.py:45
  241.9 8.0 %all_to_all.30 = f32[8,1,37]{2,1,0:T(1,128)S(1)} all-to-all(f32[8,1,37]{2,1,0:T(1,128)S(1)} %broadcast_in_dim.31), channel_id=1, replica_groups=mesh['x'=4,'k'=2,'y'=4,'z'=8] {'x','k'}, dimensions={0} | all-to-all | bytes 2368 | tf_op jit(solution)/shard_map/all_to_all | solution.py:45
  251.5 16.5 %all_to_all.31 = f32[32,3,538]{2,1,0:T(4,128)S(1)} all-to-all(f32[32,3,538]{2,1,0:T(4,128)S(1)} %broadcast_in_dim.32), channel_id=1, replica_groups=mesh['x'=4,'k'=2,'y'=4,'z'=8] {'y','z'}, dimensions={0} | all-to-all | bytes 413184 | tf_op jit(solution)/shard_map/all_to_all | solution.py:45
  268.7 1.2 broadcast_in_dim_broadcast_in_dim.3
  270.0 4.7 %all-to-all-start.5 = ((f32[8,1,128]{2,1,0:T(1,128)}), f32[8,1,128]{2,1,0:T(1,128)S(1)}, u32[]{:S(2)}, u32[]{:S(2)}) async-start(f32[8,1,128]{2,1,0:T(1,128)} %broadcast_in_dim_broadcast_in_dim.3), calls=%async_computation.5 | async-start | bytes 8192 | tf_op jit(solution)/shard_map/all_to_all | solution.py:45
  275.8 2.6 all-to-all-done.5
  (133 shorter events, 24.6 us)
Async XLA Ops:
  2.3 23.5 %all-to-all-start = ((bf16[8,36,538]{2,1,0:T(8,128)(2,1)}), bf16[8,36,538]{2,1,0:T(8,128)(2,1)S(1)}, u32[]{:S(2)}, u32[]{:S(2)}) async-start(bf16[8,36,538]{2,1,0:T(8,128)(2,1)} %broadcast_in_dim.12), calls=%async_computation | async-start | bytes 819200 | tf_op jit(solution)/shard_map/all_to_all | solution.py:45
  12.9 7.1 %collective-permute-start.6 = (bf16[64,1152]{1,0:T(8,128)(2,1)S(1)}, bf16[64,1152]{1,0:T(8,128)(2,1)S(1)}, u32[]{:S(2)}, u32[]{:S(2)}) collective-permute-start(bf16[64,1152]{1,0:T(8,128)(2,1)S(1)} %fusion.3), channel_id=1, source_target_pairs={{0,40},{8,48},{16,56},{24,32},{32,8},{40,16},{48,24},{56,0},{1,41}... | collective-permute-start | bytes 442376 | tf_op jit(solution)/shard_map/ppermute | solution.py:41
  13.7 12.9 %collective-permute-start.7 = (bf16[64,1152]{1,0:T(8,128)(2,1)S(1)}, bf16[64,1152]{1,0:T(8,128)(2,1)S(1)}, u32[]{:S(2)}, u32[]{:S(2)}) collective-permute-start(bf16[64,1152]{1,0:T(8,128)(2,1)S(1)} %fusion.3), channel_id=1, source_target_pairs={{0,48},{8,56},{16,32},{24,40},{32,16},{40,24},{48,0},{56,8},{1,49}... | collective-permute-start | bytes 442376 | tf_op jit(solution)/shard_map/ppermute | solution.py:41
  17.2 11.9 %collective-permute-start.8 = (bf16[64,1152]{1,0:T(8,128)(2,1)S(1)}, bf16[64,1152]{1,0:T(8,128)(2,1)S(1)}, u32[]{:S(2)}, u32[]{:S(2)}) collective-permute-start(bf16[64,1152]{1,0:T(8,128)(2,1)S(1)} %fusion.3), channel_id=1, source_target_pairs={{0,56},{8,32},{16,40},{24,48},{32,24},{40,0},{48,8},{56,16},{1,57}... | collective-permute-start | bytes 442376 | tf_op jit(solution)/shard_map/ppermute | solution.py:41
  26.0 10.7 %collective-permute-start.3 = (bf16[288,538]{1,0:T(8,128)(2,1)S(1)}, bf16[288,538]{1,0:T(8,128)(2,1)}, u32[]{:S(2)}, u32[]{:S(2)}) collective-permute-start(bf16[288,538]{1,0:T(8,128)(2,1)S(1)} %reshape.76), channel_id=1, source_target_pairs={{0,192},{64,0},{128,64},{192,128},{1,193},{65,1},{129,65},{193,129... | collective-permute-start | bytes 929672 | tf_op jit(solution)/shard_map/ppermute | solution.py:41
  26.6 18.1 %collective-permute-start.4 = (bf16[288,538]{1,0:T(8,128)(2,1)S(1)}, bf16[288,538]{1,0:T(8,128)(2,1)}, u32[]{:S(2)}, u32[]{:S(2)}) collective-permute-start(bf16[288,538]{1,0:T(8,128)(2,1)S(1)} %reshape.76), channel_id=1, source_target_pairs={{0,128},{64,192},{128,0},{192,64},{1,129},{65,193},{129,1},{193,65... | collective-permute-start | bytes 929672 | tf_op jit(solution)/shard_map/ppermute | solution.py:41
  29.1 17.6 %collective-permute-start.9 = (bf16[256,1152]{1,0:T(8,128)(2,1)S(1)}, bf16[256,1152]{1,0:T(8,128)(2,1)}, u32[]{:S(2)}, u32[]{:S(2)}) collective-permute-start(bf16[256,1152]{1,0:T(8,128)(2,1)S(1)} %constant_dynamic-update-slice_fusion.15), channel_id=1, source_target_pairs={{0,1},{1,2},{2,3},{3,4},{4,5},{5,6},{6,7},{7,0},{8,9},{9,10},{10,1... | collective-permute-start | bytes 1769480 | tf_op jit(solution)/shard_map/ppermute | solution.py:41
  29.8 17.0 %collective-permute-start.10 = (bf16[256,1152]{1,0:T(8,128)(2,1)S(1)}, bf16[256,1152]{1,0:T(8,128)(2,1)S(1)}, u32[]{:S(2)}, u32[]{:S(2)}) collective-permute-start(bf16[256,1152]{1,0:T(8,128)(2,1)S(1)} %constant_dynamic-update-slice_fusion.15), channel_id=1, source_target_pairs={{0,7},{1,0},{2,1},{3,2},{4,3},{5,4},{6,5},{7,6},{8,15},{9,8},{10,9... | collective-permute-start | bytes 1769480 | tf_op jit(solution)/shard_map/ppermute | solution.py:41
  32.4 13.3 %collective-permute-start.5 = (bf16[288,538]{1,0:T(8,128)(2,1)S(1)}, bf16[288,538]{1,0:T(8,128)(2,1)}, u32[]{:S(2)}, u32[]{:S(2)}) collective-permute-start(bf16[288,538]{1,0:T(8,128)(2,1)S(1)} %reshape.76), channel_id=1, source_target_pairs={{0,64},{64,128},{128,192},{192,0},{1,65},{65,129},{129,193},{193,1... | collective-permute-start | bytes 929672 | tf_op jit(solution)/shard_map/ppermute | solution.py:41
  46.7 38.3 %copy-start = (bf16[4,288,538]{2,1,0:T(8,128)(2,1)}, bf16[4,288,538]{2,1,0:T(8,128)(2,1)S(1)}, u32[]{:S(2)}) copy-start(bf16[4,288,538]{2,1,0:T(8,128)(2,1)S(1)} %bitcast_dynamic-update-slice_fusion.own) | copy-start | bytes 3718660
  46.8 0.9 copy-start.7
  46.8 38.3 %collective-permute-start.11 = (bf16[4,288,538]{2,1,0:T(8,128)(2,1)S(1)}, bf16[4,288,538]{2,1,0:T(8,128)(2,1)}, u32[]{:S(2)}, u32[]{:S(2)}) collective-permute-start(bf16[4,288,538]{2,1,0:T(8,128)(2,1)S(1)} %bitcast_dynamic-update-slice_fusion.own), channel_id=1, source_target_pairs={{0,32},{32,0},{1,33},{33,1},{2,34},{34,2},{3,35},{35,3},{4,36},{36... | collective-permute-start | bytes 3718664 | tf_op jit(solution)/shard_map/ppermute | solution.py:41
  49.8 8.0 %copy-start.8 = (bf16[256,1152]{1,0:T(8,128)(2,1)S(1)}, bf16[256,1152]{1,0:T(8,128)(2,1)}, u32[]{:S(2)}) copy-start(bf16[256,1152]{1,0:T(8,128)(2,1)} %copy-done.7) | copy-start | bytes 1769476
  50.2 34.8 %copy-start.1 = (bf16[4,2,64,538]{3,2,1,0:T(8,128)(2,1)}, bf16[4,2,64,538]{3,2,1,0:T(8,128)(2,1)S(1)}, u32[]{:S(2)}) copy-start(bf16[4,2,64,538]{3,2,1,0:T(8,128)(2,1)S(1)} %fusion.h0) | copy-start | bytes 1652740
  50.2 31.0 %collective-permute-start = (bf16[4,2,64,538]{3,2,1,0:T(8,128)(2,1)S(1)}, bf16[4,2,64,538]{3,2,1,0:T(8,128)(2,1)}, u32[]{:S(2)}, u32[]{:S(2)}) collective-permute-start(bf16[4,2,64,538]{3,2,1,0:T(8,128)(2,1)S(1)} %fusion.h0), channel_id=1, source_target_pairs={{0,24},{8,0},{16,8},{24,16},{1,25},{9,1},{17,9},{25,17},{2,26},{10... | collective-permute-start | bytes 1652744 | tf_op jit(solution)/shard_map/ppermute | solution.py:41
  53.3 28.3 %collective-permute-start.1 = (bf16[4,2,64,538]{3,2,1,0:T(8,128)(2,1)S(1)}, bf16[4,2,64,538]{3,2,1,0:T(8,128)(2,1)}, u32[]{:S(2)}, u32[]{:S(2)}) collective-permute-start(bf16[4,2,64,538]{3,2,1,0:T(8,128)(2,1)S(1)} %fusion.h0), channel_id=1, source_target_pairs={{0,16},{8,24},{16,0},{24,8},{1,17},{9,25},{17,1},{25,9},{2,18},{10... | collective-permute-start | bytes 1652744 | tf_op jit(solution)/shard_map/ppermute | solution.py:41
  54.0 31.1 %collective-permute-start.2 = (bf16[4,2,64,538]{3,2,1,0:T(8,128)(2,1)S(1)}, bf16[4,2,64,538]{3,2,1,0:T(8,128)(2,1)}, u32[]{:S(2)}, u32[]{:S(2)}) collective-permute-start(bf16[4,2,64,538]{3,2,1,0:T(8,128)(2,1)S(1)} %fusion.h0), channel_id=1, source_target_pairs={{0,8},{8,16},{16,24},{24,0},{1,9},{9,17},{17,25},{25,1},{2,10},{10... | collective-permute-start | bytes 1652744 | tf_op jit(solution)/shard_map/ppermute | solution.py:41
  55.8 41.3 %collective-permute-start.15 = (bf16[256,1152]{1,0:T(8,128)(2,1)}, bf16[256,1152]{1,0:T(8,128)(2,1)}, u32[]{:S(2)}, u32[]{:S(2)}) collective-permute-start(bf16[256,1152]{1,0:T(8,128)(2,1)} %collective-permute-done.9), channel_id=1, source_target_pairs={{0,1},{1,2},{2,3},{3,4},{4,5},{5,6},{6,7},{7,0},{8,9},{9,10},{10,1... | collective-permute-start | bytes 1769480 | tf_op jit(solution)/shard_map/ppermute | solution.py:41
  58.6 47.5 %copy-start.2 = (bf16[64,1152]{1,0:T(8,128)(2,1)S(1)}, bf16[64,1152]{1,0:T(8,128)(2,1)}, u32[]{:S(2)}) copy-start(bf16[64,1152]{1,0:T(8,128)(2,1)} %param.8) | copy-start | bytes 442372
  81.2 26.6 %collective-permute-start.16 = (bf16[256,1152]{1,0:T(8,128)(2,1)S(1)}, bf16[256,1152]{1,0:T(8,128)(2,1)}, u32[]{:S(2)}, u32[]{:S(2)}) collective-permute-start(bf16[256,1152]{1,0:T(8,128)(2,1)S(1)} %copy-done.8), channel_id=1, source_target_pairs={{0,7},{1,0},{2,1},{3,2},{4,3},{5,4},{6,5},{7,6},{8,15},{9,8},{10,9... | collective-permute-start | bytes 1769480 | tf_op jit(solution)/shard_map/ppermute | solution.py:41
  93.6 12.0 %all-to-all-start.1 = ((f32[4,64,288]{2,1,0:T(8,128)}), f32[4,64,288]{2,1,0:T(8,128)S(1)}, u32[]{:S(2)}, u32[]{:S(2)}) async-start(f32[4,64,288]{2,1,0:T(8,128)} %fusion.1), calls=%async_computation.1 | async-start | bytes 786432 | tf_op jit(solution)/shard_map/all_to_all | solution.py:45
  106.4 11.5 %collective-permute-start.12 = (bf16[64,1152]{1,0:T(8,128)(2,1)S(1)}, bf16[64,1152]{1,0:T(8,128)(2,1)S(1)}, u32[]{:S(2)}, u32[]{:S(2)}) collective-permute-start(bf16[64,1152]{1,0:T(8,128)(2,1)S(1)} %fusion.7), channel_id=1, source_target_pairs={{0,64},{64,128},{128,192},{192,0},{1,65},{65,129},{129,193},{193,1... | collective-permute-start | bytes 442376 | tf_op jit(solution)/shard_map/ppermute | solution.py:41
  109.8 15.5 %collective-permute-start.17 = (bf16[256,1152]{1,0:T(8,128)(2,1)}, bf16[256,1152]{1,0:T(8,128)(2,1)S(1)}, u32[]{:S(2)}, u32[]{:S(2)}) collective-permute-start(bf16[256,1152]{1,0:T(8,128)(2,1)} %collective-permute-done.15), channel_id=1, source_target_pairs={{0,1},{1,2},{2,3},{3,4},{4,5},{5,6},{6,7},{7,0},{8,9},{9,10},{10,1... | collective-permute-start | bytes 1769480 | tf_op jit(solution)/shard_map/ppermute | solution.py:41
  109.8 15.6 %collective-permute-start.18 = (bf16[256,1152]{1,0:T(8,128)(2,1)}, bf16[256,1152]{1,0:T(8,128)(2,1)S(1)}, u32[]{:S(2)}, u32[]{:S(2)}) collective-permute-start(bf16[256,1152]{1,0:T(8,128)(2,1)} %collective-permute-done.16), channel_id=1, source_target_pairs={{0,7},{1,0},{2,1},{3,2},{4,3},{5,4},{6,5},{7,6},{8,15},{9,8},{10,9... | collective-permute-start | bytes 1769480 | tf_op jit(solution)/shard_map/ppermute | solution.py:41
  113.1 7.7 %collective-permute-start.13 = (bf16[64,1152]{1,0:T(8,128)(2,1)S(1)}, bf16[64,1152]{1,0:T(8,128)(2,1)S(1)}, u32[]{:S(2)}, u32[]{:S(2)}) collective-permute-start(bf16[64,1152]{1,0:T(8,128)(2,1)S(1)} %fusion.7), channel_id=1, source_target_pairs={{0,128},{64,192},{128,0},{192,64},{1,129},{65,193},{129,1},{193,65... | collective-permute-start | bytes 442376 | tf_op jit(solution)/shard_map/ppermute | solution.py:41
  116.8 5.5 %collective-permute-start.14 = (bf16[64,1152]{1,0:T(8,128)(2,1)S(1)}, bf16[64,1152]{1,0:T(8,128)(2,1)S(1)}, u32[]{:S(2)}, u32[]{:S(2)}) collective-permute-start(bf16[64,1152]{1,0:T(8,128)(2,1)S(1)} %fusion.7), channel_id=1, source_target_pairs={{0,192},{64,0},{128,64},{192,128},{1,193},{65,1},{129,65},{193,129... | collective-permute-start | bytes 442376 | tf_op jit(solution)/shard_map/ppermute | solution.py:41
  122.3 14.8 %copy-start.9 = (bf16[256,1152]{1,0:T(8,128)(2,1)}, bf16[256,1152]{1,0:T(8,128)(2,1)S(1)}, u32[]{:S(2)}) copy-start(bf16[256,1152]{1,0:T(8,128)(2,1)S(1)} %constant_dynamic-update-slice_fusion.12.images) | copy-start | bytes 1769476
  125.4 8.2 %collective-permute-start.19 = (bf16[128,1152]{1,0:T(8,128)(2,1)S(1)}, bf16[128,1152]{1,0:T(8,128)(2,1)S(1)}, u32[]{:S(2)}, u32[]{:S(2)}) collective-permute-start(bf16[128,1152]{1,0:T(8,128)(2,1)S(1)} %slice.64), channel_id=1, source_target_pairs={{0,1},{1,2},{2,3},{3,4},{4,5},{5,6},{6,7},{7,0},{8,9},{9,10},{10,1... | collective-permute-start | bytes 884744 | tf_op jit(solution)/shard_map/ppermute | solution.py:41
  125.5 8.1 %collective-permute-start.20 = (bf16[128,1152]{1,0:T(8,128)(2,1)S(1)}, bf16[128,1152]{1,0:T(8,128)(2,1)S(1)}, u32[]{:S(2)}, u32[]{:S(2)}) collective-permute-start(bf16[128,1152]{1,0:T(8,128)(2,1)S(1)} %slice.65), channel_id=1, source_target_pairs={{0,7},{1,0},{2,1},{3,2},{4,3},{5,4},{6,5},{7,6},{8,15},{9,8},{10,9... | collective-permute-start | bytes 884744 | tf_op jit(solution)/shard_map/ppermute | solution.py:41
  135.1 13.8 %collective-permute-start.21 = (bf16[2048,1152]{1,0:T(8,128)(2,1)}, bf16[2048,1152]{1,0:T(8,128)(2,1)}, u32[]{:S(2)}, u32[]{:S(2)}) collective-permute-start(bf16[2048,1152]{1,0:T(8,128)(2,1)} %constant_dynamic-update-slice_fusion.texts), channel_id=1, source_target_pairs={{0,32},{32,0},{1,33},{33,1},{2,34},{34,2},{3,35},{35,3},{4,36},{36... | collective-permute-start | bytes 14155784 | tf_op jit(solution)/shard_map/ppermute | solution.py:41
  162.7 9.2 %collective-permute-start.24 = (bf16[64,1152]{1,0:T(8,128)(2,1)S(1)}, bf16[64,1152]{1,0:T(8,128)(2,1)S(1)}, u32[]{:S(2)}, u32[]{:S(2)}) collective-permute-start(bf16[64,1152]{1,0:T(8,128)(2,1)S(1)} %get-tuple-element.49), channel_id=1, source_target_pairs={{0,64},{64,128},{128,192},{192,0},{1,65},{65,129},{129,193},{193,1... | collective-permute-start | bytes 442376 | tf_op jit(solution)/shard_map/ppermute | solution.py:41
  165.4 8.3 %collective-permute-start.23 = (bf16[64,1152]{1,0:T(8,128)(2,1)S(1)}, bf16[64,1152]{1,0:T(8,128)(2,1)S(1)}, u32[]{:S(2)}, u32[]{:S(2)}) collective-permute-start(bf16[64,1152]{1,0:T(8,128)(2,1)S(1)} %get-tuple-element.50), channel_id=1, source_target_pairs={{0,128},{64,192},{128,0},{192,64},{1,129},{65,193},{129,1},{193,65... | collective-permute-start | bytes 442376 | tf_op jit(solution)/shard_map/ppermute | solution.py:41
  167.0 9.9 %collective-permute-start.22 = (bf16[64,1152]{1,0:T(8,128)(2,1)S(1)}, bf16[64,1152]{1,0:T(8,128)(2,1)S(1)}, u32[]{:S(2)}, u32[]{:S(2)}) collective-permute-start(bf16[64,1152]{1,0:T(8,128)(2,1)S(1)} %get-tuple-element.48), channel_id=1, source_target_pairs={{0,192},{64,0},{128,64},{192,128},{1,193},{65,1},{129,65},{193,129... | collective-permute-start | bytes 442376 | tf_op jit(solution)/shard_map/ppermute | solution.py:41
  169.0 30.8 %collective-permute-start.31 = (bf16[2,4,64,538]{3,2,1,0:T(8,128)(2,1)}, bf16[2,4,64,538]{3,2,1,0:T(8,128)(2,1)S(1)}, u32[]{:S(2)}, u32[]{:S(2)}) collective-permute-start(bf16[2,4,64,538]{3,2,1,0:T(8,128)(2,1)} %bitcast.15), channel_id=1, source_target_pairs={{0,96},{32,64},{64,160},{96,128},{128,224},{160,192},{192,32},{224... | collective-permute-start | bytes 1652744 | tf_op jit(solution)/shard_map/ppermute | solution.py:41
  169.0 30.8 %collective-permute-start.32 = (bf16[2,4,64,538]{3,2,1,0:T(8,128)(2,1)}, bf16[2,4,64,538]{3,2,1,0:T(8,128)(2,1)S(1)}, u32[]{:S(2)}, u32[]{:S(2)}) collective-permute-start(bf16[2,4,64,538]{3,2,1,0:T(8,128)(2,1)} %bitcast.49), channel_id=1, source_target_pairs={{0,160},{32,128},{64,224},{96,192},{128,32},{160,0},{192,96},{224,... | collective-permute-start | bytes 1652744 | tf_op jit(solution)/shard_map/ppermute | solution.py:41
  171.9 32.0 %collective-permute-start.33 = (bf16[2,4,64,538]{3,2,1,0:T(8,128)(2,1)}, bf16[2,4,64,538]{3,2,1,0:T(8,128)(2,1)S(1)}, u32[]{:S(2)}, u32[]{:S(2)}) collective-permute-start(bf16[2,4,64,538]{3,2,1,0:T(8,128)(2,1)} %bitcast.48), channel_id=1, source_target_pairs={{0,224},{32,192},{64,32},{96,0},{128,96},{160,64},{192,160},{224,1... | collective-permute-start | bytes 1652744 | tf_op jit(solution)/shard_map/ppermute | solution.py:41
  179.1 46.5 %copy-start.16 = (f32[1,256]{1,0:T(1,128)S(1)}, f32[1,256]{1,0:T(1,128)}, u32[]{:S(2)}) copy-start(f32[1,256]{1,0:T(1,128)} %get-tuple-element.40) | copy-start | bytes 3076
  179.2 46.5 %copy-start.17 = (f32[1,256]{1,0:T(1,128)S(1)}, f32[1,256]{1,0:T(1,128)}, u32[]{:S(2)}) copy-start(f32[1,256]{1,0:T(1,128)} %get-tuple-element.41) | copy-start | bytes 3076
  179.2 71.3 %copy-start.18 = (f32[36]{0:T(128)S(1)}, f32[36]{0:T(128)}, u32[]{:S(2)}) copy-start(f32[36]{0:T(128)} %param.12) | copy-start | bytes 436
  179.6 4.2 %collective-permute-start.25 = (bf16[64,288]{1,0:T(8,128)(2,1)S(1)}, bf16[64,288]{1,0:T(8,128)(2,1)S(1)}, u32[]{:S(2)}, u32[]{:S(2)}) collective-permute-start(bf16[64,288]{1,0:T(8,128)(2,1)S(1)} %get-tuple-element.53), channel_id=1, source_target_pairs={{0,24},{8,0},{16,8},{24,16},{1,25},{9,1},{17,9},{25,17},{2,26},{10... | collective-permute-start | bytes 110600 | tf_op jit(solution)/shard_map/ppermute | solution.py:41
  180.8 87.3 %copy-start.14 = (f32[538]{0:T(1024)S(1)}, f32[538]{0:T(1024)}, u32[]{:S(2)}) copy-start(f32[538]{0:T(1024)} %param.13) | copy-start | bytes 6460
  180.8 5.9 %collective-permute-start.26 = (bf16[64,288]{1,0:T(8,128)(2,1)S(1)}, bf16[64,288]{1,0:T(8,128)(2,1)S(1)}, u32[]{:S(2)}, u32[]{:S(2)}) collective-permute-start(bf16[64,288]{1,0:T(8,128)(2,1)S(1)} %get-tuple-element.52), channel_id=1, source_target_pairs={{0,16},{8,24},{16,0},{24,8},{1,17},{9,25},{17,1},{25,9},{2,18},{10... | collective-permute-start | bytes 110600 | tf_op jit(solution)/shard_map/ppermute | solution.py:41
  183.8 5.3 %collective-permute-start.27 = (bf16[64,288]{1,0:T(8,128)(2,1)S(1)}, bf16[64,288]{1,0:T(8,128)(2,1)S(1)}, u32[]{:S(2)}, u32[]{:S(2)}) collective-permute-start(bf16[64,288]{1,0:T(8,128)(2,1)S(1)} %get-tuple-element.51), channel_id=1, source_target_pairs={{0,8},{8,16},{16,24},{24,0},{1,9},{9,17},{17,25},{25,1},{2,10},{10... | collective-permute-start | bytes 110600 | tf_op jit(solution)/shard_map/ppermute | solution.py:41
  189.1 23.0 %copy-start.3 = (bf16[256,288]{1,0:T(8,128)(2,1)}, bf16[256,288]{1,0:T(8,128)(2,1)S(1)}, u32[]{:S(2)}) copy-start(bf16[256,288]{1,0:T(8,128)(2,1)S(1)} %constant_dynamic-update-slice_fusion.9.refs_0_) | copy-start | bytes 442372
  189.1 16.3 %collective-permute-start.28 = (bf16[256,288]{1,0:T(8,128)(2,1)S(1)}, bf16[256,288]{1,0:T(8,128)(2,1)S(1)}, u32[]{:S(2)}, u32[]{:S(2)}) collective-permute-start(bf16[256,288]{1,0:T(8,128)(2,1)S(1)} %constant_dynamic-update-slice_fusion.9.refs_0_), channel_id=1, source_target_pairs={{0,96},{32,64},{64,160},{96,128},{128,224},{160,192},{192,32},{224... | collective-permute-start | bytes 442376 | tf_op jit(solution)/shard_map/ppermute | solution.py:41
  189.2 18.6 %collective-permute-start.29 = (bf16[256,288]{1,0:T(8,128)(2,1)S(1)}, bf16[256,288]{1,0:T(8,128)(2,1)S(1)}, u32[]{:S(2)}, u32[]{:S(2)}) collective-permute-start(bf16[256,288]{1,0:T(8,128)(2,1)S(1)} %constant_dynamic-update-slice_fusion.9.refs_0_), channel_id=1, source_target_pairs={{0,160},{32,128},{64,224},{96,192},{128,32},{160,0},{192,96},{224,... | collective-permute-start | bytes 442376 | tf_op jit(solution)/shard_map/ppermute | solution.py:41
  199.9 12.3 %copy-start.4 = (bf16[2,4,64,538]{3,2,1,0:T(8,128)(2,1)}, bf16[2,4,64,538]{3,2,1,0:T(8,128)(2,1)S(1)}, u32[]{:S(2)}) copy-start(bf16[2,4,64,538]{3,2,1,0:T(8,128)(2,1)S(1)} %collective-permute-done.31) | copy-start | bytes 1652740
  199.9 12.2 %collective-permute-start.30 = (bf16[256,288]{1,0:T(8,128)(2,1)S(1)}, bf16[256,288]{1,0:T(8,128)(2,1)S(1)}, u32[]{:S(2)}, u32[]{:S(2)}) collective-permute-start(bf16[256,288]{1,0:T(8,128)(2,1)S(1)} %constant_dynamic-update-slice_fusion.9.refs_0_), channel_id=1, source_target_pairs={{0,224},{32,192},{64,32},{96,0},{128,96},{160,64},{192,160},{224,1... | collective-permute-start | bytes 442376 | tf_op jit(solution)/shard_map/ppermute | solution.py:41
  199.9 12.2 %copy-start.5 = (bf16[2,4,64,538]{3,2,1,0:T(8,128)(2,1)}, bf16[2,4,64,538]{3,2,1,0:T(8,128)(2,1)S(1)}, u32[]{:S(2)}) copy-start(bf16[2,4,64,538]{3,2,1,0:T(8,128)(2,1)S(1)} %collective-permute-done.32) | copy-start | bytes 1652740
  203.9 8.2 %copy-start.6 = (bf16[2,4,64,538]{3,2,1,0:T(8,128)(2,1)}, bf16[2,4,64,538]{3,2,1,0:T(8,128)(2,1)S(1)}, u32[]{:S(2)}) copy-start(bf16[2,4,64,538]{3,2,1,0:T(8,128)(2,1)S(1)} %collective-permute-done.33) | copy-start | bytes 1652740
  205.4 6.7 %copy-start.10 = (bf16[256,288]{1,0:T(8,128)(2,1)}, bf16[256,288]{1,0:T(8,128)(2,1)S(1)}, u32[]{:S(2)}) copy-start(bf16[256,288]{1,0:T(8,128)(2,1)S(1)} %collective-permute-done.28.refs_1_) | copy-start | bytes 442372
  207.8 4.4 %copy-start.11 = (bf16[256,288]{1,0:T(8,128)(2,1)}, bf16[256,288]{1,0:T(8,128)(2,1)S(1)}, u32[]{:S(2)}) copy-start(bf16[256,288]{1,0:T(8,128)(2,1)S(1)} %collective-permute-done.29.refs_2_) | copy-start | bytes 442372
  212.1 0.7 copy-start.12
  216.9 2.4 collective-permute-start.34
  221.4 19.6 %all-to-all-start.2 = ((bf16[8,36,538]{2,1,0:T(8,128)(2,1)}), bf16[8,36,538]{2,1,0:T(8,128)(2,1)S(1)}, u32[]{:S(2)}, u32[]{:S(2)}) async-start(bf16[8,36,538]{2,1,0:T(8,128)(2,1)} %reshape.86), calls=%async_computation.2 | async-start | bytes 819200 | tf_op jit(solution)/shard_map/all_to_all | solution.py:45
  250.5 28.7 %copy-start.15 = (f32[36]{0:T(128)}, f32[36]{0:T(128)S(1)}, u32[]{:S(2)}) copy-start(f32[36]{0:T(128)S(1)} %multiply_add_fusion.1) | copy-start | bytes 436
  268.7 10.6 %copy-start.13 = (f32[538]{0:T(1024)}, f32[538]{0:T(1024)S(1)}, u32[]{:S(2)}) copy-start(f32[538]{0:T(1024)S(1)} %get-tuple-element.47) | copy-start | bytes 6460
  270.0 8.5 %all-to-all-start.5 = ((f32[8,1,128]{2,1,0:T(1,128)}), f32[8,1,128]{2,1,0:T(1,128)S(1)}, u32[]{:S(2)}, u32[]{:S(2)}) async-start(f32[8,1,128]{2,1,0:T(1,128)} %broadcast_in_dim_broadcast_in_dim.3), calls=%async_computation.5 | async-start | bytes 8192 | tf_op jit(solution)/shard_map/all_to_all | solution.py:45
where the time goes:
time: 283 us; the launch traced here: 280 us
  waiting for transfers between devices  112 us (40%)
  starting transfers between devices  66.4 us (23%)
  Pallas kernels  35.4 us (13%)
  local copies, waits for them, and re-layouts  24.7 us (9%)
  blocking collectives  24.5 us (9%)
  other arithmetic  12.8 us (5%)
  between operations  4.31 us (2%)
    ppermute x35, waiting for transfers between devices, shift(): return lax.ppermute(value, names, pairs)  82.4 us
    ppermute x35, starting transfers between devices, shift(): return lax.ppermute(value, names, pairs)  45.6 us
    all_to_all x4, waiting for transfers between devices, exchange(): return lax.all_to_all(pieces, axes, split_axis=0, concat_axis=0, tiled=True)  29.8 us
    all_to_all x2, blocking collectives, exchange(): return lax.all_to_all(pieces, axes, split_axis=0, concat_axis=0, tiled=True)  24.5 us
    pallas_call x2, Pallas kernels, pair_tiles(): pl.pallas_call(functools.partial(pair_kernel, first=first, tokens=tokens,...  24.5 us
    all_to_all x4, starting transfers between devices, exchange(): return lax.all_to_all(pieces, axes, split_axis=0, concat_axis=0, tiled=True)  20.8 us
    unnamed x46, local copies, waits for them, and re-layouts  11.6 us
    pallas_call x1, Pallas kernels, project(): pl.pallas_call(project_kernel, grid=(count,), in_specs=[pl.BlockSpec((1,...  6.79 us
  transfers between devices with their start and end apart: 39, of which 24 were waited for; matrix products, arithmetic and copies ran while one was open for 9% of the time, Pallas kernels for 7%

commit v1 on v0

--- a/solution.py
+++ b/solution.py
@@ -112,26 +112,33 @@
 
 def gradient_kernel(*refs):
     grads, hid, outs = refs[:4], refs[4:8], refs[8:]
-    totals = [None, None]
+    total = None
     for s in range(4):
-        turned = grads[s][...].T
-        for kk in range(2):
-            piece = jnp.dot(
-                turned, hid[s][kk if s == 0 else 1 - kk], preferred_element_type=F32
-            )
-            totals[kk] = piece if totals[kk] is None else totals[kk] + piece
+        piece = jnp.dot(grads[s][...].T, hid[s][0], preferred_element_type=F32)
+        total = piece if total is None else total + piece
     for kk in range(2):
-        outs[kk][...] = totals[kk]
+
+        @pl.when(pl.program_id(0) == kk)
+        def _(kk=kk):
+            outs[kk][...] = total
 
 
 def gradients(grads, hid):
-    features, units = grads[0].shape[1], hid[0].shape[2]
+    tokens, features = grads[0].shape
+    units = hid[0].shape[2]
+    whole = pl.BlockSpec((features, units), lambda i: (0, 0))
     return pl.pallas_call(
         gradient_kernel,
+        grid=(2,),
+        in_specs=[pl.BlockSpec((tokens, features), lambda i: (0, 0))] * 4
+        + [pl.BlockSpec((1, tokens, units), lambda i: (i, 0, 0))]
+        + [pl.BlockSpec((1, tokens, units), lambda i: (1 - i, 0, 0))] * 3,
+        out_specs=[whole] * 2,
         out_shape=[jax.ShapeDtypeStruct((features, units), F32)] * 2,
         cost_estimate=pl.CostEstimate(
             flops=16 * grads[0].size * units, bytes_accessed=4000000, transcendentals=0
         ),
+        compiler_params=pltpu.CompilerParams(dimension_semantics=("arbitrary",)),
     )(*grads, *hid)
 
 
@@ -145,57 +152,64 @@
     return whole
 
 
-def pair_kernel(scalars, images, texts, *refs, first, tokens, batch_total):
+def pair_kernel(scalars, images, texts, *refs, first, tokens, batch_total, block):
     if first:
-        part, loss = refs
+        part, loss, kept = refs
+        part[...] = jnp.zeros(part.shape, F32)
     else:
-        before, part, sent, loss = refs
-    at = pl.program_id(0)
-    block = texts[...]
-    logits = (
-        scalars[0]
-        * lax.dot_general(
-            images[...], block, (((1,), (1,)), ((), ())), preferred_element_type=F32
+        before, part, sent, loss, kept = refs
+        part[...] = before[...]
+    loss[...] = jnp.zeros(loss.shape, F32)
+    count = texts.shape[0] // block
+
+    def block_of(at):
+        return texts[pl.ds(pl.multiple_of(at * block, block), block), :]
+
+    def logits_of(at):
+        return (
+            scalars[0]
+            * lax.dot_general(
+                images[...], block_of(at), (((1,), (1,)), ((), ())), preferred_element_type=F32
+            )
+            + scalars[1]
         )
-        + scalars[1]
-    )
-    if first:
-        rows = lax.broadcasted_iota(jnp.int32, logits.shape, 0)
-        cols = lax.broadcasted_iota(jnp.int32, logits.shape, 1) + at * logits.shape[1]
-        positive = (rows == cols) & (rows < tokens)
-        logits = jnp.where(positive, -logits, logits)
-    small = jnp.exp(-jnp.abs(logits))
-    inverse = 1.0 / (1.0 + small)
-    slope = jnp.where(logits >= 0, inverse, small * inverse) / batch_total
-    if first:
-        slope = jnp.where(positive, -slope, slope)
-    added = jnp.dot(slope.astype(BF16), block, preferred_element_type=F32)
-    losses = jnp.sum(jnp.maximum(logits, 0.0) + jnp.log1p(small), axis=0, keepdims=True)
-
-    @pl.when(at == 0)
-    def _():
-        loss[...] = losses
-        part[...] = added if first else added + before[...]
-
-    @pl.when(at > 0)
-    def _():
-        loss[...] += losses
-        part[...] += added
-
+
+    kept[0] = logits_of(0)
+
+    def one(at, _):
+        logits = kept[at & 1]
+        kept[(at + 1) & 1] = logits_of(jnp.minimum(at + 1, count - 1))
+        if first:
+            rows = lax.broadcasted_iota(jnp.int32, logits.shape, 0)
+            cols = lax.broadcasted_iota(jnp.int32, logits.shape, 1) + at * block
+            positive = (rows == cols) & (rows < tokens)
+            logits = jnp.where(positive, -logits, logits)
+        small = jnp.exp(-jnp.abs(logits))
+        base = 1.0 + small
+        inverse = 1.0 / base
+        slope = jnp.where(logits >= 0, inverse, small * inverse) / batch_total
+        if first:
+            slope = jnp.where(positive, -slope, slope)
+        part[...] += jnp.dot(
+            slope.astype(BF16), block_of(at), preferred_element_type=F32
+        )
+        softplus = jnp.maximum(logits, 0.0) + (
+            jnp.log(base) + (small - (base - 1.0)) * inverse
+        )
+        loss[...] += jnp.sum(softplus, axis=0, keepdims=True)
+        return 0
+
+    lax.fori_loop(0, count, one, 0)
     if not first:
-
-        @pl.when(at == pl.num_programs(0) - 1)
-        def _():
-            scaled = scalars[0] * part[...]
-            part[...] = scaled
-            sent[...] = scaled.astype(BF16)
+        scaled = scalars[0] * part[...]
+        part[...] = scaled
+        sent[...] = scaled.astype(BF16)
 
 
 def pair_tiles(scalars, images, texts, before, tokens, batch_total):
     first = before is None
     count, width = images.shape
     block = 256
-    whole = pl.BlockSpec((count, width), lambda i: (0, 0))
     outs = [jax.ShapeDtypeStruct((count, width), F32)]
     if not first:
         outs.append(jax.ShapeDtypeStruct((count, width), BF16))
@@ -203,21 +217,15 @@
     pairs = count * texts.shape[0]
     return pl.pallas_call(
         functools.partial(
-            pair_kernel, first=first, tokens=tokens, batch_total=batch_total
-        ),
-        grid=(texts.shape[0] // block,),
-        in_specs=[
-            pl.BlockSpec(memory_space=pltpu.SMEM),
-            whole,
-            pl.BlockSpec((block, width), lambda i: (i, 0)),
-        ]
-        + ([] if first else [whole]),
-        out_specs=[whole] * (len(outs) - 1) + [pl.BlockSpec((1, block), lambda i: (0, 0))],
+            pair_kernel, first=first, tokens=tokens, batch_total=batch_total, block=block
+        ),
+        in_specs=[pl.BlockSpec(memory_space=pltpu.SMEM)]
+        + [pl.BlockSpec(memory_space=pltpu.VMEM)] * (2 if first else 3),
         out_shape=outs,
+        scratch_shapes=[pltpu.VMEM((2, count, block), F32)],
         cost_estimate=pl.CostEstimate(
             flops=4 * pairs * width, bytes_accessed=2 * texts.size, transcendentals=3 * pairs
         ),
-        compiler_params=pltpu.CompilerParams(dimension_semantics=("arbitrary",)),
     )(scalars, images, texts, *([] if first else [before]))
 
 

time: 283 us -> 277 us (0.979)
  Pallas kernels: 35.4 us -> 29.3 us
    pallas_call x2, Pallas kernels: 24.5 us -> 18.3 us  [pair_tiles(): pl.pallas_call(functools.partial(pair_kernel, first=first, tokens=tokens,...]
  transfers between devices with their start and end apart: 39 -> 39, of which waited for: 24 -> 24; matrix products, arithmetic and copies ran while one was open for 9% -> 9% of each run, Pallas kernels for 7% -> 6%
where the time goes in v1:
time: 277 us; the launch traced here: 274 us
  waiting for transfers between devices  112 us (40%)
  starting transfers between devices  66.4 us (24%)
  Pallas kernels  29.3 us (11%)
  local copies, waits for them, and re-layouts  24.7 us (9%)
  blocking collectives  24.5 us (9%)
  other arithmetic  12.8 us (5%)
  between operations  4.31 us (2%)
    ppermute x35, waiting for transfers between devices, shift(): return lax.ppermute(value, names, pairs)  82.4 us
    ppermute x35, starting transfers between devices, shift(): return lax.ppermute(value, names, pairs)  45.6 us
    all_to_all x4, waiting for transfers between devices, exchange(): return lax.all_to_all(pieces, axes, split_axis=0, concat_axis=0, tiled=True)  29.8 us
    all_to_all x2, blocking collectives, exchange(): return lax.all_to_all(pieces, axes, split_axis=0, concat_axis=0, tiled=True)  24.5 us
    all_to_all x4, starting transfers between devices, exchange(): return lax.all_to_all(pieces, axes, split_axis=0, concat_axis=0, tiled=True)  20.8 us
    pallas_call x2, Pallas kernels, pair_tiles(): pl.pallas_call(functools.partial(pair_kernel, first=first, tokens=tokens,...  18.3 us
    unnamed x46, local copies, waits for them, and re-layouts  11.6 us
    pallas_call x1, Pallas kernels, project(): pl.pallas_call(project_kernel, grid=(count,), in_specs=[pl.BlockSpec((1,...  6.79 us
  transfers between devices with their start and end apart: 39, of which 24 were waited for; matrix products, arithmetic and copies ran while one was open for 9% of the time, Pallas kernels for 6%

profile of v1, /device:TPU:2, one launch (start us, length us, event | category | flops | bytes accessed | tf_op | source)
XLA Modules:
  0.0 274.2 jit_solution(11663043114441411364)
XLA Ops:
  2.3 8.5 %all-to-all-start = ((bf16[8,36,538]{2,1,0:T(8,128)(2,1)}), bf16[8,36,538]{2,1,0:T(8,128)(2,1)S(1)}, u32[]{:S(2)}, u32[]{:S(2)}) async-start(bf16[8,36,538]{2,1,0:T(8,128)(2,1)} %broadcast_in_dim.12), calls=%async_computation | async-start | bytes 819200 | tf_op jit(solution)/shard_map/all_to_all | solution.py:45
  10.8 1.0 fusion.2
  13.7 3.5 %collective-permute-start.7 = (bf16[64,1152]{1,0:T(8,128)(2,1)S(1)}, bf16[64,1152]{1,0:T(8,128)(2,1)S(1)}, u32[]{:S(2)}, u32[]{:S(2)}) collective-permute-start(bf16[64,1152]{1,0:T(8,128)(2,1)S(1)} %fusion.3), channel_id=1, source_target_pairs={{0,48},{8,56},{16,32},{24,40},{32,16},{40,24},{48,0},{56,8},{1,49}... | collective-permute-start | bytes 442376 | tf_op jit(solution)/shard_map/ppermute | solution.py:41
  17.7 2.2 collective-permute-done.6
  20.0 5.9 %all-to-all-done = bf16[8,36,538]{2,1,0:T(8,128)(2,1)S(1)} async-done(((bf16[8,36,538]{2,1,0:T(8,128)(2,1)}), bf16[8,36,538]{2,1,0:T(8,128)(2,1)S(1)}, u32[]{:S(2)}, u32[]{:S(2)}) %all-to-all-start) | async-done | bytes 309920 | tf_op jit(solution)/shard_map/all_to_all | solution.py:45
  26.6 2.5 collective-permute-start.4
  29.8 2.7 collective-permute-start.10
  32.4 1.8 collective-permute-start.5
  34.5 2.2 collective-permute-done.3
  37.7 7.0 %collective-permute-done.4 = bf16[288,538]{1,0:T(8,128)(2,1)} collective-permute-done((bf16[288,538]{1,0:T(8,128)(2,1)S(1)}, bf16[288,538]{1,0:T(8,128)(2,1)}, u32[]{:S(2)}, u32[]{:S(2)}) %collective-permute-start.4) | collective-permute-done | bytes 309920 | tf_op jit(solution)/shard_map/ppermute | solution.py:41
  44.7 1.0 bitcast_dynamic-update-slice_fusion.1
  45.7 1.0 bitcast_dynamic-update-slice_fusion.own
  47.7 2.0 reshape.74
  50.2 3.1 %collective-permute-start = (bf16[4,2,64,538]{3,2,1,0:T(8,128)(2,1)S(1)}, bf16[4,2,64,538]{3,2,1,0:T(8,128)(2,1)}, u32[]{:S(2)}, u32[]{:S(2)}) collective-permute-start(bf16[4,2,64,538]{3,2,1,0:T(8,128)(2,1)S(1)} %fusion.h0), channel_id=1, source_target_pairs={{0,24},{8,0},{16,8},{24,16},{1,25},{9,1},{17,9},{25,17},{2,26},{10... | collective-permute-start | bytes 1652744 | tf_op jit(solution)/shard_map/ppermute | solution.py:41
  55.8 2.0 constant_dynamic-update-slice_fusion.7
  58.6 22.6 %collective-permute-done.h1 = bf16[4,2,64,538]{3,2,1,0:T(8,128)(2,1)} collective-permute-done((bf16[4,2,64,538]{3,2,1,0:T(8,128)(2,1)S(1)}, bf16[4,2,64,538]{3,2,1,0:T(8,128)(2,1)}, u32[]{:S(2)}, u32[]{:S(2)}) %collective-permute-start) | collective-permute-done | bytes 550944 | tf_op jit(solution)/shard_map/ppermute | solution.py:41
  81.6 3.4 %collective-permute-done.2.h3 = bf16[4,2,64,538]{3,2,1,0:T(8,128)(2,1)} collective-permute-done((bf16[4,2,64,538]{3,2,1,0:T(8,128)(2,1)S(1)}, bf16[4,2,64,538]{3,2,1,0:T(8,128)(2,1)}, u32[]{:S(2)}, u32[]{:S(2)}) %collective-permute-start.2) | collective-permute-done | bytes 550944 | tf_op jit(solution)/shard_map/ppermute | solution.py:41
  85.0 6.8 %shard_map.111 = (f32[256,288]{1,0:T(8,128)}, bf16[2,256,538]{2,1,0:T(8,128)(2,1)}, bf16[2,256,538]{2,1,0:T(8,128)(2,1)}, bf16[2,256,538]{2,1,0:T(8,128)(2,1)}, bf16[2,256,538]{2,1,0:T(8,128)(2,1)}) custom-call(bf16[4,2,64,538]{3,2,1,0:T(8,128)(2,1)} %copy-done.1, bf16[4,2,64,538]{3,2,1,0:T(8,128)(2,1)} %collective-permute-done.h1, ...), custom_call_target="tpu_custom_call" | custom-call | flops 634650624 | bytes 8000000 | tf_op jit(solution)/shard_map/pallas_call | solution.py:95
  91.8 1.8 fusion.1
  93.6 3.5 %all-to-all-start.1 = ((f32[4,64,288]{2,1,0:T(8,128)}), f32[4,64,288]{2,1,0:T(8,128)S(1)}, u32[]{:S(2)}, u32[]{:S(2)}) async-start(f32[4,64,288]{2,1,0:T(8,128)} %fusion.1), calls=%async_computation.1 | async-start | bytes 786432 | tf_op jit(solution)/shard_map/all_to_all | solution.py:45
  97.1 1.9 constant_dynamic-update-slice_fusion.5
  99.0 6.6 %all-to-all-done.1 = f32[4,64,288]{2,1,0:T(8,128)S(1)} async-done(((f32[4,64,288]{2,1,0:T(8,128)}), f32[4,64,288]{2,1,0:T(8,128)S(1)}, u32[]{:S(2)}, u32[]{:S(2)}) %all-to-all-start.1) | async-done | bytes 294944 | tf_op jit(solution)/shard_map/all_to_all | solution.py:45
  106.4 1.5 collective-permute-start.12
  107.8 2.0 constant_dynamic-update-slice_fusion.4
  109.8 3.2 %collective-permute-start.18 = (bf16[256,1152]{1,0:T(8,128)(2,1)}, bf16[256,1152]{1,0:T(8,128)(2,1)S(1)}, u32[]{:S(2)}, u32[]{:S(2)}) collective-permute-start(bf16[256,1152]{1,0:T(8,128)(2,1)} %collective-permute-done.16), channel_id=1, source_target_pairs={{0,7},{1,0},{2,1},{3,2},{4,3},{5,4},{6,5},{7,6},{8,15},{9,8},{10,9... | collective-permute-start | bytes 1769480 | tf_op jit(solution)/shard_map/ppermute | solution.py:41
  113.1 3.7 %collective-permute-start.13 = (bf16[64,1152]{1,0:T(8,128)(2,1)S(1)}, bf16[64,1152]{1,0:T(8,128)(2,1)S(1)}, u32[]{:S(2)}, u32[]{:S(2)}) collective-permute-start(bf16[64,1152]{1,0:T(8,128)(2,1)S(1)} %fusion.7), channel_id=1, source_target_pairs={{0,128},{64,192},{128,0},{192,64},{1,129},{65,193},{129,1},{193,65... | collective-permute-start | bytes 442376 | tf_op jit(solution)/shard_map/ppermute | solution.py:41
  116.8 1.0 collective-permute-start.14
  117.9 2.9 %collective-permute-done.13 = bf16[64,1152]{1,0:T(8,128)(2,1)S(1)} collective-permute-done((bf16[64,1152]{1,0:T(8,128)(2,1)S(1)}, bf16[64,1152]{1,0:T(8,128)(2,1)S(1)}, u32[]{:S(2)}, u32[]{:S(2)}) %collective-permute-start.13) | collective-permute-done | bytes 147488 | tf_op jit(solution)/shard_map/ppermute | solution.py:41
  120.8 1.5 collective-permute-done.14
  122.3 3.0 %collective-permute-done.17 = bf16[256,1152]{1,0:T(8,128)(2,1)S(1)} collective-permute-done((bf16[256,1152]{1,0:T(8,128)(2,1)}, bf16[256,1152]{1,0:T(8,128)(2,1)S(1)}, u32[]{:S(2)}, u32[]{:S(2)}) %collective-permute-start.17) | collective-permute-done | bytes 589856 | tf_op jit(solution)/shard_map/ppermute | solution.py:41
  125.5 3.2 %collective-permute-start.20 = (bf16[128,1152]{1,0:T(8,128)(2,1)S(1)}, bf16[128,1152]{1,0:T(8,128)(2,1)S(1)}, u32[]{:S(2)}, u32[]{:S(2)}) collective-permute-start(bf16[128,1152]{1,0:T(8,128)(2,1)S(1)} %slice.65), channel_id=1, source_target_pairs={{0,7},{1,0},{2,1},{3,2},{4,3},{5,4},{6,5},{7,6},{8,15},{9,8},{10,9... | collective-permute-start | bytes 884744 | tf_op jit(solution)/shard_map/ppermute | solution.py:41
  130.5 3.2 %collective-permute-done.19 = bf16[128,1152]{1,0:T(8,128)(2,1)S(1)} collective-permute-done((bf16[128,1152]{1,0:T(8,128)(2,1)S(1)}, bf16[128,1152]{1,0:T(8,128)(2,1)S(1)}, u32[]{:S(2)}, u32[]{:S(2)}) %collective-permute-start.19) | collective-permute-done | bytes 294944 | tf_op jit(solution)/shard_map/ppermute | solution.py:41
  137.1 8.8 %shard_map.112 = (f32[256,1152]{1,0:T(8,128)}, f32[1,256]{1,0:T(1,128)}) custom-call(f32[2]{0:T(128)} %pad_maximum_fusion.scalars, bf16[256,1152]{1,0:T(8,128)(2,1)} %copy-done.9, bf16[2048,1152]{1,0:T(8,128)(2,1)} %constant_dynamic-update-slice_fusion.texts), custom_call_target="tpu_custom_call" | custom-call | flops 2415919104 | bytes 4718592 | tf_op jit(solution)/shard_map/pallas_call | solution.py:218
  145.9 9.5 %shard_map.113 = (f32[256,1152]{1,0:T(8,128)}, bf16[256,1152]{1,0:T(8,128)(2,1)}, f32[1,256]{1,0:T(1,128)}) custom-call(f32[2]{0:T(128)} %pad_maximum_fusion.scalars, bf16[256,1152]{1,0:T(8,128)(2,1)} %copy-done.9, bf16[2048,1152]{1,0:T(8,128)(2,1)} %collective-permute-done.21.texts, f32[256,1152]{1,0:T(8,128)} %get-tuple-element.31.refs_0_), custom_call_target="tpu_custom_call" | custom-call | flops 2415919104 | bytes 4718592 | tf_op jit(solution)/shard_map/pallas_call | solution.py:218
  155.4 1.1 fusion.8
  156.5 2.7 collective-permute-start.24
  159.2 1.6 collective-permute-start.23
  160.8 2.0 collective-permute-start.22
  162.8 2.8 %collective-permute-start.32 = (bf16[2,4,64,538]{3,2,1,0:T(8,128)(2,1)}, bf16[2,4,64,538]{3,2,1,0:T(8,128)(2,1)S(1)}, u32[]{:S(2)}, u32[]{:S(2)}) collective-permute-start(bf16[2,4,64,538]{3,2,1,0:T(8,128)(2,1)} %bitcast.49), channel_id=1, source_target_pairs={{0,160},{32,128},{64,224},{96,192},{128,32},{160,0},{192,96},{224,... | collective-permute-start | bytes 1652744 | tf_op jit(solution)/shard_map/ppermute | solution.py:41
  165.7 1.8 collective-permute-done.23
  167.4 3.2 %collective-permute-done.22 = bf16[64,1152]{1,0:T(8,128)(2,1)S(1)} collective-permute-done((bf16[64,1152]{1,0:T(8,128)(2,1)S(1)}, bf16[64,1152]{1,0:T(8,128)(2,1)S(1)}, u32[]{:S(2)}, u32[]{:S(2)}) %collective-permute-start.22) | collective-permute-done | bytes 147488 | tf_op jit(solution)/shard_map/ppermute | solution.py:41
  170.7 1.2 multiply_reduce_fusion
  171.8 1.1 divide_convert_fusion
  173.4 1.2 collective-permute-start.25
  174.6 1.6 collective-permute-start.26
  176.2 1.3 collective-permute-done.25
  178.1 2.4 collective-permute-done.26
  180.6 2.3 collective-permute-done.27
  183.0 1.8 collective-permute-start.29
  184.8 8.9 %collective-permute-done.31 = bf16[2,4,64,538]{3,2,1,0:T(8,128)(2,1)S(1)} collective-permute-done((bf16[2,4,64,538]{3,2,1,0:T(8,128)(2,1)}, bf16[2,4,64,538]{3,2,1,0:T(8,128)(2,1)S(1)}, u32[]{:S(2)}, u32[]{:S(2)}) %collective-permute-start.31) | collective-permute-done | bytes 550944 | tf_op jit(solution)/shard_map/ppermute | solution.py:41
  193.7 4.0 %collective-permute-done.33 = bf16[2,4,64,538]{3,2,1,0:T(8,128)(2,1)S(1)} collective-permute-done((bf16[2,4,64,538]{3,2,1,0:T(8,128)(2,1)}, bf16[2,4,64,538]{3,2,1,0:T(8,128)(2,1)S(1)}, u32[]{:S(2)}, u32[]{:S(2)}) %collective-permute-start.33) | collective-permute-done | bytes 550944 | tf_op jit(solution)/shard_map/ppermute | solution.py:41
  197.7 1.5 collective-permute-done.28.refs_1_
  199.2 2.4 collective-permute-done.29.refs_2_
  201.6 4.3 %collective-permute-done.30.refs_3_ = bf16[256,288]{1,0:T(8,128)(2,1)S(1)} collective-permute-done((bf16[256,288]{1,0:T(8,128)(2,1)S(1)}, bf16[256,288]{1,0:T(8,128)(2,1)S(1)}, u32[]{:S(2)}, u32[]{:S(2)}) %collective-permute-start.30) | collective-permute-done | bytes 147488 | tf_op jit(solution)/shard_map/ppermute | solution.py:41
  206.6 4.2 %shard_map.114 = (f32[288,538]{1,0:T(8,128)}, f32[288,538]{1,0:T(8,128)}) custom-call(bf16[256,288]{1,0:T(8,128)(2,1)} %copy-done.3, bf16[256,288]{1,0:T(8,128)(2,1)} %copy-done.10, bf16[256,288]{1,0:T(8,128)(2,1)} %copy-done.11, bf16[256,288]{1,0:T(8,128)(2,1)} %copy-done.12, bf16[2,256,538]{2,1,0:T(8,128)(2,1)} %get-tuple-element.34.refs_4_, ...), custom_call_target="tpu_custom_call" | custom-call | flops 634650624 | bytes 4000000 | tf_op jit(solution)/shard_map/pallas_call | solution.py:130
  210.9 2.3 collective-permute-done.34
  213.2 1.2 add_convert_fusion
  215.2 4.2 %all-to-all-start.2 = ((bf16[8,36,538]{2,1,0:T(8,128)(2,1)}), bf16[8,36,538]{2,1,0:T(8,128)(2,1)S(1)}, u32[]{:S(2)}, u32[]{:S(2)}) async-start(bf16[8,36,538]{2,1,0:T(8,128)(2,1)} %reshape.86), calls=%async_computation.2 | async-start | bytes 819200 | tf_op jit(solution)/shard_map/all_to_all | solution.py:45
  220.1 14.7 %all-to-all-done.2 = bf16[8,36,538]{2,1,0:T(8,128)(2,1)S(1)} async-done(((bf16[8,36,538]{2,1,0:T(8,128)(2,1)}), bf16[8,36,538]{2,1,0:T(8,128)(2,1)S(1)}, u32[]{:S(2)}, u32[]{:S(2)}) %all-to-all-start.2) | async-done | bytes 309920 | tf_op jit(solution)/shard_map/all_to_all | solution.py:45
  235.7 8.0 %all_to_all.30 = f32[8,1,37]{2,1,0:T(1,128)S(1)} all-to-all(f32[8,1,37]{2,1,0:T(1,128)S(1)} %broadcast_in_dim.31), channel_id=1, replica_groups=mesh['x'=4,'k'=2,'y'=4,'z'=8] {'x','k'}, dimensions={0} | all-to-all | bytes 2368 | tf_op jit(solution)/shard_map/all_to_all | solution.py:45
  245.3 16.5 %all_to_all.31 = f32[32,3,538]{2,1,0:T(4,128)S(1)} all-to-all(f32[32,3,538]{2,1,0:T(4,128)S(1)} %broadcast_in_dim.32), channel_id=1, replica_groups=mesh['x'=4,'k'=2,'y'=4,'z'=8] {'y','z'}, dimensions={0} | all-to-all | bytes 413184 | tf_op jit(solution)/shard_map/all_to_all | solution.py:45
  262.5 1.2 broadcast_in_dim_broadcast_in_dim.3
  263.8 4.7 %all-to-all-start.5 = ((f32[8,1,128]{2,1,0:T(1,128)}), f32[8,1,128]{2,1,0:T(1,128)S(1)}, u32[]{:S(2)}, u32[]{:S(2)}) async-start(f32[8,1,128]{2,1,0:T(1,128)} %broadcast_in_dim_broadcast_in_dim.3), calls=%async_computation.5 | async-start | bytes 8192 | tf_op jit(solution)/shard_map/all_to_all | solution.py:45
  269.6 2.6 all-to-all-done.5
  (133 shorter events, 24.6 us)
Async XLA Ops:
  2.3 23.5 %all-to-all-start = ((bf16[8,36,538]{2,1,0:T(8,128)(2,1)}), bf16[8,36,538]{2,1,0:T(8,128)(2,1)S(1)}, u32[]{:S(2)}, u32[]{:S(2)}) async-start(bf16[8,36,538]{2,1,0:T(8,128)(2,1)} %broadcast_in_dim.12), calls=%async_computation | async-start | bytes 819200 | tf_op jit(solution)/shard_map/all_to_all | solution.py:45
  12.9 7.1 %collective-permute-start.6 = (bf16[64,1152]{1,0:T(8,128)(2,1)S(1)}, bf16[64,1152]{1,0:T(8,128)(2,1)S(1)}, u32[]{:S(2)}, u32[]{:S(2)}) collective-permute-start(bf16[64,1152]{1,0:T(8,128)(2,1)S(1)} %fusion.3), channel_id=1, source_target_pairs={{0,40},{8,48},{16,56},{24,32},{32,8},{40,16},{48,24},{56,0},{1,41}... | collective-permute-start | bytes 442376 | tf_op jit(solution)/shard_map/ppermute | solution.py:41
  13.7 12.9 %collective-permute-start.7 = (bf16[64,1152]{1,0:T(8,128)(2,1)S(1)}, bf16[64,1152]{1,0:T(8,128)(2,1)S(1)}, u32[]{:S(2)}, u32[]{:S(2)}) collective-permute-start(bf16[64,1152]{1,0:T(8,128)(2,1)S(1)} %fusion.3), channel_id=1, source_target_pairs={{0,48},{8,56},{16,32},{24,40},{32,16},{40,24},{48,0},{56,8},{1,49}... | collective-permute-start | bytes 442376 | tf_op jit(solution)/shard_map/ppermute | solution.py:41
  17.2 11.9 %collective-permute-start.8 = (bf16[64,1152]{1,0:T(8,128)(2,1)S(1)}, bf16[64,1152]{1,0:T(8,128)(2,1)S(1)}, u32[]{:S(2)}, u32[]{:S(2)}) collective-permute-start(bf16[64,1152]{1,0:T(8,128)(2,1)S(1)} %fusion.3), channel_id=1, source_target_pairs={{0,56},{8,32},{16,40},{24,48},{32,24},{40,0},{48,8},{56,16},{1,57}... | collective-permute-start | bytes 442376 | tf_op jit(solution)/shard_map/ppermute | solution.py:41
  26.0 10.7 %collective-permute-start.3 = (bf16[288,538]{1,0:T(8,128)(2,1)S(1)}, bf16[288,538]{1,0:T(8,128)(2,1)}, u32[]{:S(2)}, u32[]{:S(2)}) collective-permute-start(bf16[288,538]{1,0:T(8,128)(2,1)S(1)} %reshape.76), channel_id=1, source_target_pairs={{0,192},{64,0},{128,64},{192,128},{1,193},{65,1},{129,65},{193,129... | collective-permute-start | bytes 929672 | tf_op jit(solution)/shard_map/ppermute | solution.py:41
  26.6 18.1 %collective-permute-start.4 = (bf16[288,538]{1,0:T(8,128)(2,1)S(1)}, bf16[288,538]{1,0:T(8,128)(2,1)}, u32[]{:S(2)}, u32[]{:S(2)}) collective-permute-start(bf16[288,538]{1,0:T(8,128)(2,1)S(1)} %reshape.76), channel_id=1, source_target_pairs={{0,128},{64,192},{128,0},{192,64},{1,129},{65,193},{129,1},{193,65... | collective-permute-start | bytes 929672 | tf_op jit(solution)/shard_map/ppermute | solution.py:41
  29.1 17.6 %collective-permute-start.9 = (bf16[256,1152]{1,0:T(8,128)(2,1)S(1)}, bf16[256,1152]{1,0:T(8,128)(2,1)}, u32[]{:S(2)}, u32[]{:S(2)}) collective-permute-start(bf16[256,1152]{1,0:T(8,128)(2,1)S(1)} %constant_dynamic-update-slice_fusion.15), channel_id=1, source_target_pairs={{0,1},{1,2},{2,3},{3,4},{4,5},{5,6},{6,7},{7,0},{8,9},{9,10},{10,1... | collective-permute-start | bytes 1769480 | tf_op jit(solution)/shard_map/ppermute | solution.py:41
  29.8 17.0 %collective-permute-start.10 = (bf16[256,1152]{1,0:T(8,128)(2,1)S(1)}, bf16[256,1152]{1,0:T(8,128)(2,1)S(1)}, u32[]{:S(2)}, u32[]{:S(2)}) collective-permute-start(bf16[256,1152]{1,0:T(8,128)(2,1)S(1)} %constant_dynamic-update-slice_fusion.15), channel_id=1, source_target_pairs={{0,7},{1,0},{2,1},{3,2},{4,3},{5,4},{6,5},{7,6},{8,15},{9,8},{10,9... | collective-permute-start | bytes 1769480 | tf_op jit(solution)/shard_map/ppermute | solution.py:41
  32.4 13.3 %collective-permute-start.5 = (bf16[288,538]{1,0:T(8,128)(2,1)S(1)}, bf16[288,538]{1,0:T(8,128)(2,1)}, u32[]{:S(2)}, u32[]{:S(2)}) collective-permute-start(bf16[288,538]{1,0:T(8,128)(2,1)S(1)} %reshape.76), channel_id=1, source_target_pairs={{0,64},{64,128},{128,192},{192,0},{1,65},{65,129},{129,193},{193,1... | collective-permute-start | bytes 929672 | tf_op jit(solution)/shard_map/ppermute | solution.py:41
  46.7 38.3 %copy-start = (bf16[4,288,538]{2,1,0:T(8,128)(2,1)}, bf16[4,288,538]{2,1,0:T(8,128)(2,1)S(1)}, u32[]{:S(2)}) copy-start(bf16[4,288,538]{2,1,0:T(8,128)(2,1)S(1)} %bitcast_dynamic-update-slice_fusion.own) | copy-start | bytes 3718660
  46.8 0.9 copy-start.7
  46.8 38.3 %collective-permute-start.11 = (bf16[4,288,538]{2,1,0:T(8,128)(2,1)S(1)}, bf16[4,288,538]{2,1,0:T(8,128)(2,1)}, u32[]{:S(2)}, u32[]{:S(2)}) collective-permute-start(bf16[4,288,538]{2,1,0:T(8,128)(2,1)S(1)} %bitcast_dynamic-update-slice_fusion.own), channel_id=1, source_target_pairs={{0,32},{32,0},{1,33},{33,1},{2,34},{34,2},{3,35},{35,3},{4,36},{36... | collective-permute-start | bytes 3718664 | tf_op jit(solution)/shard_map/ppermute | solution.py:41
  49.8 8.0 %copy-start.8 = (bf16[256,1152]{1,0:T(8,128)(2,1)S(1)}, bf16[256,1152]{1,0:T(8,128)(2,1)}, u32[]{:S(2)}) copy-start(bf16[256,1152]{1,0:T(8,128)(2,1)} %copy-done.7) | copy-start | bytes 1769476
  50.2 34.8 %copy-start.1 = (bf16[4,2,64,538]{3,2,1,0:T(8,128)(2,1)}, bf16[4,2,64,538]{3,2,1,0:T(8,128)(2,1)S(1)}, u32[]{:S(2)}) copy-start(bf16[4,2,64,538]{3,2,1,0:T(8,128)(2,1)S(1)} %fusion.h0) | copy-start | bytes 1652740
  50.2 31.0 %collective-permute-start = (bf16[4,2,64,538]{3,2,1,0:T(8,128)(2,1)S(1)}, bf16[4,2,64,538]{3,2,1,0:T(8,128)(2,1)}, u32[]{:S(2)}, u32[]{:S(2)}) collective-permute-start(bf16[4,2,64,538]{3,2,1,0:T(8,128)(2,1)S(1)} %fusion.h0), channel_id=1, source_target_pairs={{0,24},{8,0},{16,8},{24,16},{1,25},{9,1},{17,9},{25,17},{2,26},{10... | collective-permute-start | bytes 1652744 | tf_op jit(solution)/shard_map/ppermute | solution.py:41
  53.3 28.3 %collective-permute-start.1 = (bf16[4,2,64,538]{3,2,1,0:T(8,128)(2,1)S(1)}, bf16[4,2,64,538]{3,2,1,0:T(8,128)(2,1)}, u32[]{:S(2)}, u32[]{:S(2)}) collective-permute-start(bf16[4,2,64,538]{3,2,1,0:T(8,128)(2,1)S(1)} %fusion.h0), channel_id=1, source_target_pairs={{0,16},{8,24},{16,0},{24,8},{1,17},{9,25},{17,1},{25,9},{2,18},{10... | collective-permute-start | bytes 1652744 | tf_op jit(solution)/shard_map/ppermute | solution.py:41
  54.0 31.1 %collective-permute-start.2 = (bf16[4,2,64,538]{3,2,1,0:T(8,128)(2,1)S(1)}, bf16[4,2,64,538]{3,2,1,0:T(8,128)(2,1)}, u32[]{:S(2)}, u32[]{:S(2)}) collective-permute-start(bf16[4,2,64,538]{3,2,1,0:T(8,128)(2,1)S(1)} %fusion.h0), channel_id=1, source_target_pairs={{0,8},{8,16},{16,24},{24,0},{1,9},{9,17},{17,25},{25,1},{2,10},{10... | collective-permute-start | bytes 1652744 | tf_op jit(solution)/shard_map/ppermute | solution.py:41
  55.8 41.3 %collective-permute-start.15 = (bf16[256,1152]{1,0:T(8,128)(2,1)}, bf16[256,1152]{1,0:T(8,128)(2,1)}, u32[]{:S(2)}, u32[]{:S(2)}) collective-permute-start(bf16[256,1152]{1,0:T(8,128)(2,1)} %collective-permute-done.9), channel_id=1, source_target_pairs={{0,1},{1,2},{2,3},{3,4},{4,5},{5,6},{6,7},{7,0},{8,9},{9,10},{10,1... | collective-permute-start | bytes 1769480 | tf_op jit(solution)/shard_map/ppermute | solution.py:41
  58.6 47.5 %copy-start.2 = (bf16[64,1152]{1,0:T(8,128)(2,1)S(1)}, bf16[64,1152]{1,0:T(8,128)(2,1)}, u32[]{:S(2)}) copy-start(bf16[64,1152]{1,0:T(8,128)(2,1)} %param.8) | copy-start | bytes 442372
  81.2 26.6 %collective-permute-start.16 = (bf16[256,1152]{1,0:T(8,128)(2,1)S(1)}, bf16[256,1152]{1,0:T(8,128)(2,1)}, u32[]{:S(2)}, u32[]{:S(2)}) collective-permute-start(bf16[256,1152]{1,0:T(8,128)(2,1)S(1)} %copy-done.8), channel_id=1, source_target_pairs={{0,7},{1,0},{2,1},{3,2},{4,3},{5,4},{6,5},{7,6},{8,15},{9,8},{10,9... | collective-permute-start | bytes 1769480 | tf_op jit(solution)/shard_map/ppermute | solution.py:41
  93.6 12.0 %all-to-all-start.1 = ((f32[4,64,288]{2,1,0:T(8,128)}), f32[4,64,288]{2,1,0:T(8,128)S(1)}, u32[]{:S(2)}, u32[]{:S(2)}) async-start(f32[4,64,288]{2,1,0:T(8,128)} %fusion.1), calls=%async_computation.1 | async-start | bytes 786432 | tf_op jit(solution)/shard_map/all_to_all | solution.py:45
  106.4 11.5 %collective-permute-start.12 = (bf16[64,1152]{1,0:T(8,128)(2,1)S(1)}, bf16[64,1152]{1,0:T(8,128)(2,1)S(1)}, u32[]{:S(2)}, u32[]{:S(2)}) collective-permute-start(bf16[64,1152]{1,0:T(8,128)(2,1)S(1)} %fusion.7), channel_id=1, source_target_pairs={{0,64},{64,128},{128,192},{192,0},{1,65},{65,129},{129,193},{193,1... | collective-permute-start | bytes 442376 | tf_op jit(solution)/shard_map/ppermute | solution.py:41
  109.8 15.5 %collective-permute-start.17 = (bf16[256,1152]{1,0:T(8,128)(2,1)}, bf16[256,1152]{1,0:T(8,128)(2,1)S(1)}, u32[]{:S(2)}, u32[]{:S(2)}) collective-permute-start(bf16[256,1152]{1,0:T(8,128)(2,1)} %collective-permute-done.15), channel_id=1, source_target_pairs={{0,1},{1,2},{2,3},{3,4},{4,5},{5,6},{6,7},{7,0},{8,9},{9,10},{10,1... | collective-permute-start | bytes 1769480 | tf_op jit(solution)/shard_map/ppermute | solution.py:41
  109.8 15.6 %collective-permute-start.18 = (bf16[256,1152]{1,0:T(8,128)(2,1)}, bf16[256,1152]{1,0:T(8,128)(2,1)S(1)}, u32[]{:S(2)}, u32[]{:S(2)}) collective-permute-start(bf16[256,1152]{1,0:T(8,128)(2,1)} %collective-permute-done.16), channel_id=1, source_target_pairs={{0,7},{1,0},{2,1},{3,2},{4,3},{5,4},{6,5},{7,6},{8,15},{9,8},{10,9... | collective-permute-start | bytes 1769480 | tf_op jit(solution)/shard_map/ppermute | solution.py:41
  113.1 7.7 %collective-permute-start.13 = (bf16[64,1152]{1,0:T(8,128)(2,1)S(1)}, bf16[64,1152]{1,0:T(8,128)(2,1)S(1)}, u32[]{:S(2)}, u32[]{:S(2)}) collective-permute-start(bf16[64,1152]{1,0:T(8,128)(2,1)S(1)} %fusion.7), channel_id=1, source_target_pairs={{0,128},{64,192},{128,0},{192,64},{1,129},{65,193},{129,1},{193,65... | collective-permute-start | bytes 442376 | tf_op jit(solution)/shard_map/ppermute | solution.py:41
  116.8 5.5 %collective-permute-start.14 = (bf16[64,1152]{1,0:T(8,128)(2,1)S(1)}, bf16[64,1152]{1,0:T(8,128)(2,1)S(1)}, u32[]{:S(2)}, u32[]{:S(2)}) collective-permute-start(bf16[64,1152]{1,0:T(8,128)(2,1)S(1)} %fusion.7), channel_id=1, source_target_pairs={{0,192},{64,0},{128,64},{192,128},{1,193},{65,1},{129,65},{193,129... | collective-permute-start | bytes 442376 | tf_op jit(solution)/shard_map/ppermute | solution.py:41
  122.3 14.8 %copy-start.9 = (bf16[256,1152]{1,0:T(8,128)(2,1)}, bf16[256,1152]{1,0:T(8,128)(2,1)S(1)}, u32[]{:S(2)}) copy-start(bf16[256,1152]{1,0:T(8,128)(2,1)S(1)} %constant_dynamic-update-slice_fusion.12.images) | copy-start | bytes 1769476
  125.4 8.2 %collective-permute-start.19 = (bf16[128,1152]{1,0:T(8,128)(2,1)S(1)}, bf16[128,1152]{1,0:T(8,128)(2,1)S(1)}, u32[]{:S(2)}, u32[]{:S(2)}) collective-permute-start(bf16[128,1152]{1,0:T(8,128)(2,1)S(1)} %slice.64), channel_id=1, source_target_pairs={{0,1},{1,2},{2,3},{3,4},{4,5},{5,6},{6,7},{7,0},{8,9},{9,10},{10,1... | collective-permute-start | bytes 884744 | tf_op jit(solution)/shard_map/ppermute | solution.py:41
  125.5 8.1 %collective-permute-start.20 = (bf16[128,1152]{1,0:T(8,128)(2,1)S(1)}, bf16[128,1152]{1,0:T(8,128)(2,1)S(1)}, u32[]{:S(2)}, u32[]{:S(2)}) collective-permute-start(bf16[128,1152]{1,0:T(8,128)(2,1)S(1)} %slice.65), channel_id=1, source_target_pairs={{0,7},{1,0},{2,1},{3,2},{4,3},{5,4},{6,5},{7,6},{8,15},{9,8},{10,9... | collective-permute-start | bytes 884744 | tf_op jit(solution)/shard_map/ppermute | solution.py:41
  135.1 10.8 %collective-permute-start.21 = (bf16[2048,1152]{1,0:T(8,128)(2,1)}, bf16[2048,1152]{1,0:T(8,128)(2,1)}, u32[]{:S(2)}, u32[]{:S(2)}) collective-permute-start(bf16[2048,1152]{1,0:T(8,128)(2,1)} %constant_dynamic-update-slice_fusion.texts), channel_id=1, source_target_pairs={{0,32},{32,0},{1,33},{33,1},{2,34},{34,2},{3,35},{35,3},{4,36},{36... | collective-permute-start | bytes 14155784 | tf_op jit(solution)/shard_map/ppermute | solution.py:41
  156.5 9.2 %collective-permute-start.24 = (bf16[64,1152]{1,0:T(8,128)(2,1)S(1)}, bf16[64,1152]{1,0:T(8,128)(2,1)S(1)}, u32[]{:S(2)}, u32[]{:S(2)}) collective-permute-start(bf16[64,1152]{1,0:T(8,128)(2,1)S(1)} %get-tuple-element.49), channel_id=1, source_target_pairs={{0,64},{64,128},{128,192},{192,0},{1,65},{65,129},{129,193},{193,1... | collective-permute-start | bytes 442376 | tf_op jit(solution)/shard_map/ppermute | solution.py:41
  159.2 8.3 %collective-permute-start.23 = (bf16[64,1152]{1,0:T(8,128)(2,1)S(1)}, bf16[64,1152]{1,0:T(8,128)(2,1)S(1)}, u32[]{:S(2)}, u32[]{:S(2)}) collective-permute-start(bf16[64,1152]{1,0:T(8,128)(2,1)S(1)} %get-tuple-element.50), channel_id=1, source_target_pairs={{0,128},{64,192},{128,0},{192,64},{1,129},{65,193},{129,1},{193,65... | collective-permute-start | bytes 442376 | tf_op jit(solution)/shard_map/ppermute | solution.py:41
  160.8 9.9 %collective-permute-start.22 = (bf16[64,1152]{1,0:T(8,128)(2,1)S(1)}, bf16[64,1152]{1,0:T(8,128)(2,1)S(1)}, u32[]{:S(2)}, u32[]{:S(2)}) collective-permute-start(bf16[64,1152]{1,0:T(8,128)(2,1)S(1)} %get-tuple-element.48), channel_id=1, source_target_pairs={{0,192},{64,0},{128,64},{192,128},{1,193},{65,1},{129,65},{193,129... | collective-permute-start | bytes 442376 | tf_op jit(solution)/shard_map/ppermute | solution.py:41
  162.8 30.8 %collective-permute-start.31 = (bf16[2,4,64,538]{3,2,1,0:T(8,128)(2,1)}, bf16[2,4,64,538]{3,2,1,0:T(8,128)(2,1)S(1)}, u32[]{:S(2)}, u32[]{:S(2)}) collective-permute-start(bf16[2,4,64,538]{3,2,1,0:T(8,128)(2,1)} %bitcast.15), channel_id=1, source_target_pairs={{0,96},{32,64},{64,160},{96,128},{128,224},{160,192},{192,32},{224... | collective-permute-start | bytes 1652744 | tf_op jit(solution)/shard_map/ppermute | solution.py:41
  162.8 30.8 %collective-permute-start.32 = (bf16[2,4,64,538]{3,2,1,0:T(8,128)(2,1)}, bf16[2,4,64,538]{3,2,1,0:T(8,128)(2,1)S(1)}, u32[]{:S(2)}, u32[]{:S(2)}) collective-permute-start(bf16[2,4,64,538]{3,2,1,0:T(8,128)(2,1)} %bitcast.49), channel_id=1, source_target_pairs={{0,160},{32,128},{64,224},{96,192},{128,32},{160,0},{192,96},{224,... | collective-permute-start | bytes 1652744 | tf_op jit(solution)/shard_map/ppermute | solution.py:41
  165.6 32.0 %collective-permute-start.33 = (bf16[2,4,64,538]{3,2,1,0:T(8,128)(2,1)}, bf16[2,4,64,538]{3,2,1,0:T(8,128)(2,1)S(1)}, u32[]{:S(2)}, u32[]{:S(2)}) collective-permute-start(bf16[2,4,64,538]{3,2,1,0:T(8,128)(2,1)} %bitcast.48), channel_id=1, source_target_pairs={{0,224},{32,192},{64,32},{96,0},{128,96},{160,64},{192,160},{224,1... | collective-permute-start | bytes 1652744 | tf_op jit(solution)/shard_map/ppermute | solution.py:41
  172.9 46.5 %copy-start.16 = (f32[1,256]{1,0:T(1,128)S(1)}, f32[1,256]{1,0:T(1,128)}, u32[]{:S(2)}) copy-start(f32[1,256]{1,0:T(1,128)} %get-tuple-element.40) | copy-start | bytes 3076
  172.9 46.5 %copy-start.17 = (f32[1,256]{1,0:T(1,128)S(1)}, f32[1,256]{1,0:T(1,128)}, u32[]{:S(2)}) copy-start(f32[1,256]{1,0:T(1,128)} %get-tuple-element.41) | copy-start | bytes 3076
  173.0 71.4 %copy-start.18 = (f32[36]{0:T(128)S(1)}, f32[36]{0:T(128)}, u32[]{:S(2)}) copy-start(f32[36]{0:T(128)} %param.12) | copy-start | bytes 436
  173.4 4.2 %collective-permute-start.25 = (bf16[64,288]{1,0:T(8,128)(2,1)S(1)}, bf16[64,288]{1,0:T(8,128)(2,1)S(1)}, u32[]{:S(2)}, u32[]{:S(2)}) collective-permute-start(bf16[64,288]{1,0:T(8,128)(2,1)S(1)} %get-tuple-element.53), channel_id=1, source_target_pairs={{0,24},{8,0},{16,8},{24,16},{1,25},{9,1},{17,9},{25,17},{2,26},{10... | collective-permute-start | bytes 110600 | tf_op jit(solution)/shard_map/ppermute | solution.py:41
  174.6 87.3 %copy-start.14 = (f32[538]{0:T(1024)S(1)}, f32[538]{0:T(1024)}, u32[]{:S(2)}) copy-start(f32[538]{0:T(1024)} %param.13) | copy-start | bytes 6460
  174.6 5.9 %collective-permute-start.26 = (bf16[64,288]{1,0:T(8,128)(2,1)S(1)}, bf16[64,288]{1,0:T(8,128)(2,1)S(1)}, u32[]{:S(2)}, u32[]{:S(2)}) collective-permute-start(bf16[64,288]{1,0:T(8,128)(2,1)S(1)} %get-tuple-element.52), channel_id=1, source_target_pairs={{0,16},{8,24},{16,0},{24,8},{1,17},{9,25},{17,1},{25,9},{2,18},{10... | collective-permute-start | bytes 110600 | tf_op jit(solution)/shard_map/ppermute | solution.py:41
  177.5 5.3 %collective-permute-start.27 = (bf16[64,288]{1,0:T(8,128)(2,1)S(1)}, bf16[64,288]{1,0:T(8,128)(2,1)S(1)}, u32[]{:S(2)}, u32[]{:S(2)}) collective-permute-start(bf16[64,288]{1,0:T(8,128)(2,1)S(1)} %get-tuple-element.51), channel_id=1, source_target_pairs={{0,8},{8,16},{16,24},{24,0},{1,9},{9,17},{17,25},{25,1},{2,10},{10... | collective-permute-start | bytes 110600 | tf_op jit(solution)/shard_map/ppermute | solution.py:41
  182.9 23.0 %copy-start.3 = (bf16[256,288]{1,0:T(8,128)(2,1)}, bf16[256,288]{1,0:T(8,128)(2,1)S(1)}, u32[]{:S(2)}) copy-start(bf16[256,288]{1,0:T(8,128)(2,1)S(1)} %constant_dynamic-update-slice_fusion.9.refs_0_) | copy-start | bytes 442372
  182.9 16.3 %collective-permute-start.28 = (bf16[256,288]{1,0:T(8,128)(2,1)S(1)}, bf16[256,288]{1,0:T(8,128)(2,1)S(1)}, u32[]{:S(2)}, u32[]{:S(2)}) collective-permute-start(bf16[256,288]{1,0:T(8,128)(2,1)S(1)} %constant_dynamic-update-slice_fusion.9.refs_0_), channel_id=1, source_target_pairs={{0,96},{32,64},{64,160},{96,128},{128,224},{160,192},{192,32},{224... | collective-permute-start | bytes 442376 | tf_op jit(solution)/shard_map/ppermute | solution.py:41
  183.0 18.6 %collective-permute-start.29 = (bf16[256,288]{1,0:T(8,128)(2,1)S(1)}, bf16[256,288]{1,0:T(8,128)(2,1)S(1)}, u32[]{:S(2)}, u32[]{:S(2)}) collective-permute-start(bf16[256,288]{1,0:T(8,128)(2,1)S(1)} %constant_dynamic-update-slice_fusion.9.refs_0_), channel_id=1, source_target_pairs={{0,160},{32,128},{64,224},{96,192},{128,32},{160,0},{192,96},{224,... | collective-permute-start | bytes 442376 | tf_op jit(solution)/shard_map/ppermute | solution.py:41
  193.7 12.2 %copy-start.4 = (bf16[2,4,64,538]{3,2,1,0:T(8,128)(2,1)}, bf16[2,4,64,538]{3,2,1,0:T(8,128)(2,1)S(1)}, u32[]{:S(2)}) copy-start(bf16[2,4,64,538]{3,2,1,0:T(8,128)(2,1)S(1)} %collective-permute-done.31) | copy-start | bytes 1652740
  193.7 12.2 %collective-permute-start.30 = (bf16[256,288]{1,0:T(8,128)(2,1)S(1)}, bf16[256,288]{1,0:T(8,128)(2,1)S(1)}, u32[]{:S(2)}, u32[]{:S(2)}) collective-permute-start(bf16[256,288]{1,0:T(8,128)(2,1)S(1)} %constant_dynamic-update-slice_fusion.9.refs_0_), channel_id=1, source_target_pairs={{0,224},{32,192},{64,32},{96,0},{128,96},{160,64},{192,160},{224,1... | collective-permute-start | bytes 442376 | tf_op jit(solution)/shard_map/ppermute | solution.py:41
  193.7 12.2 %copy-start.5 = (bf16[2,4,64,538]{3,2,1,0:T(8,128)(2,1)}, bf16[2,4,64,538]{3,2,1,0:T(8,128)(2,1)S(1)}, u32[]{:S(2)}) copy-start(bf16[2,4,64,538]{3,2,1,0:T(8,128)(2,1)S(1)} %collective-permute-done.32) | copy-start | bytes 1652740
  197.7 8.2 %copy-start.6 = (bf16[2,4,64,538]{3,2,1,0:T(8,128)(2,1)}, bf16[2,4,64,538]{3,2,1,0:T(8,128)(2,1)S(1)}, u32[]{:S(2)}) copy-start(bf16[2,4,64,538]{3,2,1,0:T(8,128)(2,1)S(1)} %collective-permute-done.33) | copy-start | bytes 1652740
  199.2 6.7 %copy-start.10 = (bf16[256,288]{1,0:T(8,128)(2,1)}, bf16[256,288]{1,0:T(8,128)(2,1)S(1)}, u32[]{:S(2)}) copy-start(bf16[256,288]{1,0:T(8,128)(2,1)S(1)} %collective-permute-done.28.refs_1_) | copy-start | bytes 442372
  201.6 4.4 %copy-start.11 = (bf16[256,288]{1,0:T(8,128)(2,1)}, bf16[256,288]{1,0:T(8,128)(2,1)S(1)}, u32[]{:S(2)}) copy-start(bf16[256,288]{1,0:T(8,128)(2,1)S(1)} %collective-permute-done.29.refs_2_) | copy-start | bytes 442372
  205.9 0.7 copy-start.12
  210.8 2.4 collective-permute-start.34
  215.2 19.6 %all-to-all-start.2 = ((bf16[8,36,538]{2,1,0:T(8,128)(2,1)}), bf16[8,36,538]{2,1,0:T(8,128)(2,1)S(1)}, u32[]{:S(2)}, u32[]{:S(2)}) async-start(bf16[8,36,538]{2,1,0:T(8,128)(2,1)} %reshape.86), calls=%async_computation.2 | async-start | bytes 819200 | tf_op jit(solution)/shard_map/all_to_all | solution.py:45
  244.4 28.7 %copy-start.15 = (f32[36]{0:T(128)}, f32[36]{0:T(128)S(1)}, u32[]{:S(2)}) copy-start(f32[36]{0:T(128)S(1)} %multiply_add_fusion.1) | copy-start | bytes 436
  262.5 10.6 %copy-start.13 = (f32[538]{0:T(1024)}, f32[538]{0:T(1024)S(1)}, u32[]{:S(2)}) copy-start(f32[538]{0:T(1024)S(1)} %get-tuple-element.47) | copy-start | bytes 6460
  263.8 8.5 %all-to-all-start.5 = ((f32[8,1,128]{2,1,0:T(1,128)}), f32[8,1,128]{2,1,0:T(1,128)S(1)}, u32[]{:S(2)}, u32[]{:S(2)}) async-start(f32[8,1,128]{2,1,0:T(1,128)} %broadcast_in_dim_broadcast_in_dim.3), calls=%async_computation.5 | async-start | bytes 8192 | tf_op jit(solution)/shard_map/all_to_all | solution.py:45

commit v2 on v1

--- a/solution.py
+++ b/solution.py
@@ -47,10 +47,6 @@
 
 def everywhere(array, axes):
     return exchange(jnp.broadcast_to(array, (lax.axis_size(axes), *array.shape)), axes)
-
-
-def after(values, *others):
-    return lax.optimization_barrier((values, others))[0]
 
 
 def rolled(pieces, by, count):
@@ -255,13 +251,17 @@
 
     up, down = ring_step(texts_y, texts_y, "z")
     ring_pieces = [texts_y, up, down]
+    up, down = ring_step(up, down, "z")
+    ring_pieces += [up, down]
+    up, down = ring_step(up, down, "z")
+    ring_pieces += [up, down]
+    half = texts_y.shape[0] // 2
+    ring_pieces += ring_step(up[:half], down[half:], "z")
 
     weight_z = everywhere(weight.astype(BF16), "z").reshape(quarter, half_ff)
     weight_own = [weight_z] + [shift(weight_z, x=-s) for s in (1, 2, 3)]
     weight_own = joined([w[None] for w in weight_own])
-    weight_other = shift(after(weight_own, up, down), k=1)
-    up, down = ring_step(up, down, "z")
-    ring_pieces += [up, down]
+    weight_other = shift(weight_own, k=1)
     mixed_part, *hid_all = project(hid_y, weight_own, weight_other)
     mixed_part = mixed_part.reshape(4, tokens, quarter)
 
@@ -275,14 +275,10 @@
     length = jnp.sqrt(jnp.sum(mixed * mixed, axis=1, keepdims=True) + EPSILON)
     unit = mixed / length
     images = unit.astype(BF16)
-    up, down = ring_step(*after((up, down), mixed_part), "z")
-    ring_pieces += [up, down]
-    half = texts_y.shape[0] // 2
-    ring_pieces += ring_step(*after((up[:half], down[half:]), images), "z")
 
     logit_scale = jnp.exp(log_scale)
     image_rows = joined([images] + [shift(images, x=s) for s in (1, 2, 3)])
-    texts_own = jnp.concatenate(ring_pieces[:-2] + after(ring_pieces[-2:], image_rows))
+    texts_own = jnp.concatenate(ring_pieces)
     texts_other = shift(texts_own, k=1)
     scalars = jnp.stack([logit_scale, bias])
     part_a, loss_a = pair_tiles(scalars, image_rows, texts_own, None, tokens, batch_total)
@@ -312,13 +308,13 @@
     loss_row = row_total[-1]
     new_row = DECAY_RATE * row_moment + (1.0 - DECAY_RATE) * row_total[:-1] / FF
     scaled = jnp.sum(gradient * gradient / new_row[:, None], axis=0)
-    col_message = jnp.stack(
-        [jnp.sum(squared, axis=0), scaled, jnp.full((slice_ff,), loss_row)]
-    )
-    col_total = jnp.sum(everywhere(col_message, COL), axis=0)
-    new_col = DECAY_RATE * col_moment + (1.0 - DECAY_RATE) * col_total[0] / D
-    loss = col_total[2, 0] / batch_total
-    ours = jnp.sum(col_total[1] / new_col)
+    col_message = jnp.concatenate(
+        [jnp.sum(squared, axis=0), scaled, loss_row.reshape(1)]
+    ).reshape(1, 2 * slice_ff + 1)
+    col_total = jnp.sum(everywhere(col_message, COL), axis=(0, 1))
+    new_col = DECAY_RATE * col_moment + (1.0 - DECAY_RATE) * col_total[:slice_ff] / D
+    loss = col_total[-1] / batch_total
+    ours = jnp.sum(col_total[slice_ff:-1] / new_col)
     update_total = jnp.sum(everywhere(jnp.full((1, 128), ours), ROW), axis=(0, 1))[0]
     update_rms = jnp.sqrt(update_total / (D * FF))
     raw_update = gradient / jnp.sqrt(new_row[:, None] * new_col[None, :])

time: 277 us -> 308 us (1.11)
  waiting for transfers between devices: 112 us -> 139 us
  blocking collectives: 24.5 us -> 33.4 us
  local copies, waits for them, and re-layouts: 24.7 us -> 19.5 us
    ppermute x35, waiting for transfers between devices: 82.4 us -> 121 us  [shift(): return lax.ppermute(value, names, pairs)]
    all_to_all x4 -> x3, waiting for transfers between devices: 29.8 us -> 17.3 us  [exchange(): return lax.all_to_all(pieces, axes, split_axis=0, concat_axis=0, tiled=True)]
    all_to_all x2 -> x3, blocking collectives: 24.5 us -> 33.4 us  [exchange(): return lax.all_to_all(pieces, axes, split_axis=0, concat_axis=0, tiled=True)]
    ppermute x35, starting transfers between devices: 45.6 us -> 53.6 us  [shift(): return lax.ppermute(value, names, pairs)]
    all_to_all x4 -> x3, starting transfers between devices: 20.8 us -> 14.6 us  [exchange(): return lax.all_to_all(pieces, axes, split_axis=0, concat_axis=0, tiled=True)]
    unnamed x46, local copies, waits for them, and re-layouts: 11.6 us -> 8.47 us
  transfers between devices with their start and end apart: 39 -> 38, of which waited for: 24 -> 25; matrix products, arithmetic and copies ran while one was open for 9% -> 6% of each run, Pallas kernels for 6% -> 5%
where the time goes in v2:
time: 308 us; the launch traced here: 305 us
  waiting for transfers between devices  139 us (45%)
  starting transfers between devices  68.3 us (22%)
  blocking collectives  33.4 us (11%)
  Pallas kernels  29.2 us (9%)
  local copies, waits for them, and re-layouts  19.5 us (6%)
  other arithmetic  12.1 us (4%)
  between operations  4.31 us (1%)
    ppermute x35, waiting for transfers between devices, shift(): return lax.ppermute(value, names, pairs)  121 us
    ppermute x35, starting transfers between devices, shift(): return lax.ppermute(value, names, pairs)  53.6 us
    all_to_all x3, blocking collectives, exchange(): return lax.all_to_all(pieces, axes, split_axis=0, concat_axis=0, tiled=True)  33.4 us
    pallas_call x2, Pallas kernels, pair_tiles(): pl.pallas_call(functools.partial(pair_kernel, first=first, tokens=tokens,...  18.3 us
    all_to_all x3, waiting for transfers between devices, exchange(): return lax.all_to_all(pieces, axes, split_axis=0, concat_axis=0, tiled=True)  17.3 us
    all_to_all x3, starting transfers between devices, exchange(): return lax.all_to_all(pieces, axes, split_axis=0, concat_axis=0, tiled=True)  14.6 us
    unnamed x46, local copies, waits for them, and re-layouts  8.47 us
    pallas_call x1, Pallas kernels, project(): pl.pallas_call(project_kernel, grid=(count,), in_specs=[pl.BlockSpec((1,...  6.71 us
  transfers between devices with their start and end apart: 38, of which 25 were waited for; matrix products, arithmetic and copies ran while one was open for 6% of the time, Pallas kernels for 5%

profile of v2, /device:TPU:2, one launch (start us, length us, event | category | flops | bytes accessed | tf_op | source)
XLA Modules:
  0.0 305.4 jit_solution(14040606787367701391)
XLA Ops:
  0.6 1.0 fusion.2
  1.7 1.0 fusion.3
  2.7 1.1 collective-permute-start.10
  3.8 3.2 %collective-permute-start.11 = (bf16[64,1152]{1,0:T(8,128)(2,1)S(1)}, bf16[64,1152]{1,0:T(8,128)(2,1)S(1)}, u32[]{:S(2)}, u32[]{:S(2)}) collective-permute-start(bf16[64,1152]{1,0:T(8,128)(2,1)S(1)} %fusion.3), channel_id=1, source_target_pairs={{0,48},{8,56},{16,32},{24,40},{32,16},{40,24},{48,0},{56,8},{1,49}... | collective-permute-start | bytes 442376 | tf_op jit(solution)/shard_map/ppermute | solution.py:41
  7.8 2.0 collective-permute-done.10
  9.8 4.7 %collective-permute-done.11 = bf16[64,1152]{1,0:T(8,128)(2,1)S(1)} collective-permute-done((bf16[64,1152]{1,0:T(8,128)(2,1)S(1)}, bf16[64,1152]{1,0:T(8,128)(2,1)S(1)}, u32[]{:S(2)}, u32[]{:S(2)}) %collective-permute-start.11) | collective-permute-done | bytes 147488 | tf_op jit(solution)/shard_map/ppermute | solution.py:41
  14.6 2.0 collective-permute-start.13
  16.6 4.0 %collective-permute-start.14 = (bf16[256,1152]{1,0:T(8,128)(2,1)S(1)}, bf16[256,1152]{1,0:T(8,128)(2,1)S(1)}, u32[]{:S(2)}, u32[]{:S(2)}) collective-permute-start(bf16[256,1152]{1,0:T(8,128)(2,1)S(1)} %constant_dynamic-update-slice_fusion.12), channel_id=1, source_target_pairs={{0,7},{1,0},{2,1},{3,2},{4,3},{5,4},{6,5},{7,6},{8,15},{9,8},{10,9... | collective-permute-start | bytes 1769480 | tf_op jit(solution)/shard_map/ppermute | solution.py:41
  20.6 13.5 %collective-permute-done.13 = bf16[256,1152]{1,0:T(8,128)(2,1)S(1)} collective-permute-done((bf16[256,1152]{1,0:T(8,128)(2,1)S(1)}, bf16[256,1152]{1,0:T(8,128)(2,1)S(1)}, u32[]{:S(2)}, u32[]{:S(2)}) %collective-permute-start.13) | collective-permute-done | bytes 589856 | tf_op jit(solution)/shard_map/ppermute | solution.py:41
  34.1 3.2 %collective-permute-start.16 = (bf16[256,1152]{1,0:T(8,128)(2,1)S(1)}, bf16[256,1152]{1,0:T(8,128)(2,1)S(1)}, u32[]{:S(2)}, u32[]{:S(2)}) collective-permute-start(bf16[256,1152]{1,0:T(8,128)(2,1)S(1)} %collective-permute-done.14), channel_id=1, source_target_pairs={{0,7},{1,0},{2,1},{3,2},{4,3},{5,4},{6,5},{7,6},{8,15},{9,8},{10,9... | collective-permute-start | bytes 1769480 | tf_op jit(solution)/shard_map/ppermute | solution.py:41
  39.0 5.6 %all-to-all-start = ((bf16[8,36,538]{2,1,0:T(8,128)(2,1)}), bf16[8,36,538]{2,1,0:T(8,128)(2,1)S(1)}, u32[]{:S(2)}, u32[]{:S(2)}) async-start(bf16[8,36,538]{2,1,0:T(8,128)(2,1)} %broadcast_in_dim.12), calls=%async_computation | async-start | bytes 819200 | tf_op jit(solution)/shard_map/all_to_all | solution.py:45
  46.4 7.1 %collective-permute-done.15 = bf16[256,1152]{1,0:T(8,128)(2,1)S(1)} collective-permute-done((bf16[256,1152]{1,0:T(8,128)(2,1)S(1)}, bf16[256,1152]{1,0:T(8,128)(2,1)S(1)}, u32[]{:S(2)}, u32[]{:S(2)}) %collective-permute-start.15) | collective-permute-done | bytes 589856 | tf_op jit(solution)/shard_map/ppermute | solution.py:41
  54.3 4.1 %collective-permute-start.18 = (bf16[256,1152]{1,0:T(8,128)(2,1)S(1)}, bf16[256,1152]{1,0:T(8,128)(2,1)S(1)}, u32[]{:S(2)}, u32[]{:S(2)}) collective-permute-start(bf16[256,1152]{1,0:T(8,128)(2,1)S(1)} %collective-permute-done.16), channel_id=1, source_target_pairs={{0,7},{1,0},{2,1},{3,2},{4,3},{5,4},{6,5},{7,6},{8,15},{9,8},{10,9... | collective-permute-start | bytes 1769480 | tf_op jit(solution)/shard_map/ppermute | solution.py:41
  61.1 10.4 %collective-permute-done.17 = bf16[256,1152]{1,0:T(8,128)(2,1)S(1)} collective-permute-done((bf16[256,1152]{1,0:T(8,128)(2,1)S(1)}, bf16[256,1152]{1,0:T(8,128)(2,1)S(1)}, u32[]{:S(2)}, u32[]{:S(2)}) %collective-permute-start.17) | collective-permute-done | bytes 589856 | tf_op jit(solution)/shard_map/ppermute | solution.py:41
  71.7 3.3 %collective-permute-start.20 = (bf16[128,1152]{1,0:T(8,128)(2,1)S(1)}, bf16[128,1152]{1,0:T(8,128)(2,1)S(1)}, u32[]{:S(2)}, u32[]{:S(2)}) collective-permute-start(bf16[128,1152]{1,0:T(8,128)(2,1)S(1)} %slice.65), channel_id=1, source_target_pairs={{0,7},{1,0},{2,1},{3,2},{4,3},{5,4},{6,5},{7,6},{8,15},{9,8},{10,9... | collective-permute-start | bytes 884744 | tf_op jit(solution)/shard_map/ppermute | solution.py:41
  76.8 3.6 %collective-permute-done.19 = bf16[128,1152]{1,0:T(8,128)(2,1)S(1)} collective-permute-done((bf16[128,1152]{1,0:T(8,128)(2,1)S(1)}, bf16[128,1152]{1,0:T(8,128)(2,1)S(1)}, u32[]{:S(2)}, u32[]{:S(2)}) %collective-permute-start.19) | collective-permute-done | bytes 294944 | tf_op jit(solution)/shard_map/ppermute | solution.py:41
  82.7 2.4 collective-permute-start.4
  85.1 1.8 collective-permute-start.5
  87.1 6.1 %collective-permute-done.3 = bf16[288,538]{1,0:T(8,128)(2,1)} collective-permute-done((bf16[288,538]{1,0:T(8,128)(2,1)S(1)}, bf16[288,538]{1,0:T(8,128)(2,1)}, u32[]{:S(2)}, u32[]{:S(2)}) %collective-permute-start.3) | collective-permute-done | bytes 309920 | tf_op jit(solution)/shard_map/ppermute | solution.py:41
  93.2 1.0 bitcast_dynamic-update-slice_fusion.2
  94.3 7.8 %collective-permute-done.4 = bf16[288,538]{1,0:T(8,128)(2,1)} collective-permute-done((bf16[288,538]{1,0:T(8,128)(2,1)S(1)}, bf16[288,538]{1,0:T(8,128)(2,1)}, u32[]{:S(2)}, u32[]{:S(2)}) %collective-permute-start.4) | collective-permute-done | bytes 309920 | tf_op jit(solution)/shard_map/ppermute | solution.py:41
  102.1 1.0 bitcast_dynamic-update-slice_fusion.1
  104.6 2.2 collective-permute-start
  106.8 1.2 collective-permute-start.1
  108.0 1.2 collective-permute-start.2
  109.2 26.3 %collective-permute-done.h1 = bf16[4,2,64,538]{3,2,1,0:T(8,128)(2,1)S(1)} collective-permute-done((bf16[4,2,64,538]{3,2,1,0:T(8,128)(2,1)S(1)}, bf16[4,2,64,538]{3,2,1,0:T(8,128)(2,1)S(1)}, u32[]{:S(2)}, u32[]{:S(2)}) %collective-permute-start) | collective-permute-done | bytes 550944 | tf_op jit(solution)/shard_map/ppermute | solution.py:41
  135.6 3.8 %collective-permute-done.2.h3 = bf16[4,2,64,538]{3,2,1,0:T(8,128)(2,1)} collective-permute-done((bf16[4,2,64,538]{3,2,1,0:T(8,128)(2,1)S(1)}, bf16[4,2,64,538]{3,2,1,0:T(8,128)(2,1)}, u32[]{:S(2)}, u32[]{:S(2)}) %collective-permute-start.2) | collective-permute-done | bytes 550944 | tf_op jit(solution)/shard_map/ppermute | solution.py:41
  139.4 6.7 %shard_map.111 = (f32[256,288]{1,0:T(8,128)}, bf16[2,256,538]{2,1,0:T(8,128)(2,1)}, bf16[2,256,538]{2,1,0:T(8,128)(2,1)}, bf16[2,256,538]{2,1,0:T(8,128)(2,1)}, bf16[2,256,538]{2,1,0:T(8,128)(2,1)}) custom-call(bf16[4,2,64,538]{3,2,1,0:T(8,128)(2,1)} %copy-done.1, bf16[4,2,64,538]{3,2,1,0:T(8,128)(2,1)} %copy-done.7, ...), custom_call_target="tpu_custom_call" | custom-call | flops 634650624 | bytes 8000000 | tf_op jit(solution)/shard_map/pallas_call | solution.py:91
  146.1 1.1 fusion.1
  147.1 10.9 %all_to_all.30 = f32[4,64,288]{2,1,0:T(8,128)S(1)} all-to-all(f32[4,64,288]{2,1,0:T(8,128)S(1)} %fusion.1), channel_id=1, replica_groups=mesh['x'=4,'k'=2,'y'=4,'z'=8] {'y'}, dimensions={0} | all-to-all | bytes 589824 | tf_op jit(solution)/shard_map/all_to_all | solution.py:45
  158.8 1.2 collective-permute-start.7
  162.1 3.4 %collective-permute-start.8 = (bf16[64,1152]{1,0:T(8,128)(2,1)S(1)}, bf16[64,1152]{1,0:T(8,128)(2,1)S(1)}, u32[]{:S(2)}, u32[]{:S(2)}) collective-permute-start(bf16[64,1152]{1,0:T(8,128)(2,1)S(1)} %fusion.8), channel_id=1, source_target_pairs={{0,128},{64,192},{128,0},{192,64},{1,129},{65,193},{129,1},{193,65... | collective-permute-start | bytes 442376 | tf_op jit(solution)/shard_map/ppermute | solution.py:41
  165.5 1.6 collective-permute-start.9
  167.1 2.9 collective-permute-done.8
  170.1 1.5 collective-permute-done.9
  172.4 8.8 %shard_map.112 = (f32[256,1152]{1,0:T(8,128)}, f32[1,256]{1,0:T(1,128)}) custom-call(f32[2]{0:T(128)} %pad_maximum_fusion.scalars, bf16[256,1152]{1,0:T(8,128)(2,1)} %copy-done.8, bf16[2048,1152]{1,0:T(8,128)(2,1)} %constant_dynamic-update-slice_fusion.texts), custom_call_target="tpu_custom_call" | custom-call | flops 2415919104 | bytes 4718592 | tf_op jit(solution)/shard_map/pallas_call | solution.py:214
  181.2 9.5 %shard_map.113 = (f32[256,1152]{1,0:T(8,128)}, bf16[256,1152]{1,0:T(8,128)(2,1)}, f32[1,256]{1,0:T(1,128)}) custom-call(f32[2]{0:T(128)} %pad_maximum_fusion.scalars, bf16[256,1152]{1,0:T(8,128)(2,1)} %copy-done.8, bf16[2048,1152]{1,0:T(8,128)(2,1)} %collective-permute-done.21.texts, f32[256,1152]{1,0:T(8,128)} %get-tuple-element.17.refs_0_), custom_call_target="tpu_custom_call" | custom-call | flops 2415919104 | bytes 4718592 | tf_op jit(solution)/shard_map/pallas_call | solution.py:214
  190.7 1.1 fusion.10
  192.4 3.2 %collective-permute-start.23 = (bf16[64,1152]{1,0:T(8,128)(2,1)S(1)}, bf16[64,1152]{1,0:T(8,128)(2,1)S(1)}, u32[]{:S(2)}, u32[]{:S(2)}) collective-permute-start(bf16[64,1152]{1,0:T(8,128)(2,1)S(1)} %get-tuple-element.34), channel_id=1, source_target_pairs={{0,128},{64,192},{128,0},{192,64},{1,129},{65,193},{129,1},{193,65... | collective-permute-start | bytes 442376 | tf_op jit(solution)/shard_map/ppermute | solution.py:41
  195.6 2.1 collective-permute-start.22
  197.7 1.8 collective-permute-start.32
  200.3 2.7 collective-permute-done.22
  203.0 1.2 multiply_reduce_fusion
  204.2 1.1 divide_convert_fusion
  205.8 1.3 collective-permute-start.25
  207.0 1.5 collective-permute-start.26
  208.6 1.3 collective-permute-done.25
  210.8 1.9 collective-permute-done.26
  212.7 2.5 collective-permute-done.27
  215.3 4.4 %collective-permute-start.29 = (bf16[256,288]{1,0:T(8,128)(2,1)S(1)}, bf16[256,288]{1,0:T(8,128)(2,1)S(1)}, u32[]{:S(2)}, u32[]{:S(2)}) collective-permute-start(bf16[256,288]{1,0:T(8,128)(2,1)S(1)} %constant_dynamic-update-slice_fusion.9.refs_0_), channel_id=1, source_target_pairs={{0,160},{32,128},{64,224},{96,192},{128,32},{160,0},{192,96},{224,... | collective-permute-start | bytes 442376 | tf_op jit(solution)/shard_map/ppermute | solution.py:41
  219.7 11.4 %collective-permute-done.33 = bf16[2,4,64,538]{3,2,1,0:T(8,128)(2,1)S(1)} collective-permute-done((bf16[2,4,64,538]{3,2,1,0:T(8,128)(2,1)}, bf16[2,4,64,538]{3,2,1,0:T(8,128)(2,1)S(1)}, u32[]{:S(2)}, u32[]{:S(2)}) %collective-permute-start.33) | collective-permute-done | bytes 550944 | tf_op jit(solution)/shard_map/ppermute | solution.py:41
  231.2 2.1 collective-permute-done.28.refs_1_
  233.3 2.1 collective-permute-done.29.refs_2_
  235.3 3.6 %collective-permute-done.30.refs_3_ = bf16[256,288]{1,0:T(8,128)(2,1)S(1)} collective-permute-done((bf16[256,288]{1,0:T(8,128)(2,1)S(1)}, bf16[256,288]{1,0:T(8,128)(2,1)S(1)}, u32[]{:S(2)}, u32[]{:S(2)}) %collective-permute-start.30) | collective-permute-done | bytes 147488 | tf_op jit(solution)/shard_map/ppermute | solution.py:41
  239.6 4.2 %shard_map.114 = (f32[288,538]{1,0:T(8,128)}, f32[288,538]{1,0:T(8,128)}) custom-call(bf16[256,288]{1,0:T(8,128)(2,1)} %copy-done.3, bf16[256,288]{1,0:T(8,128)(2,1)} %copy-done.10, bf16[256,288]{1,0:T(8,128)(2,1)} %copy-done.11, bf16[256,288]{1,0:T(8,128)(2,1)} %copy-done.12, bf16[2,256,538]{2,1,0:T(8,128)(2,1)} %get-tuple-element.20.refs_4_, ...), custom_call_target="tpu_custom_call" | custom-call | flops 634650624 | bytes 4000000 | tf_op jit(solution)/shard_map/pallas_call | solution.py:126
  244.0 2.3 collective-permute-done.34
  246.3 1.2 add_convert_fusion
  248.3 4.4 %all-to-all-start.2 = ((bf16[8,36,538]{2,1,0:T(8,128)(2,1)}), bf16[8,36,538]{2,1,0:T(8,128)(2,1)S(1)}, u32[]{:S(2)}, u32[]{:S(2)}) async-start(bf16[8,36,538]{2,1,0:T(8,128)(2,1)} %reshape.85), calls=%async_computation.2 | async-start | bytes 819200 | tf_op jit(solution)/shard_map/all_to_all | solution.py:45
  253.3 14.7 %all-to-all-done.2 = bf16[8,36,538]{2,1,0:T(8,128)(2,1)S(1)} async-done(((bf16[8,36,538]{2,1,0:T(8,128)(2,1)}), bf16[8,36,538]{2,1,0:T(8,128)(2,1)S(1)}, u32[]{:S(2)}, u32[]{:S(2)}) %all-to-all-start.2) | async-done | bytes 309920 | tf_op jit(solution)/shard_map/all_to_all | solution.py:45
  269.0 8.7 %all_to_all.31 = f32[8,1,37]{2,1,0:T(1,128)S(1)} all-to-all(f32[8,1,37]{2,1,0:T(1,128)S(1)} %broadcast_in_dim.31), channel_id=1, replica_groups=mesh['x'=4,'k'=2,'y'=4,'z'=8] {'x','k'}, dimensions={0} | all-to-all | bytes 2368 | tf_op jit(solution)/shard_map/all_to_all | solution.py:45
  279.2 13.8 %all_to_all.32 = f32[32,1,1077]{2,1,0:T(1,128)S(1)} all-to-all(f32[32,1,1077]{2,1,0:T(1,128)S(1)} %broadcast_in_dim.32), channel_id=1, replica_groups=mesh['x'=4,'k'=2,'y'=4,'z'=8] {'y','z'}, dimensions={0} | all-to-all | bytes 275712 | tf_op jit(solution)/shard_map/all_to_all | solution.py:45
  293.8 1.2 broadcast_in_dim_broadcast_in_dim.3
  295.0 4.7 %all-to-all-start.5 = ((f32[8,1,128]{2,1,0:T(1,128)}), f32[8,1,128]{2,1,0:T(1,128)S(1)}, u32[]{:S(2)}, u32[]{:S(2)}) async-start(f32[8,1,128]{2,1,0:T(1,128)} %broadcast_in_dim_broadcast_in_dim.3), calls=%async_computation.5 | async-start | bytes 8192 | tf_op jit(solution)/shard_map/all_to_all | solution.py:45
  300.9 2.6 all-to-all-done.5
  (128 shorter events, 25.6 us)
Async XLA Ops:
  2.7 7.1 %collective-permute-start.10 = (bf16[64,1152]{1,0:T(8,128)(2,1)S(1)}, bf16[64,1152]{1,0:T(8,128)(2,1)S(1)}, u32[]{:S(2)}, u32[]{:S(2)}) collective-permute-start(bf16[64,1152]{1,0:T(8,128)(2,1)S(1)} %fusion.3), channel_id=1, source_target_pairs={{0,40},{8,48},{16,56},{24,32},{32,8},{40,16},{48,24},{56,0},{1,41}... | collective-permute-start | bytes 442376 | tf_op jit(solution)/shard_map/ppermute | solution.py:41
  3.8 10.7 %collective-permute-start.11 = (bf16[64,1152]{1,0:T(8,128)(2,1)S(1)}, bf16[64,1152]{1,0:T(8,128)(2,1)S(1)}, u32[]{:S(2)}, u32[]{:S(2)}) collective-permute-start(bf16[64,1152]{1,0:T(8,128)(2,1)S(1)} %fusion.3), channel_id=1, source_target_pairs={{0,48},{8,56},{16,32},{24,40},{32,16},{40,24},{48,0},{56,8},{1,49}... | collective-permute-start | bytes 442376 | tf_op jit(solution)/shard_map/ppermute | solution.py:41
  7.0 7.6 %collective-permute-start.12 = (bf16[64,1152]{1,0:T(8,128)(2,1)S(1)}, bf16[64,1152]{1,0:T(8,128)(2,1)S(1)}, u32[]{:S(2)}, u32[]{:S(2)}) collective-permute-start(bf16[64,1152]{1,0:T(8,128)(2,1)S(1)} %fusion.3), channel_id=1, source_target_pairs={{0,56},{8,32},{16,40},{24,48},{32,24},{40,0},{48,8},{56,16},{1,57}... | collective-permute-start | bytes 442376 | tf_op jit(solution)/shard_map/ppermute | solution.py:41
  14.6 19.5 %collective-permute-start.13 = (bf16[256,1152]{1,0:T(8,128)(2,1)S(1)}, bf16[256,1152]{1,0:T(8,128)(2,1)S(1)}, u32[]{:S(2)}, u32[]{:S(2)}) collective-permute-start(bf16[256,1152]{1,0:T(8,128)(2,1)S(1)} %constant_dynamic-update-slice_fusion.12), channel_id=1, source_target_pairs={{0,1},{1,2},{2,3},{3,4},{4,5},{5,6},{6,7},{7,0},{8,9},{9,10},{10,1... | collective-permute-start | bytes 1769480 | tf_op jit(solution)/shard_map/ppermute | solution.py:41
  16.6 17.6 %collective-permute-start.14 = (bf16[256,1152]{1,0:T(8,128)(2,1)S(1)}, bf16[256,1152]{1,0:T(8,128)(2,1)S(1)}, u32[]{:S(2)}, u32[]{:S(2)}) collective-permute-start(bf16[256,1152]{1,0:T(8,128)(2,1)S(1)} %constant_dynamic-update-slice_fusion.12), channel_id=1, source_target_pairs={{0,7},{1,0},{2,1},{3,2},{4,3},{5,4},{6,5},{7,6},{8,15},{9,8},{10,9... | collective-permute-start | bytes 1769480 | tf_op jit(solution)/shard_map/ppermute | solution.py:41
  34.1 19.3 %collective-permute-start.15 = (bf16[256,1152]{1,0:T(8,128)(2,1)S(1)}, bf16[256,1152]{1,0:T(8,128)(2,1)S(1)}, u32[]{:S(2)}, u32[]{:S(2)}) collective-permute-start(bf16[256,1152]{1,0:T(8,128)(2,1)S(1)} %collective-permute-done.13), channel_id=1, source_target_pairs={{0,1},{1,2},{2,3},{3,4},{4,5},{5,6},{6,7},{7,0},{8,9},{9,10},{10,1... | collective-permute-start | bytes 1769480 | tf_op jit(solution)/shard_map/ppermute | solution.py:41
  34.1 20.2 %collective-permute-start.16 = (bf16[256,1152]{1,0:T(8,128)(2,1)S(1)}, bf16[256,1152]{1,0:T(8,128)(2,1)S(1)}, u32[]{:S(2)}, u32[]{:S(2)}) collective-permute-start(bf16[256,1152]{1,0:T(8,128)(2,1)S(1)} %collective-permute-done.14), channel_id=1, source_target_pairs={{0,7},{1,0},{2,1},{3,2},{4,3},{5,4},{6,5},{7,6},{8,15},{9,8},{10,9... | collective-permute-start | bytes 1769480 | tf_op jit(solution)/shard_map/ppermute | solution.py:41
  39.0 42.9 %all-to-all-start = ((bf16[8,36,538]{2,1,0:T(8,128)(2,1)}), bf16[8,36,538]{2,1,0:T(8,128)(2,1)S(1)}, u32[]{:S(2)}, u32[]{:S(2)}) async-start(bf16[8,36,538]{2,1,0:T(8,128)(2,1)} %broadcast_in_dim.12), calls=%async_computation | async-start | bytes 819200 | tf_op jit(solution)/shard_map/all_to_all | solution.py:45
  53.5 18.1 %collective-permute-start.17 = (bf16[256,1152]{1,0:T(8,128)(2,1)S(1)}, bf16[256,1152]{1,0:T(8,128)(2,1)S(1)}, u32[]{:S(2)}, u32[]{:S(2)}) collective-permute-start(bf16[256,1152]{1,0:T(8,128)(2,1)S(1)} %collective-permute-done.15), channel_id=1, source_target_pairs={{0,1},{1,2},{2,3},{3,4},{4,5},{5,6},{6,7},{7,0},{8,9},{9,10},{10,1... | collective-permute-start | bytes 1769480 | tf_op jit(solution)/shard_map/ppermute | solution.py:41
  54.3 17.3 %collective-permute-start.18 = (bf16[256,1152]{1,0:T(8,128)(2,1)S(1)}, bf16[256,1152]{1,0:T(8,128)(2,1)S(1)}, u32[]{:S(2)}, u32[]{:S(2)}) collective-permute-start(bf16[256,1152]{1,0:T(8,128)(2,1)S(1)} %collective-permute-done.16), channel_id=1, source_target_pairs={{0,7},{1,0},{2,1},{3,2},{4,3},{5,4},{6,5},{7,6},{8,15},{9,8},{10,9... | collective-permute-start | bytes 1769480 | tf_op jit(solution)/shard_map/ppermute | solution.py:41
  71.6 8.9 %collective-permute-start.19 = (bf16[128,1152]{1,0:T(8,128)(2,1)S(1)}, bf16[128,1152]{1,0:T(8,128)(2,1)S(1)}, u32[]{:S(2)}, u32[]{:S(2)}) collective-permute-start(bf16[128,1152]{1,0:T(8,128)(2,1)S(1)} %slice.64), channel_id=1, source_target_pairs={{0,1},{1,2},{2,3},{3,4},{4,5},{5,6},{6,7},{7,0},{8,9},{9,10},{10,1... | collective-permute-start | bytes 884744 | tf_op jit(solution)/shard_map/ppermute | solution.py:41
  71.7 31.6 %copy-start.9 = (bf16[64,4304]{1,0:T(8,128)(2,1)S(1)}, bf16[64,4304]{1,0:T(8,128)(2,1)}, u32[]{:S(2)}) copy-start(bf16[64,4304]{1,0:T(8,128)(2,1)} %param.9) | copy-start | bytes 1652740
  71.7 9.5 %collective-permute-start.20 = (bf16[128,1152]{1,0:T(8,128)(2,1)S(1)}, bf16[128,1152]{1,0:T(8,128)(2,1)S(1)}, u32[]{:S(2)}, u32[]{:S(2)}) collective-permute-start(bf16[128,1152]{1,0:T(8,128)(2,1)S(1)} %slice.65), channel_id=1, source_target_pairs={{0,7},{1,0},{2,1},{3,2},{4,3},{5,4},{6,5},{7,6},{8,15},{9,8},{10,9... | collective-permute-start | bytes 884744 | tf_op jit(solution)/shard_map/ppermute | solution.py:41
  81.9 99.2 %collective-permute-start.21 = (bf16[2048,1152]{1,0:T(8,128)(2,1)}, bf16[2048,1152]{1,0:T(8,128)(2,1)}, u32[]{:S(2)}, u32[]{:S(2)}) collective-permute-start(bf16[2048,1152]{1,0:T(8,128)(2,1)} %constant_dynamic-update-slice_fusion.texts), channel_id=1, source_target_pairs={{0,32},{32,0},{1,33},{33,1},{2,34},{34,2},{3,35},{35,3},{4,36},{36... | collective-permute-start | bytes 14155784 | tf_op jit(solution)/shard_map/ppermute | solution.py:41
  82.1 11.2 %collective-permute-start.3 = (bf16[288,538]{1,0:T(8,128)(2,1)S(1)}, bf16[288,538]{1,0:T(8,128)(2,1)}, u32[]{:S(2)}, u32[]{:S(2)}) collective-permute-start(bf16[288,538]{1,0:T(8,128)(2,1)S(1)} %reshape.75), channel_id=1, source_target_pairs={{0,192},{64,0},{128,64},{192,128},{1,193},{65,1},{129,65},{193,129... | collective-permute-start | bytes 929672 | tf_op jit(solution)/shard_map/ppermute | solution.py:41
  82.7 19.4 %collective-permute-start.4 = (bf16[288,538]{1,0:T(8,128)(2,1)S(1)}, bf16[288,538]{1,0:T(8,128)(2,1)}, u32[]{:S(2)}, u32[]{:S(2)}) collective-permute-start(bf16[288,538]{1,0:T(8,128)(2,1)S(1)} %reshape.75), channel_id=1, source_target_pairs={{0,128},{64,192},{128,0},{192,64},{1,129},{65,193},{129,1},{193,65... | collective-permute-start | bytes 929672 | tf_op jit(solution)/shard_map/ppermute | solution.py:41
  85.1 18.0 %collective-permute-start.5 = (bf16[288,538]{1,0:T(8,128)(2,1)S(1)}, bf16[288,538]{1,0:T(8,128)(2,1)S(1)}, u32[]{:S(2)}, u32[]{:S(2)}) collective-permute-start(bf16[288,538]{1,0:T(8,128)(2,1)S(1)} %reshape.75), channel_id=1, source_target_pairs={{0,64},{64,128},{128,192},{192,0},{1,65},{65,129},{129,193},{193,1... | collective-permute-start | bytes 929672 | tf_op jit(solution)/shard_map/ppermute | solution.py:41
  103.2 36.2 %copy-start = (bf16[4,288,538]{2,1,0:T(8,128)(2,1)}, bf16[4,288,538]{2,1,0:T(8,128)(2,1)S(1)}, u32[]{:S(2)}) copy-start(bf16[4,288,538]{2,1,0:T(8,128)(2,1)S(1)} %bitcast_dynamic-update-slice_fusion.own) | copy-start | bytes 3718660
  103.2 36.2 %collective-permute-start.6 = (bf16[4,288,538]{2,1,0:T(8,128)(2,1)S(1)}, bf16[4,288,538]{2,1,0:T(8,128)(2,1)}, u32[]{:S(2)}, u32[]{:S(2)}) collective-permute-start(bf16[4,288,538]{2,1,0:T(8,128)(2,1)S(1)} %bitcast_dynamic-update-slice_fusion.own), channel_id=1, source_target_pairs={{0,32},{32,0},{1,33},{33,1},{2,34},{34,2},{3,35},{35,3},{4,36},{36... | collective-permute-start | bytes 3718664 | tf_op jit(solution)/shard_map/ppermute | solution.py:41
  104.3 54.3 %copy-start.2 = (bf16[64,1152]{1,0:T(8,128)(2,1)S(1)}, bf16[64,1152]{1,0:T(8,128)(2,1)}, u32[]{:S(2)}) copy-start(bf16[64,1152]{1,0:T(8,128)(2,1)} %param.8) | copy-start | bytes 442372
  104.6 34.7 %copy-start.1 = (bf16[4,2,64,538]{3,2,1,0:T(8,128)(2,1)}, bf16[4,2,64,538]{3,2,1,0:T(8,128)(2,1)S(1)}, u32[]{:S(2)}) copy-start(bf16[4,2,64,538]{3,2,1,0:T(8,128)(2,1)S(1)} %fusion.h0) | copy-start | bytes 1652740
  104.6 30.9 %collective-permute-start = (bf16[4,2,64,538]{3,2,1,0:T(8,128)(2,1)S(1)}, bf16[4,2,64,538]{3,2,1,0:T(8,128)(2,1)S(1)}, u32[]{:S(2)}, u32[]{:S(2)}) collective-permute-start(bf16[4,2,64,538]{3,2,1,0:T(8,128)(2,1)S(1)} %fusion.h0), channel_id=1, source_target_pairs={{0,24},{8,0},{16,8},{24,16},{1,25},{9,1},{17,9},{25,17},{2,26},{10... | collective-permute-start | bytes 1652744 | tf_op jit(solution)/shard_map/ppermute | solution.py:41
  106.8 28.7 %collective-permute-start.1 = (bf16[4,2,64,538]{3,2,1,0:T(8,128)(2,1)S(1)}, bf16[4,2,64,538]{3,2,1,0:T(8,128)(2,1)}, u32[]{:S(2)}, u32[]{:S(2)}) collective-permute-start(bf16[4,2,64,538]{3,2,1,0:T(8,128)(2,1)S(1)} %fusion.h0), channel_id=1, source_target_pairs={{0,16},{8,24},{16,0},{24,8},{1,17},{9,25},{17,1},{25,9},{2,18},{10... | collective-permute-start | bytes 1652744 | tf_op jit(solution)/shard_map/ppermute | solution.py:41
  108.0 31.3 %collective-permute-start.2 = (bf16[4,2,64,538]{3,2,1,0:T(8,128)(2,1)S(1)}, bf16[4,2,64,538]{3,2,1,0:T(8,128)(2,1)}, u32[]{:S(2)}, u32[]{:S(2)}) collective-permute-start(bf16[4,2,64,538]{3,2,1,0:T(8,128)(2,1)S(1)} %fusion.h0), channel_id=1, source_target_pairs={{0,8},{8,16},{16,24},{24,0},{1,9},{9,17},{17,25},{25,1},{2,10},{10... | collective-permute-start | bytes 1652744 | tf_op jit(solution)/shard_map/ppermute | solution.py:41
  135.6 3.8 %copy-start.7 = (bf16[4,2,64,538]{3,2,1,0:T(8,128)(2,1)}, bf16[4,2,64,538]{3,2,1,0:T(8,128)(2,1)S(1)}, u32[]{:S(2)}) copy-start(bf16[4,2,64,538]{3,2,1,0:T(8,128)(2,1)S(1)} %collective-permute-done.h1) | copy-start | bytes 1652740
  158.8 8.3 %collective-permute-start.7 = (bf16[64,1152]{1,0:T(8,128)(2,1)S(1)}, bf16[64,1152]{1,0:T(8,128)(2,1)S(1)}, u32[]{:S(2)}, u32[]{:S(2)}) collective-permute-start(bf16[64,1152]{1,0:T(8,128)(2,1)S(1)} %fusion.8), channel_id=1, source_target_pairs={{0,64},{64,128},{128,192},{192,0},{1,65},{65,129},{129,193},{193,1... | collective-permute-start | bytes 442376 | tf_op jit(solution)/shard_map/ppermute | solution.py:41
  162.1 8.0 %collective-permute-start.8 = (bf16[64,1152]{1,0:T(8,128)(2,1)S(1)}, bf16[64,1152]{1,0:T(8,128)(2,1)S(1)}, u32[]{:S(2)}, u32[]{:S(2)}) collective-permute-start(bf16[64,1152]{1,0:T(8,128)(2,1)S(1)} %fusion.8), channel_id=1, source_target_pairs={{0,128},{64,192},{128,0},{192,64},{1,129},{65,193},{129,1},{193,65... | collective-permute-start | bytes 442376 | tf_op jit(solution)/shard_map/ppermute | solution.py:41
  165.5 6.0 %collective-permute-start.9 = (bf16[64,1152]{1,0:T(8,128)(2,1)S(1)}, bf16[64,1152]{1,0:T(8,128)(2,1)S(1)}, u32[]{:S(2)}, u32[]{:S(2)}) collective-permute-start(bf16[64,1152]{1,0:T(8,128)(2,1)S(1)} %fusion.8), channel_id=1, source_target_pairs={{0,192},{64,0},{128,64},{192,128},{1,193},{65,1},{129,65},{193,129... | collective-permute-start | bytes 442376 | tf_op jit(solution)/shard_map/ppermute | solution.py:41
  171.6 0.8 copy-start.8
  191.8 7.8 %collective-permute-start.24 = (bf16[64,1152]{1,0:T(8,128)(2,1)S(1)}, bf16[64,1152]{1,0:T(8,128)(2,1)S(1)}, u32[]{:S(2)}, u32[]{:S(2)}) collective-permute-start(bf16[64,1152]{1,0:T(8,128)(2,1)S(1)} %get-tuple-element.33), channel_id=1, source_target_pairs={{0,64},{64,128},{128,192},{192,0},{1,65},{65,129},{129,193},{193,1... | collective-permute-start | bytes 442376 | tf_op jit(solution)/shard_map/ppermute | solution.py:41
  192.4 7.9 %collective-permute-start.23 = (bf16[64,1152]{1,0:T(8,128)(2,1)S(1)}, bf16[64,1152]{1,0:T(8,128)(2,1)S(1)}, u32[]{:S(2)}, u32[]{:S(2)}) collective-permute-start(bf16[64,1152]{1,0:T(8,128)(2,1)S(1)} %get-tuple-element.34), channel_id=1, source_target_pairs={{0,128},{64,192},{128,0},{192,64},{1,129},{65,193},{129,1},{193,65... | collective-permute-start | bytes 442376 | tf_op jit(solution)/shard_map/ppermute | solution.py:41
  195.6 7.4 %collective-permute-start.22 = (bf16[64,1152]{1,0:T(8,128)(2,1)S(1)}, bf16[64,1152]{1,0:T(8,128)(2,1)S(1)}, u32[]{:S(2)}, u32[]{:S(2)}) collective-permute-start(bf16[64,1152]{1,0:T(8,128)(2,1)S(1)} %get-tuple-element.32), channel_id=1, source_target_pairs={{0,192},{64,0},{128,64},{192,128},{1,193},{65,1},{129,65},{193,129... | collective-permute-start | bytes 442376 | tf_op jit(solution)/shard_map/ppermute | solution.py:41
  197.7 22.0 %collective-permute-start.31 = (bf16[2,4,64,538]{3,2,1,0:T(8,128)(2,1)}, bf16[2,4,64,538]{3,2,1,0:T(8,128)(2,1)S(1)}, u32[]{:S(2)}, u32[]{:S(2)}) collective-permute-start(bf16[2,4,64,538]{3,2,1,0:T(8,128)(2,1)} %bitcast.15), channel_id=1, source_target_pairs={{0,96},{32,64},{64,160},{96,128},{128,224},{160,192},{192,32},{224... | collective-permute-start | bytes 1652744 | tf_op jit(solution)/shard_map/ppermute | solution.py:41
  197.7 22.0 %collective-permute-start.32 = (bf16[2,4,64,538]{3,2,1,0:T(8,128)(2,1)}, bf16[2,4,64,538]{3,2,1,0:T(8,128)(2,1)S(1)}, u32[]{:S(2)}, u32[]{:S(2)}) collective-permute-start(bf16[2,4,64,538]{3,2,1,0:T(8,128)(2,1)} %bitcast.48), channel_id=1, source_target_pairs={{0,160},{32,128},{64,224},{96,192},{128,32},{160,0},{192,96},{224,... | collective-permute-start | bytes 1652744 | tf_op jit(solution)/shard_map/ppermute | solution.py:41
  199.5 31.7 %collective-permute-start.33 = (bf16[2,4,64,538]{3,2,1,0:T(8,128)(2,1)}, bf16[2,4,64,538]{3,2,1,0:T(8,128)(2,1)S(1)}, u32[]{:S(2)}, u32[]{:S(2)}) collective-permute-start(bf16[2,4,64,538]{3,2,1,0:T(8,128)(2,1)} %bitcast.47), channel_id=1, source_target_pairs={{0,224},{32,192},{64,32},{96,0},{128,96},{160,64},{192,160},{224,1... | collective-permute-start | bytes 1652744 | tf_op jit(solution)/shard_map/ppermute | solution.py:41
  205.3 47.4 %copy-start.16 = (f32[1,256]{1,0:T(1,128)S(1)}, f32[1,256]{1,0:T(1,128)}, u32[]{:S(2)}) copy-start(f32[1,256]{1,0:T(1,128)} %get-tuple-element.26) | copy-start | bytes 3076
  205.3 47.4 %copy-start.17 = (f32[1,256]{1,0:T(1,128)S(1)}, f32[1,256]{1,0:T(1,128)}, u32[]{:S(2)}) copy-start(f32[1,256]{1,0:T(1,128)} %get-tuple-element.27) | copy-start | bytes 3076
  205.3 72.9 %copy-start.18 = (f32[36]{0:T(128)S(1)}, f32[36]{0:T(128)}, u32[]{:S(2)}) copy-start(f32[36]{0:T(128)} %param.12) | copy-start | bytes 436
  205.6 87.5 %copy-start.14 = (f32[538]{0:T(1024)S(1)}, f32[538]{0:T(1024)}, u32[]{:S(2)}) copy-start(f32[538]{0:T(1024)} %param.13) | copy-start | bytes 6460
  205.8 4.2 %collective-permute-start.25 = (bf16[64,288]{1,0:T(8,128)(2,1)S(1)}, bf16[64,288]{1,0:T(8,128)(2,1)S(1)}, u32[]{:S(2)}, u32[]{:S(2)}) collective-permute-start(bf16[64,288]{1,0:T(8,128)(2,1)S(1)} %get-tuple-element.37), channel_id=1, source_target_pairs={{0,24},{8,0},{16,8},{24,16},{1,25},{9,1},{17,9},{25,17},{2,26},{10... | collective-permute-start | bytes 110600 | tf_op jit(solution)/shard_map/ppermute | solution.py:41
  207.0 5.7 %collective-permute-start.26 = (bf16[64,288]{1,0:T(8,128)(2,1)S(1)}, bf16[64,288]{1,0:T(8,128)(2,1)S(1)}, u32[]{:S(2)}, u32[]{:S(2)}) collective-permute-start(bf16[64,288]{1,0:T(8,128)(2,1)S(1)} %get-tuple-element.36), channel_id=1, source_target_pairs={{0,16},{8,24},{16,0},{24,8},{1,17},{9,25},{17,1},{25,9},{2,18},{10... | collective-permute-start | bytes 110600 | tf_op jit(solution)/shard_map/ppermute | solution.py:41
  209.9 5.3 %collective-permute-start.27 = (bf16[64,288]{1,0:T(8,128)(2,1)S(1)}, bf16[64,288]{1,0:T(8,128)(2,1)S(1)}, u32[]{:S(2)}, u32[]{:S(2)}) collective-permute-start(bf16[64,288]{1,0:T(8,128)(2,1)S(1)} %get-tuple-element.35), channel_id=1, source_target_pairs={{0,8},{8,16},{16,24},{24,0},{1,9},{9,17},{17,25},{25,1},{2,10},{10... | collective-permute-start | bytes 110600 | tf_op jit(solution)/shard_map/ppermute | solution.py:41
  215.2 23.7 %copy-start.3 = (bf16[256,288]{1,0:T(8,128)(2,1)}, bf16[256,288]{1,0:T(8,128)(2,1)S(1)}, u32[]{:S(2)}) copy-start(bf16[256,288]{1,0:T(8,128)(2,1)S(1)} %constant_dynamic-update-slice_fusion.9.refs_0_) | copy-start | bytes 442372
  215.3 18.0 %collective-permute-start.28 = (bf16[256,288]{1,0:T(8,128)(2,1)S(1)}, bf16[256,288]{1,0:T(8,128)(2,1)S(1)}, u32[]{:S(2)}, u32[]{:S(2)}) collective-permute-start(bf16[256,288]{1,0:T(8,128)(2,1)S(1)} %constant_dynamic-update-slice_fusion.9.refs_0_), channel_id=1, source_target_pairs={{0,96},{32,64},{64,160},{96,128},{128,224},{160,192},{192,32},{224... | collective-permute-start | bytes 442376 | tf_op jit(solution)/shard_map/ppermute | solution.py:41
  215.3 20.0 %collective-permute-start.29 = (bf16[256,288]{1,0:T(8,128)(2,1)S(1)}, bf16[256,288]{1,0:T(8,128)(2,1)S(1)}, u32[]{:S(2)}, u32[]{:S(2)}) collective-permute-start(bf16[256,288]{1,0:T(8,128)(2,1)S(1)} %constant_dynamic-update-slice_fusion.9.refs_0_), channel_id=1, source_target_pairs={{0,160},{32,128},{64,224},{96,192},{128,32},{160,0},{192,96},{224,... | collective-permute-start | bytes 442376 | tf_op jit(solution)/shard_map/ppermute | solution.py:41
  219.7 19.2 %copy-start.4 = (bf16[2,4,64,538]{3,2,1,0:T(8,128)(2,1)}, bf16[2,4,64,538]{3,2,1,0:T(8,128)(2,1)S(1)}, u32[]{:S(2)}) copy-start(bf16[2,4,64,538]{3,2,1,0:T(8,128)(2,1)S(1)} %collective-permute-done.31) | copy-start | bytes 1652740
  219.7 19.2 %collective-permute-start.30 = (bf16[256,288]{1,0:T(8,128)(2,1)S(1)}, bf16[256,288]{1,0:T(8,128)(2,1)S(1)}, u32[]{:S(2)}, u32[]{:S(2)}) collective-permute-start(bf16[256,288]{1,0:T(8,128)(2,1)S(1)} %constant_dynamic-update-slice_fusion.9.refs_0_), channel_id=1, source_target_pairs={{0,224},{32,192},{64,32},{96,0},{128,96},{160,64},{192,160},{224,1... | collective-permute-start | bytes 442376 | tf_op jit(solution)/shard_map/ppermute | solution.py:41
  219.7 19.2 %copy-start.5 = (bf16[2,4,64,538]{3,2,1,0:T(8,128)(2,1)}, bf16[2,4,64,538]{3,2,1,0:T(8,128)(2,1)S(1)}, u32[]{:S(2)}) copy-start(bf16[2,4,64,538]{3,2,1,0:T(8,128)(2,1)S(1)} %collective-permute-done.32) | copy-start | bytes 1652740
  231.2 7.8 %copy-start.6 = (bf16[2,4,64,538]{3,2,1,0:T(8,128)(2,1)}, bf16[2,4,64,538]{3,2,1,0:T(8,128)(2,1)S(1)}, u32[]{:S(2)}) copy-start(bf16[2,4,64,538]{3,2,1,0:T(8,128)(2,1)S(1)} %collective-permute-done.33) | copy-start | bytes 1652740
  233.3 5.7 %copy-start.10 = (bf16[256,288]{1,0:T(8,128)(2,1)}, bf16[256,288]{1,0:T(8,128)(2,1)S(1)}, u32[]{:S(2)}) copy-start(bf16[256,288]{1,0:T(8,128)(2,1)S(1)} %collective-permute-done.28.refs_1_) | copy-start | bytes 442372
  235.3 3.6 %copy-start.11 = (bf16[256,288]{1,0:T(8,128)(2,1)}, bf16[256,288]{1,0:T(8,128)(2,1)S(1)}, u32[]{:S(2)}) copy-start(bf16[256,288]{1,0:T(8,128)(2,1)S(1)} %collective-permute-done.29.refs_2_) | copy-start | bytes 442372
  238.9 0.7 copy-start.12
  243.9 2.4 collective-permute-start.34
  248.3 19.7 %all-to-all-start.2 = ((bf16[8,36,538]{2,1,0:T(8,128)(2,1)}), bf16[8,36,538]{2,1,0:T(8,128)(2,1)S(1)}, u32[]{:S(2)}, u32[]{:S(2)}) async-start(bf16[8,36,538]{2,1,0:T(8,128)(2,1)} %reshape.85), calls=%async_computation.2 | async-start | bytes 819200 | tf_op jit(solution)/shard_map/all_to_all | solution.py:45
  278.3 26.0 %copy-start.15 = (f32[36]{0:T(128)}, f32[36]{0:T(128)S(1)}, u32[]{:S(2)}) copy-start(f32[36]{0:T(128)S(1)} %multiply_add_fusion) | copy-start | bytes 436
  293.8 10.6 %copy-start.13 = (f32[538]{0:T(1024)}, f32[538]{0:T(1024)S(1)}, u32[]{:S(2)}) copy-start(f32[538]{0:T(1024)S(1)} %get-tuple-element.31) | copy-start | bytes 6460
  295.0 8.5 %all-to-all-start.5 = ((f32[8,1,128]{2,1,0:T(1,128)}), f32[8,1,128]{2,1,0:T(1,128)S(1)}, u32[]{:S(2)}, u32[]{:S(2)}) async-start(f32[8,1,128]{2,1,0:T(1,128)} %broadcast_in_dim_broadcast_in_dim.3), calls=%async_computation.5 | async-start | bytes 8192 | tf_op jit(solution)/shard_map/all_to_all | solution.py:45

commit v3 on v2

--- a/solution.py
+++ b/solution.py
@@ -49,93 +49,12 @@
     return exchange(jnp.broadcast_to(array, (lax.axis_size(axes), *array.shape)), axes)
 
 
-def rolled(pieces, by, count):
-    twice = jnp.concatenate([pieces, pieces])
-    return lax.dynamic_slice_in_dim(twice, by & (count - 1), count, 0)
+def after(values, *others):
+    return lax.optimization_barrier((values, others))[0]
 
 
 def ring_step(up, down, axis):
     return shift(up, **{axis: 1}), shift(down, **{axis: -1})
-
-
-def project_kernel(h0, h1, h2, h3, own, other, part, *hid):
-    at = pl.program_id(0)
-    total = None
-    for kk in range(2):
-        rows = jnp.concatenate([h[0, kk] for h in (h0, h1, h2, h3)], axis=0)
-        for s in range(4):
-
-            @pl.when(at == s)
-            def _(s=s, rows=rows):
-                hid[s][kk] = rows
-
-        piece = lax.dot_general(
-            rows, (own, other)[kk][0], (((1,), (1,)), ((), ())), preferred_element_type=F32
-        )
-        total = piece if total is None else total + piece
-
-    @pl.when(at == 0)
-    def _():
-        part[...] = total
-
-    @pl.when(at > 0)
-    def _():
-        part[...] += total
-
-
-def project(hid_y, own, other):
-    count, _, tokens, units = hid_y[0].shape
-    features = own.shape[1]
-    weights = pl.BlockSpec((1, features, units), lambda i: (i, 0, 0))
-    rows = (2, 4 * tokens, units)
-    return pl.pallas_call(
-        project_kernel,
-        grid=(count,),
-        in_specs=[pl.BlockSpec((1, 2, tokens, units), lambda i: (i, 0, 0, 0))] * 4
-        + [weights] * 2,
-        out_specs=[pl.BlockSpec((4 * tokens, features), lambda i: (0, 0))]
-        + [pl.BlockSpec(rows, lambda i: (0, 0, 0))] * 4,
-        out_shape=[jax.ShapeDtypeStruct((4 * tokens, features), F32)]
-        + [jax.ShapeDtypeStruct(rows, BF16)] * 4,
-        cost_estimate=pl.CostEstimate(
-            flops=2 * count * 2 * 4 * tokens * units * features,
-            bytes_accessed=8000000,
-            transcendentals=0,
-        ),
-        compiler_params=pltpu.CompilerParams(dimension_semantics=("arbitrary",)),
-    )(*hid_y, own, other)
-
-
-def gradient_kernel(*refs):
-    grads, hid, outs = refs[:4], refs[4:8], refs[8:]
-    total = None
-    for s in range(4):
-        piece = jnp.dot(grads[s][...].T, hid[s][0], preferred_element_type=F32)
-        total = piece if total is None else total + piece
-    for kk in range(2):
-
-        @pl.when(pl.program_id(0) == kk)
-        def _(kk=kk):
-            outs[kk][...] = total
-
-
-def gradients(grads, hid):
-    tokens, features = grads[0].shape
-    units = hid[0].shape[2]
-    whole = pl.BlockSpec((features, units), lambda i: (0, 0))
-    return pl.pallas_call(
-        gradient_kernel,
-        grid=(2,),
-        in_specs=[pl.BlockSpec((tokens, features), lambda i: (0, 0))] * 4
-        + [pl.BlockSpec((1, tokens, units), lambda i: (i, 0, 0))]
-        + [pl.BlockSpec((1, tokens, units), lambda i: (1 - i, 0, 0))] * 3,
-        out_specs=[whole] * 2,
-        out_shape=[jax.ShapeDtypeStruct((features, units), F32)] * 2,
-        cost_estimate=pl.CostEstimate(
-            flops=16 * grads[0].size * units, bytes_accessed=4000000, transcendentals=0
-        ),
-        compiler_params=pltpu.CompilerParams(dimension_semantics=("arbitrary",)),
-    )(*grads, *hid)
 
 
 def joined(pieces):
@@ -205,7 +124,7 @@
 def pair_tiles(scalars, images, texts, before, tokens, batch_total):
     first = before is None
     count, width = images.shape
-    block = 256
+    block = 512
     outs = [jax.ShapeDtypeStruct((count, width), F32)]
     if not first:
         outs.append(jax.ShapeDtypeStruct((count, width), BF16))
@@ -231,54 +150,70 @@
     slice_ff = weight.shape[1]
     k_place = lax.axis_index("k")
 
+    first_core = k_place == 0
     quarter = D // 4
     x_place = lax.axis_index("x")
-    y_place = lax.axis_index("y")
-    half_ff = slice_ff
+    hidden_by_x = jnp.moveaxis(hidden.reshape(tokens, 4, 2 * slice_ff), 1, 0)
+    hidden_x = jnp.zeros((4, tokens, 2 * slice_ff), BF16)
+    for s in range(4):
+        piece = lax.dynamic_index_in_dim(hidden_by_x, (x_place + s) & 3, 0, keepdims=True)
+        if s > 0:
+            piece = shift(piece, x=s)
+        hidden_x = lax.dynamic_update_index_in_dim(hidden_x, piece, (x_place - s) & 3, 0)
+    hidden_x = hidden_x.reshape(4 * tokens, 2 * slice_ff)
+    hid_y = [hidden_x] + [shift(hidden_x, y=-s) for s in (1, 2, 3)]
 
     text_float = text.astype(F32)
     text_units = (
         text_float / jnp.sqrt(jnp.sum(text_float * text_float, axis=1, keepdims=True) + EPSILON)
     ).astype(BF16)
     texts_y = joined([text_units] + [shift(text_units, k=1, y=s) for s in (1, 2, 3)])
-
-    by_slice = jnp.moveaxis(hidden.reshape(tokens, 8, half_ff), 1, 0).reshape(
-        4, 2, tokens, half_ff
-    )
-    by_slice = jnp.where(k_place == 0, by_slice, by_slice[:, ::-1])
-    hid_mine = rolled(by_slice, x_place, 4)
-    hid_y = [hid_mine] + [shift(hid_mine, y=-s) for s in (1, 2, 3)]
-
     up, down = ring_step(texts_y, texts_y, "z")
     ring_pieces = [texts_y, up, down]
     up, down = ring_step(up, down, "z")
     ring_pieces += [up, down]
-    up, down = ring_step(up, down, "z")
+
+    weight_own = everywhere(weight.astype(BF16), "z").reshape(quarter, slice_ff)
+    weight_other = shift(weight_own, k=1)
+    weight_x = jnp.concatenate(
+        [
+            jnp.where(first_core, weight_own, weight_other),
+            jnp.where(first_core, weight_other, weight_own),
+        ],
+        axis=1,
+    )
+    partial = jnp.stack(
+        [
+            lax.dot_general(
+                piece, weight_x, (((1,), (1,)), ((), ())), preferred_element_type=F32
+            )
+            .astype(BF16)
+            .reshape(4, tokens, quarter)
+            for piece in hid_y
+        ]
+    )
+    y_place = lax.axis_index("y")
+    partial = jnp.stack(
+        [
+            lax.dynamic_index_in_dim(partial, (c - y_place) & 3, 0, keepdims=False)
+            for c in range(4)
+        ],
+        axis=1,
+    )
+    up, down = ring_step(*after((up, down), partial), "z")
     ring_pieces += [up, down]
+    arrived = exchange(partial.reshape(16, tokens, quarter), ("x", "y"))
     half = texts_y.shape[0] // 2
+    up, down = after((up, down), arrived)
     ring_pieces += ring_step(up[:half], down[half:], "z")
-
-    weight_z = everywhere(weight.astype(BF16), "z").reshape(quarter, half_ff)
-    weight_own = [weight_z] + [shift(weight_z, x=-s) for s in (1, 2, 3)]
-    weight_own = joined([w[None] for w in weight_own])
-    weight_other = shift(weight_own, k=1)
-    mixed_part, *hid_all = project(hid_y, weight_own, weight_other)
-    mixed_part = mixed_part.reshape(4, tokens, quarter)
-
-    by_y = (2, 4, tokens, half_ff)
-    hid_x = [hid_all[0]] + [
-        shift(hid_all[s].reshape(by_y), x=s, k=1).reshape(hid_all[s].shape)
-        for s in (1, 2, 3)
-    ]
-    arrived = exchange(rolled(mixed_part, -y_place, 4), "y")
-    mixed = pooled.astype(F32) + jnp.moveaxis(arrived, 0, 1).reshape(tokens, D)
+    projected = jnp.sum(arrived.astype(F32).reshape(4, 4, tokens, quarter), axis=0)
+    mixed = pooled.astype(F32) + jnp.moveaxis(projected, 0, 1).reshape(tokens, D)
     length = jnp.sqrt(jnp.sum(mixed * mixed, axis=1, keepdims=True) + EPSILON)
     unit = mixed / length
     images = unit.astype(BF16)
-
     logit_scale = jnp.exp(log_scale)
     image_rows = joined([images] + [shift(images, x=s) for s in (1, 2, 3)])
-    texts_own = jnp.concatenate(ring_pieces)
+    texts_own = jnp.concatenate(ring_pieces[:-2] + after(ring_pieces[-2:], image_rows))
     texts_other = shift(texts_own, k=1)
     scalars = jnp.stack([logit_scale, bias])
     part_a, loss_a = pair_tiles(scalars, image_rows, texts_own, None, tokens, batch_total)
@@ -293,12 +228,19 @@
     ).astype(BF16)
 
     quarters = jnp.moveaxis(mixed_grad.reshape(tokens, 4, quarter), 1, 0)
-    quarters = rolled(quarters, y_place, 4)
-    grad_y = [quarters[0]] + [shift(quarters[s], y=s) for s in (1, 2, 3)]
-    grad_mine = joined([grad_y[-s] for s in range(4)])
-    grad_x = [grad_mine] + [shift(grad_mine, x=s, k=1) for s in (1, 2, 3)]
-    both = gradients(grad_x, hid_x)
-    chip_grad = both[0] + shift(both[1], k=1)
+    grad_rows = exchange(
+        jnp.broadcast_to(quarters[None], (4, 4, tokens, quarter)).reshape(16, tokens, quarter),
+        ("x", "y"),
+    ).reshape(4, 4, tokens, quarter)
+    grad_by_y = jnp.moveaxis(grad_rows, 1, 0).reshape(4, 4 * tokens, quarter)
+    both = F32(0.0)
+    for s in range(4):
+        part = lax.dynamic_index_in_dim(grad_by_y, (y_place + s) & 3, 0, keepdims=False)
+        both = both + lax.dot_general(
+            part, hid_y[s], (((0,), (0,)), ((), ())), preferred_element_type=F32
+        )
+    low, high = both[:, :slice_ff], both[:, slice_ff:]
+    chip_grad = jnp.where(first_core, low, high) + shift(jnp.where(first_core, high, low), k=1)
     arrived_grad = exchange(chip_grad.astype(BF16).reshape(8, D // 32, slice_ff), "z")
     gradient = jnp.sum(arrived_grad.astype(F32), axis=0)
 

time: 308 us -> 241 us (0.78)
  waiting for transfers between devices: 139 us -> 79.9 us
  Pallas kernels: 29.2 us -> 18.1 us
  matrix products: 0 us -> 11 us
  blocking collectives: 33.4 us -> 22.6 us
  local copies, waits for them, and re-layouts: 19.5 us -> 23.8 us
    ppermute x35 -> x26, waiting for transfers between devices: 121 us -> 37.1 us  [shift(): return lax.ppermute(value, names, pairs)]
    all_to_all x3 -> x5, waiting for transfers between devices: 17.3 us -> 42.9 us  [exchange(): return lax.all_to_all(pieces, axes, split_axis=0, concat_axis=0, tiled=True)]
    ppermute x35 -> x26, starting transfers between devices: 53.6 us -> 36.6 us  [shift(): return lax.ppermute(value, names, pairs)]
    all_to_all x3 -> x5, starting transfers between devices: 14.6 us -> 30.1 us  [exchange(): return lax.all_to_all(pieces, axes, split_axis=0, concat_axis=0, tiled=True)]
    dot_general x0 -> x8, matrix products: none -> 11 us  [the longest x4 5.96 us: step(): lax.dot_general(piece, weight_x, (((1,), (1,)), ((), ())), preferred_elem...]
    pallas_call x2 -> x0, Pallas kernels: 11 us -> none  [the longest x1 6.71 us: project(): pl.pallas_call(project_kernel, grid=(count,), in_specs=[pl.BlockSpec((1,...]
    all_to_all x3 -> x2, blocking collectives: 33.4 us -> 22.6 us  [exchange(): return lax.all_to_all(pieces, axes, split_axis=0, concat_axis=0, tiled=True)]
    unnamed x46 -> x37, local copies, waits for them, and re-layouts: 8.47 us -> 9.39 us
  transfers between devices with their start and end apart: 38 -> 31, of which waited for: 25 -> 15; matrix products, arithmetic and copies ran while one was open for 6% -> 11% of each run, Pallas kernels for 5% -> 4%
where the time goes in v3:
time: 241 us; the launch traced here: 238 us
  waiting for transfers between devices  79.9 us (33%)
  starting transfers between devices  66.6 us (28%)
  local copies, waits for them, and re-layouts  23.8 us (10%)
  blocking collectives  22.6 us (9%)
  Pallas kernels  18.1 us (8%)
  other arithmetic  11.4 us (5%)
  matrix products  11 us (5%)
  between operations  4.38 us (2%)
    all_to_all x5, waiting for transfers between devices, exchange(): return lax.all_to_all(pieces, axes, split_axis=0, concat_axis=0, tiled=True)  42.9 us
    ppermute x26, waiting for transfers between devices, shift(): return lax.ppermute(value, names, pairs)  37.1 us
    ppermute x26, starting transfers between devices, shift(): return lax.ppermute(value, names, pairs)  36.6 us
    all_to_all x5, starting transfers between devices, exchange(): return lax.all_to_all(pieces, axes, split_axis=0, concat_axis=0, tiled=True)  30.1 us
    all_to_all x2, blocking collectives, exchange(): return lax.all_to_all(pieces, axes, split_axis=0, concat_axis=0, tiled=True)  22.6 us
    pallas_call x2, Pallas kernels, pair_tiles(): pl.pallas_call(functools.partial(pair_kernel, first=first, tokens=tokens,...  18.1 us
    unnamed x37, local copies, waits for them, and re-layouts  9.39 us
    dot_general x4, matrix products, step(): lax.dot_general(piece, weight_x, (((1,), (1,)), ((), ())), preferred_elem...  5.96 us
  transfers between devices with their start and end apart: 31, of which 15 were waited for; matrix products, arithmetic and copies ran while one was open for 11% of the time, Pallas kernels for 4%

profile of v3, /device:TPU:2, one launch (start us, length us, event | category | flops | bytes accessed | tf_op | source)
XLA Modules:
  0.0 237.8 jit_solution(2974302513925113770)
XLA Ops:
  0.6 1.0 fusion.2
  1.7 1.0 fusion.3
  2.7 1.1 collective-permute-start.10
  3.8 3.2 %collective-permute-start.11 = (bf16[64,1152]{1,0:T(8,128)(2,1)S(1)}, bf16[64,1152]{1,0:T(8,128)(2,1)S(1)}, u32[]{:S(2)}, u32[]{:S(2)}) collective-permute-start(bf16[64,1152]{1,0:T(8,128)(2,1)S(1)} %fusion.3), channel_id=1, source_target_pairs={{0,48},{8,56},{16,32},{24,40},{32,16},{40,24},{48,0},{56,8},{1,49}... | collective-permute-start | bytes 442376 | tf_op jit(solution)/shard_map/ppermute | solution.py:41
  7.8 1.5 reshape.79
  9.3 1.2 constant_dynamic-slice_fusion
  10.5 1.6 collective-permute-start
  12.1 1.2 collective-permute-start.1
  14.1 8.5 %all-to-all-start = ((bf16[8,36,538]{2,1,0:T(8,128)(2,1)}), bf16[8,36,538]{2,1,0:T(8,128)(2,1)S(1)}, u32[]{:S(2)}, u32[]{:S(2)}) async-start(bf16[8,36,538]{2,1,0:T(8,128)(2,1)} %broadcast_in_dim.11), calls=%async_computation | async-start | bytes 819200 | tf_op jit(solution)/shard_map/all_to_all | solution.py:45
  22.8 2.2 collective-permute-start.2
  25.1 2.1 collective-permute-start.13
  27.2 1.3 collective-permute-start.14
  28.6 0.9 constant_dynamic-update-slice_fusion.16
  29.5 8.4 %all-to-all-done = bf16[8,36,538]{2,1,0:T(8,128)(2,1)S(1)} async-done(((bf16[8,36,538]{2,1,0:T(8,128)(2,1)}), bf16[8,36,538]{2,1,0:T(8,128)(2,1)S(1)}, u32[]{:S(2)}, u32[]{:S(2)}) %all-to-all-start) | async-done | bytes 309920 | tf_op jit(solution)/shard_map/all_to_all | solution.py:45
  38.1 0.9 constant_dynamic-update-slice_fusion.15
  40.0 1.5 collective-permute-start.5
  41.5 0.9 constant_dynamic-update-slice_fusion.8
  42.3 5.5 %collective-permute-done.13 = bf16[256,1152]{1,0:T(8,128)(2,1)S(1)} collective-permute-done((bf16[256,1152]{1,0:T(8,128)(2,1)S(1)}, bf16[256,1152]{1,0:T(8,128)(2,1)S(1)}, u32[]{:S(2)}, u32[]{:S(2)}) %collective-permute-start.13) | collective-permute-done | bytes 589856 | tf_op jit(solution)/shard_map/ppermute | solution.py:41
  48.1 3.0 %collective-permute-start.16 = (bf16[256,1152]{1,0:T(8,128)(2,1)S(1)}, bf16[256,1152]{1,0:T(8,128)(2,1)}, u32[]{:S(2)}, u32[]{:S(2)}) collective-permute-start(bf16[256,1152]{1,0:T(8,128)(2,1)S(1)} %collective-permute-done.14), channel_id=1, source_target_pairs={{0,7},{1,0},{2,1},{3,2},{4,3},{5,4},{6,5},{7,6},{8,15},{9,8},{10,9... | collective-permute-start | bytes 1769480 | tf_op jit(solution)/shard_map/ppermute | solution.py:41
  51.1 1.1 broadcast_select_fusion.1
  52.2 15.2 %collective-permute-done.6 = bf16[256,1076]{0,1:T(8,128)(2,1)} collective-permute-done((bf16[256,1076]{0,1:T(8,128)(2,1)S(1)}, bf16[256,1076]{0,1:T(8,128)(2,1)}, u32[]{:S(2)}, u32[]{:S(2)}) %collective-permute-start.6) | collective-permute-done | bytes 550944 | tf_op jit(solution)/shard_map/ppermute | solution.py:41
  67.4 1.4 convolution_convert_fusion
  69.0 1.5 convolution_convert_fusion.1
  70.8 1.6 convolution_convert_fusion.3
  72.4 1.4 convolution_convert_fusion.2
  74.4 1.1 pad_maximum_fusion.1
  75.5 5.6 %all-to-all-start.1 = ((bf16[16,64,288]{2,1,0:T(8,128)(2,1)}), bf16[16,64,288]{2,1,0:T(8,128)(2,1)S(1)}, u32[]{:S(2)}, u32[]{:S(2)}) async-start(bf16[16,64,288]{2,1,0:T(8,128)(2,1)} %bitcast.11), calls=%async_computation.1 | async-start | bytes 1572864 | tf_op jit(solution)/shard_map/all_to_all | solution.py:45
  82.0 0.9 constant_dynamic-update-slice_fusion.6
  82.9 1.7 collective-permute-start.17
  84.6 1.6 collective-permute-start.18
  86.1 1.9 constant_dynamic-update-slice_fusion.5
  88.1 5.0 %all-to-all-done.1 = bf16[16,64,288]{2,1,0:T(8,128)(2,1)S(1)} async-done(((bf16[16,64,288]{2,1,0:T(8,128)(2,1)}), bf16[16,64,288]{2,1,0:T(8,128)(2,1)S(1)}, u32[]{:S(2)}, u32[]{:S(2)}) %all-to-all-start.1) | async-done | bytes 589856 | tf_op jit(solution)/shard_map/all_to_all | solution.py:45
  94.2 1.7 collective-permute-start.7
  96.0 1.9 constant_dynamic-update-slice_fusion.4
  98.0 3.2 %collective-permute-start.8 = (bf16[64,1152]{1,0:T(8,128)(2,1)S(1)}, bf16[64,1152]{1,0:T(8,128)(2,1)S(1)}, u32[]{:S(2)}, u32[]{:S(2)}) collective-permute-start(bf16[64,1152]{1,0:T(8,128)(2,1)S(1)} %fusion.22), channel_id=1, source_target_pairs={{0,128},{64,192},{128,0},{192,64},{1,129},{65,193},{129,1},{193,65... | collective-permute-start | bytes 442376 | tf_op jit(solution)/shard_map/ppermute | solution.py:41
  101.5 3.4 %collective-permute-done.8 = bf16[64,1152]{1,0:T(8,128)(2,1)S(1)} collective-permute-done((bf16[64,1152]{1,0:T(8,128)(2,1)S(1)}, bf16[64,1152]{1,0:T(8,128)(2,1)S(1)}, u32[]{:S(2)}, u32[]{:S(2)}) %collective-permute-start.8) | collective-permute-done | bytes 147488 | tf_op jit(solution)/shard_map/ppermute | solution.py:41
  104.9 1.5 collective-permute-done.9
  106.6 1.7 collective-permute-start.19
  108.3 1.6 collective-permute-start.20
  110.0 0.9 constant_dynamic-update-slice_fusion.3
  111.7 2.9 %collective-permute-done.19 = bf16[128,1152]{1,0:T(8,128)(2,1)S(1)} collective-permute-done((bf16[128,1152]{1,0:T(8,128)(2,1)S(1)}, bf16[128,1152]{1,0:T(8,128)(2,1)S(1)}, u32[]{:S(2)}, u32[]{:S(2)}) %collective-permute-start.19) | collective-permute-done | bytes 294944 | tf_op jit(solution)/shard_map/ppermute | solution.py:41
  118.6 8.8 %shard_map.111 = (f32[256,1152]{1,0:T(8,128)}, f32[1,512]{1,0:T(1,128)}) custom-call(f32[2]{0:T(128)} %pad_maximum_fusion.3.scalars, bf16[256,1152]{1,0:T(8,128)(2,1)} %copy-done.1, bf16[2048,1152]{1,0:T(8,128)(2,1)} %constant_dynamic-update-slice_fusion.texts), custom_call_target="tpu_custom_call" | custom-call | flops 2415919104 | bytes 4718592 | tf_op jit(solution)/shard_map/pallas_call | solution.py:133
  127.3 9.3 %shard_map.112 = (f32[256,1152]{1,0:T(8,128)}, bf16[256,1152]{1,0:T(8,128)(2,1)}, f32[1,512]{1,0:T(1,128)}) custom-call(f32[2]{0:T(128)} %pad_maximum_fusion.3.scalars, bf16[256,1152]{1,0:T(8,128)(2,1)} %copy-done.1, bf16[2048,1152]{1,0:T(8,128)(2,1)} %collective-permute-done.21.texts, f32[256,1152]{1,0:T(8,128)} %get-tuple-element.21.refs_0_), custom_call_target="tpu_custom_call" | custom-call | flops 2415919104 | bytes 4718592 | tf_op jit(solution)/shard_map/pallas_call | solution.py:133
  136.7 1.1 fusion.24
  138.4 2.9 %collective-permute-start.23 = (bf16[64,1152]{1,0:T(8,128)(2,1)S(1)}, bf16[64,1152]{1,0:T(8,128)(2,1)S(1)}, u32[]{:S(2)}, u32[]{:S(2)}) collective-permute-start(bf16[64,1152]{1,0:T(8,128)(2,1)S(1)} %get-tuple-element.38), channel_id=1, source_target_pairs={{0,128},{64,192},{128,0},{192,64},{1,129},{65,193},{129,1},{193,65... | collective-permute-start | bytes 442376 | tf_op jit(solution)/shard_map/ppermute | solution.py:41
  141.3 2.1 collective-permute-start.22
  144.1 2.5 %collective-permute-done.23 = bf16[64,1152]{1,0:T(8,128)(2,1)S(1)} collective-permute-done((bf16[64,1152]{1,0:T(8,128)(2,1)S(1)}, bf16[64,1152]{1,0:T(8,128)(2,1)S(1)}, u32[]{:S(2)}, u32[]{:S(2)}) %collective-permute-start.23) | collective-permute-done | bytes 147488 | tf_op jit(solution)/shard_map/ppermute | solution.py:41
  146.6 2.4 %collective-permute-done.22 = bf16[64,1152]{1,0:T(8,128)(2,1)S(1)} collective-permute-done((bf16[64,1152]{1,0:T(8,128)(2,1)S(1)}, bf16[64,1152]{1,0:T(8,128)(2,1)S(1)}, u32[]{:S(2)}, u32[]{:S(2)}) %collective-permute-start.22) | collective-permute-done | bytes 147488 | tf_op jit(solution)/shard_map/ppermute | solution.py:41
  149.1 1.2 multiply_reduce_fusion
  150.2 1.1 divide_convert_fusion
  151.6 1.0 broadcast_in_dim.12
  152.6 7.3 %all-to-all-start.2 = ((bf16[16,64,288]{2,1,0:T(8,128)(2,1)}), bf16[16,64,288]{2,1,0:T(8,128)(2,1)S(1)}, u32[]{:S(2)}, u32[]{:S(2)}) async-start(bf16[16,64,288]{2,1,0:T(8,128)(2,1)} %bitcast.15), calls=%async_computation.2 | async-start | bytes 1572864 | tf_op jit(solution)/shard_map/all_to_all | solution.py:45
  159.9 12.2 %all-to-all-done.2 = bf16[16,64,288]{2,1,0:T(8,128)(2,1)S(1)} async-done(((bf16[16,64,288]{2,1,0:T(8,128)(2,1)}), bf16[16,64,288]{2,1,0:T(8,128)(2,1)S(1)}, u32[]{:S(2)}, u32[]{:S(2)}) %all-to-all-start.2) | async-done | bytes 589856 | tf_op jit(solution)/shard_map/all_to_all | solution.py:45
  172.2 1.5 fusion.5
  173.7 1.5 fusion.7
  175.3 1.5 fusion.9
  177.6 2.2 collective-permute-done.25
  181.0 4.0 %all-to-all-start.3 = ((bf16[8,36,538]{2,1,0:T(8,128)(2,1)}), bf16[8,36,538]{2,1,0:T(8,128)(2,1)S(1)}, u32[]{:S(2)}, u32[]{:S(2)}) async-start(bf16[8,36,538]{2,1,0:T(8,128)(2,1)} %reshape.90), calls=%async_computation.3 | async-start | bytes 819200 | tf_op jit(solution)/shard_map/all_to_all | solution.py:45
  185.6 14.7 %all-to-all-done.3 = bf16[8,36,538]{2,1,0:T(8,128)(2,1)S(1)} async-done(((bf16[8,36,538]{2,1,0:T(8,128)(2,1)}), bf16[8,36,538]{2,1,0:T(8,128)(2,1)S(1)}, u32[]{:S(2)}, u32[]{:S(2)}) %all-to-all-start.3) | async-done | bytes 309920 | tf_op jit(solution)/shard_map/all_to_all | solution.py:45
  201.3 8.8 %all_to_all.35 = f32[8,1,37]{2,1,0:T(1,128)S(1)} all-to-all(f32[8,1,37]{2,1,0:T(1,128)S(1)} %broadcast_in_dim.13), channel_id=1, replica_groups=mesh['x'=4,'k'=2,'y'=4,'z'=8] {'x','k'}, dimensions={0} | all-to-all | bytes 2368 | tf_op jit(solution)/shard_map/all_to_all | solution.py:45
  211.6 13.8 %all_to_all.36 = f32[32,1,1077]{2,1,0:T(1,128)S(1)} all-to-all(f32[32,1,1077]{2,1,0:T(1,128)S(1)} %broadcast_in_dim.14), channel_id=1, replica_groups=mesh['x'=4,'k'=2,'y'=4,'z'=8] {'y','z'}, dimensions={0} | all-to-all | bytes 275712 | tf_op jit(solution)/shard_map/all_to_all | solution.py:45
  226.2 1.2 broadcast_in_dim_broadcast_in_dim.3
  227.4 4.7 %all-to-all-start.6 = ((f32[8,1,128]{2,1,0:T(1,128)}), f32[8,1,128]{2,1,0:T(1,128)S(1)}, u32[]{:S(2)}, u32[]{:S(2)}) async-start(f32[8,1,128]{2,1,0:T(1,128)} %broadcast_in_dim_broadcast_in_dim.3), calls=%async_computation.6 | async-start | bytes 8192 | tf_op jit(solution)/shard_map/all_to_all | solution.py:45
  233.3 2.6 %all-to-all-done.6 = f32[8,1,128]{2,1,0:T(1,128)S(1)} async-done(((f32[8,1,128]{2,1,0:T(1,128)}), f32[8,1,128]{2,1,0:T(1,128)S(1)}, u32[]{:S(2)}, u32[]{:S(2)}) %all-to-all-start.6) | async-done | bytes 4128 | tf_op jit(solution)/shard_map/all_to_all | solution.py:45
  (114 shorter events, 18.9 us)
Async XLA Ops:
  2.7 22.3 %collective-permute-start.10 = (bf16[64,1152]{1,0:T(8,128)(2,1)S(1)}, bf16[64,1152]{1,0:T(8,128)(2,1)S(1)}, u32[]{:S(2)}, u32[]{:S(2)}) collective-permute-start(bf16[64,1152]{1,0:T(8,128)(2,1)S(1)} %fusion.3), channel_id=1, source_target_pairs={{0,40},{8,48},{16,56},{24,32},{32,8},{40,16},{48,24},{56,0},{1,41}... | collective-permute-start | bytes 442376 | tf_op jit(solution)/shard_map/ppermute | solution.py:41
  3.8 21.3 %collective-permute-start.11 = (bf16[64,1152]{1,0:T(8,128)(2,1)S(1)}, bf16[64,1152]{1,0:T(8,128)(2,1)S(1)}, u32[]{:S(2)}, u32[]{:S(2)}) collective-permute-start(bf16[64,1152]{1,0:T(8,128)(2,1)S(1)} %fusion.3), channel_id=1, source_target_pairs={{0,48},{8,56},{16,32},{24,40},{32,16},{40,24},{48,0},{56,8},{1,49}... | collective-permute-start | bytes 442376 | tf_op jit(solution)/shard_map/ppermute | solution.py:41
  7.0 18.1 %collective-permute-start.12 = (bf16[64,1152]{1,0:T(8,128)(2,1)S(1)}, bf16[64,1152]{1,0:T(8,128)(2,1)S(1)}, u32[]{:S(2)}, u32[]{:S(2)}) collective-permute-start(bf16[64,1152]{1,0:T(8,128)(2,1)S(1)} %fusion.3), channel_id=1, source_target_pairs={{0,56},{8,32},{16,40},{24,48},{32,24},{40,0},{48,8},{56,16},{1,57}... | collective-permute-start | bytes 442376 | tf_op jit(solution)/shard_map/ppermute | solution.py:41
  9.3 4.1 %copy-start.6 = (f32[36,538]{1,0:T(8,128)S(1)}, f32[36,538]{1,0:T(8,128)}, u32[]{:S(2)}) copy-start(f32[36,538]{1,0:T(8,128)} %param.11) | copy-start | bytes 232420
  10.5 12.2 %collective-permute-start = (bf16[1,64,1076]{2,1,0:T(8,128)(2,1)S(1)}, bf16[1,64,1076]{2,1,0:T(8,128)(2,1)S(1)}, u32[]{:S(2)}, u32[]{:S(2)}) collective-permute-start(bf16[1,64,1076]{2,1,0:T(8,128)(2,1)S(1)} %bitcast.80), channel_id=1, source_target_pairs={{0,64},{64,128},{128,192},{192,0},{1,65},{65,129},{129,193},{193,1... | collective-permute-start | bytes 413192 | tf_op jit(solution)/shard_map/ppermute | solution.py:41
  12.1 16.4 %collective-permute-start.1 = (bf16[1,64,1076]{2,1,0:T(8,128)(2,1)S(1)}, bf16[1,64,1076]{2,1,0:T(8,128)(2,1)}, u32[]{:S(2)}, u32[]{:S(2)}) collective-permute-start(bf16[1,64,1076]{2,1,0:T(8,128)(2,1)S(1)} %bitcast.78), channel_id=1, source_target_pairs={{0,128},{64,192},{128,0},{192,64},{1,129},{65,193},{129,1},{193,65... | collective-permute-start | bytes 413192 | tf_op jit(solution)/shard_map/ppermute | solution.py:41
  14.1 23.7 %all-to-all-start = ((bf16[8,36,538]{2,1,0:T(8,128)(2,1)}), bf16[8,36,538]{2,1,0:T(8,128)(2,1)S(1)}, u32[]{:S(2)}, u32[]{:S(2)}) async-start(bf16[8,36,538]{2,1,0:T(8,128)(2,1)} %broadcast_in_dim.11), calls=%async_computation | async-start | bytes 819200 | tf_op jit(solution)/shard_map/all_to_all | solution.py:45
  22.8 15.3 %collective-permute-start.2 = (bf16[1,64,1076]{2,1,0:T(8,128)(2,1)S(1)}, bf16[1,64,1076]{2,1,0:T(8,128)(2,1)}, u32[]{:S(2)}, u32[]{:S(2)}) collective-permute-start(bf16[1,64,1076]{2,1,0:T(8,128)(2,1)S(1)} %bitcast.79), channel_id=1, source_target_pairs={{0,192},{64,0},{128,64},{192,128},{1,193},{65,1},{129,65},{193,129... | collective-permute-start | bytes 413192 | tf_op jit(solution)/shard_map/ppermute | solution.py:41
  25.1 22.7 %collective-permute-start.13 = (bf16[256,1152]{1,0:T(8,128)(2,1)S(1)}, bf16[256,1152]{1,0:T(8,128)(2,1)S(1)}, u32[]{:S(2)}, u32[]{:S(2)}) collective-permute-start(bf16[256,1152]{1,0:T(8,128)(2,1)S(1)} %constant_dynamic-update-slice_fusion.9), channel_id=1, source_target_pairs={{0,1},{1,2},{2,3},{3,4},{4,5},{5,6},{6,7},{7,0},{8,9},{9,10},{10,1... | collective-permute-start | bytes 1769480 | tf_op jit(solution)/shard_map/ppermute | solution.py:41
  27.2 20.6 %collective-permute-start.14 = (bf16[256,1152]{1,0:T(8,128)(2,1)S(1)}, bf16[256,1152]{1,0:T(8,128)(2,1)S(1)}, u32[]{:S(2)}, u32[]{:S(2)}) collective-permute-start(bf16[256,1152]{1,0:T(8,128)(2,1)S(1)} %constant_dynamic-update-slice_fusion.9), channel_id=1, source_target_pairs={{0,7},{1,0},{2,1},{3,2},{4,3},{5,4},{6,5},{7,6},{8,15},{9,8},{10,9... | collective-permute-start | bytes 1769480 | tf_op jit(solution)/shard_map/ppermute | solution.py:41
  38.0 10.2 %collective-permute-start.3 = (bf16[288,538]{1,0:T(8,128)(2,1)S(1)}, bf16[288,538]{1,0:T(8,128)(2,1)}, u32[]{:S(2)}, u32[]{:S(2)}) collective-permute-start(bf16[288,538]{1,0:T(8,128)(2,1)S(1)} %reshape.81), channel_id=1, source_target_pairs={{0,32},{32,0},{1,33},{33,1},{2,34},{34,2},{3,35},{35,3},{4,36},{36... | collective-permute-start | bytes 929672 | tf_op jit(solution)/shard_map/ppermute | solution.py:41
  39.2 28.2 %collective-permute-start.6 = (bf16[256,1076]{0,1:T(8,128)(2,1)S(1)}, bf16[256,1076]{0,1:T(8,128)(2,1)}, u32[]{:S(2)}, u32[]{:S(2)}) collective-permute-start(bf16[256,1076]{0,1:T(8,128)(2,1)S(1)} %copy.56), channel_id=1, source_target_pairs={{0,8},{8,16},{16,24},{24,0},{1,9},{9,17},{17,25},{25,1},{2,10},{10... | collective-permute-start | bytes 1652744 | tf_op jit(solution)/shard_map/ppermute | solution.py:41
  40.0 29.0 %collective-permute-start.5 = (bf16[256,1076]{0,1:T(8,128)(2,1)S(1)}, bf16[256,1076]{0,1:T(8,128)(2,1)}, u32[]{:S(2)}, u32[]{:S(2)}) collective-permute-start(bf16[256,1076]{0,1:T(8,128)(2,1)S(1)} %copy.56), channel_id=1, source_target_pairs={{0,16},{8,24},{16,0},{24,8},{1,17},{9,25},{17,1},{25,9},{2,18},{10... | collective-permute-start | bytes 1652744 | tf_op jit(solution)/shard_map/ppermute | solution.py:41
  47.9 24.5 %collective-permute-start.4 = (bf16[256,1076]{0,1:T(8,128)(2,1)S(1)}, bf16[256,1076]{0,1:T(8,128)(2,1)}, u32[]{:S(2)}, u32[]{:S(2)}) collective-permute-start(bf16[256,1076]{0,1:T(8,128)(2,1)S(1)} %copy.56), channel_id=1, source_target_pairs={{0,24},{8,0},{16,8},{24,16},{1,25},{9,1},{17,9},{25,17},{2,26},{10... | collective-permute-start | bytes 1652744 | tf_op jit(solution)/shard_map/ppermute | solution.py:41
  47.9 35.0 %collective-permute-start.15 = (bf16[256,1152]{1,0:T(8,128)(2,1)S(1)}, bf16[256,1152]{1,0:T(8,128)(2,1)}, u32[]{:S(2)}, u32[]{:S(2)}) collective-permute-start(bf16[256,1152]{1,0:T(8,128)(2,1)S(1)} %collective-permute-done.13), channel_id=1, source_target_pairs={{0,1},{1,2},{2,3},{3,4},{4,5},{5,6},{6,7},{7,0},{8,9},{9,10},{10,1... | collective-permute-start | bytes 1769480 | tf_op jit(solution)/shard_map/ppermute | solution.py:41
  48.1 34.8 %collective-permute-start.16 = (bf16[256,1152]{1,0:T(8,128)(2,1)S(1)}, bf16[256,1152]{1,0:T(8,128)(2,1)}, u32[]{:S(2)}, u32[]{:S(2)}) collective-permute-start(bf16[256,1152]{1,0:T(8,128)(2,1)S(1)} %collective-permute-done.14), channel_id=1, source_target_pairs={{0,7},{1,0},{2,1},{3,2},{4,3},{5,4},{6,5},{7,6},{8,15},{9,8},{10,9... | collective-permute-start | bytes 1769480 | tf_op jit(solution)/shard_map/ppermute | solution.py:41
  52.2 15.2 %copy-start.4 = (bf16[288,538]{1,0:T(8,128)(2,1)}, bf16[288,538]{1,0:T(8,128)(2,1)S(1)}, u32[]{:S(2)}) copy-start(bf16[288,538]{1,0:T(8,128)(2,1)S(1)} %get-tuple-element.35) | copy-start | bytes 929668
  52.2 16.8 %copy-start.2 = (bf16[288,538]{1,0:T(8,128)(2,1)}, bf16[288,538]{1,0:T(8,128)(2,1)S(1)}, u32[]{:S(2)}) copy-start(bf16[288,538]{1,0:T(8,128)(2,1)S(1)} %get-tuple-element.34) | copy-start | bytes 929668
  70.6 1.8 copy-start.3
  70.8 1.6 copy-start.5
  75.5 17.5 %all-to-all-start.1 = ((bf16[16,64,288]{2,1,0:T(8,128)(2,1)}), bf16[16,64,288]{2,1,0:T(8,128)(2,1)S(1)}, u32[]{:S(2)}, u32[]{:S(2)}) async-start(bf16[16,64,288]{2,1,0:T(8,128)(2,1)} %bitcast.11), calls=%async_computation.1 | async-start | bytes 1572864 | tf_op jit(solution)/shard_map/all_to_all | solution.py:45
  82.9 23.6 %collective-permute-start.17 = (bf16[256,1152]{1,0:T(8,128)(2,1)}, bf16[256,1152]{1,0:T(8,128)(2,1)S(1)}, u32[]{:S(2)}, u32[]{:S(2)}) collective-permute-start(bf16[256,1152]{1,0:T(8,128)(2,1)} %collective-permute-done.15), channel_id=1, source_target_pairs={{0,1},{1,2},{2,3},{3,4},{4,5},{5,6},{6,7},{7,0},{8,9},{9,10},{10,1... | collective-permute-start | bytes 1769480 | tf_op jit(solution)/shard_map/ppermute | solution.py:41
  84.6 22.0 %collective-permute-start.18 = (bf16[256,1152]{1,0:T(8,128)(2,1)}, bf16[256,1152]{1,0:T(8,128)(2,1)S(1)}, u32[]{:S(2)}, u32[]{:S(2)}) collective-permute-start(bf16[256,1152]{1,0:T(8,128)(2,1)} %collective-permute-done.16), channel_id=1, source_target_pairs={{0,7},{1,0},{2,1},{3,2},{4,3},{5,4},{6,5},{7,6},{8,15},{9,8},{10,9... | collective-permute-start | bytes 1769480 | tf_op jit(solution)/shard_map/ppermute | solution.py:41
  93.1 0.9 copy-start
  94.2 7.2 %collective-permute-start.7 = (bf16[64,1152]{1,0:T(8,128)(2,1)S(1)}, bf16[64,1152]{1,0:T(8,128)(2,1)S(1)}, u32[]{:S(2)}, u32[]{:S(2)}) collective-permute-start(bf16[64,1152]{1,0:T(8,128)(2,1)S(1)} %fusion.22), channel_id=1, source_target_pairs={{0,64},{64,128},{128,192},{192,0},{1,65},{65,129},{129,193},{193,1... | collective-permute-start | bytes 442376 | tf_op jit(solution)/shard_map/ppermute | solution.py:41
  98.0 6.9 %collective-permute-start.8 = (bf16[64,1152]{1,0:T(8,128)(2,1)S(1)}, bf16[64,1152]{1,0:T(8,128)(2,1)S(1)}, u32[]{:S(2)}, u32[]{:S(2)}) collective-permute-start(bf16[64,1152]{1,0:T(8,128)(2,1)S(1)} %fusion.22), channel_id=1, source_target_pairs={{0,128},{64,192},{128,0},{192,64},{1,129},{65,193},{129,1},{193,65... | collective-permute-start | bytes 442376 | tf_op jit(solution)/shard_map/ppermute | solution.py:41
  101.2 5.3 %collective-permute-start.9 = (bf16[64,1152]{1,0:T(8,128)(2,1)S(1)}, bf16[64,1152]{1,0:T(8,128)(2,1)S(1)}, u32[]{:S(2)}, u32[]{:S(2)}) collective-permute-start(bf16[64,1152]{1,0:T(8,128)(2,1)S(1)} %fusion.22), channel_id=1, source_target_pairs={{0,192},{64,0},{128,64},{192,128},{1,193},{65,1},{129,65},{193,129... | collective-permute-start | bytes 442376 | tf_op jit(solution)/shard_map/ppermute | solution.py:41
  106.5 5.2 %copy-start.1 = (bf16[256,1152]{1,0:T(8,128)(2,1)}, bf16[256,1152]{1,0:T(8,128)(2,1)S(1)}, u32[]{:S(2)}) copy-start(bf16[256,1152]{1,0:T(8,128)(2,1)S(1)} %constant_dynamic-update-slice_fusion.12.images) | copy-start | bytes 1769476
  106.6 8.0 %collective-permute-start.19 = (bf16[128,1152]{1,0:T(8,128)(2,1)S(1)}, bf16[128,1152]{1,0:T(8,128)(2,1)S(1)}, u32[]{:S(2)}, u32[]{:S(2)}) collective-permute-start(bf16[128,1152]{1,0:T(8,128)(2,1)S(1)} %slice.42), channel_id=1, source_target_pairs={{0,1},{1,2},{2,3},{3,4},{4,5},{5,6},{6,7},{7,0},{8,9},{9,10},{10,1... | collective-permute-start | bytes 884744 | tf_op jit(solution)/shard_map/ppermute | solution.py:41
  108.3 6.8 %collective-permute-start.20 = (bf16[128,1152]{1,0:T(8,128)(2,1)S(1)}, bf16[128,1152]{1,0:T(8,128)(2,1)S(1)}, u32[]{:S(2)}, u32[]{:S(2)}) collective-permute-start(bf16[128,1152]{1,0:T(8,128)(2,1)S(1)} %slice.43), channel_id=1, source_target_pairs={{0,7},{1,0},{2,1},{3,2},{4,3},{5,4},{6,5},{7,6},{8,15},{9,8},{10,9... | collective-permute-start | bytes 884744 | tf_op jit(solution)/shard_map/ppermute | solution.py:41
  116.6 10.8 %collective-permute-start.21 = (bf16[2048,1152]{1,0:T(8,128)(2,1)}, bf16[2048,1152]{1,0:T(8,128)(2,1)}, u32[]{:S(2)}, u32[]{:S(2)}) collective-permute-start(bf16[2048,1152]{1,0:T(8,128)(2,1)} %constant_dynamic-update-slice_fusion.texts), channel_id=1, source_target_pairs={{0,32},{32,0},{1,33},{33,1},{2,34},{34,2},{3,35},{35,3},{4,36},{36... | collective-permute-start | bytes 14155784 | tf_op jit(solution)/shard_map/ppermute | solution.py:41
  137.8 6.3 %collective-permute-start.24 = (bf16[64,1152]{1,0:T(8,128)(2,1)S(1)}, bf16[64,1152]{1,0:T(8,128)(2,1)S(1)}, u32[]{:S(2)}, u32[]{:S(2)}) collective-permute-start(bf16[64,1152]{1,0:T(8,128)(2,1)S(1)} %get-tuple-element.37), channel_id=1, source_target_pairs={{0,64},{64,128},{128,192},{192,0},{1,65},{65,129},{129,193},{193,1... | collective-permute-start | bytes 442376 | tf_op jit(solution)/shard_map/ppermute | solution.py:41
  138.4 8.2 %collective-permute-start.23 = (bf16[64,1152]{1,0:T(8,128)(2,1)S(1)}, bf16[64,1152]{1,0:T(8,128)(2,1)S(1)}, u32[]{:S(2)}, u32[]{:S(2)}) collective-permute-start(bf16[64,1152]{1,0:T(8,128)(2,1)S(1)} %get-tuple-element.38), channel_id=1, source_target_pairs={{0,128},{64,192},{128,0},{192,64},{1,129},{65,193},{129,1},{193,65... | collective-permute-start | bytes 442376 | tf_op jit(solution)/shard_map/ppermute | solution.py:41
  141.3 7.7 %collective-permute-start.22 = (bf16[64,1152]{1,0:T(8,128)(2,1)S(1)}, bf16[64,1152]{1,0:T(8,128)(2,1)S(1)}, u32[]{:S(2)}, u32[]{:S(2)}) collective-permute-start(bf16[64,1152]{1,0:T(8,128)(2,1)S(1)} %get-tuple-element.36), channel_id=1, source_target_pairs={{0,192},{64,0},{128,64},{192,128},{1,193},{65,1},{129,65},{193,129... | collective-permute-start | bytes 442376 | tf_op jit(solution)/shard_map/ppermute | solution.py:41
  152.6 19.5 %all-to-all-start.2 = ((bf16[16,64,288]{2,1,0:T(8,128)(2,1)}), bf16[16,64,288]{2,1,0:T(8,128)(2,1)S(1)}, u32[]{:S(2)}, u32[]{:S(2)}) async-start(bf16[16,64,288]{2,1,0:T(8,128)(2,1)} %bitcast.15), calls=%async_computation.2 | async-start | bytes 1572864 | tf_op jit(solution)/shard_map/all_to_all | solution.py:45
  177.5 2.3 collective-permute-start.25
  180.1 4.9 %copy-start.10 = (f32[1,512]{1,0:T(1,128)S(1)}, f32[1,512]{1,0:T(1,128)}, u32[]{:S(2)}) copy-start(f32[1,512]{1,0:T(1,128)} %get-tuple-element.24) | copy-start | bytes 6148
  180.1 4.9 %copy-start.11 = (f32[1,512]{1,0:T(1,128)S(1)}, f32[1,512]{1,0:T(1,128)}, u32[]{:S(2)}) copy-start(f32[1,512]{1,0:T(1,128)} %get-tuple-element.25) | copy-start | bytes 6148
  180.1 30.6 %copy-start.12 = (f32[36]{0:T(128)S(1)}, f32[36]{0:T(128)}, u32[]{:S(2)}) copy-start(f32[36]{0:T(128)} %param.12) | copy-start | bytes 436
  180.1 45.4 %copy-start.8 = (f32[538]{0:T(1024)S(1)}, f32[538]{0:T(1024)}, u32[]{:S(2)}) copy-start(f32[538]{0:T(1024)} %param.13) | copy-start | bytes 6460
  181.0 19.4 %all-to-all-start.3 = ((bf16[8,36,538]{2,1,0:T(8,128)(2,1)}), bf16[8,36,538]{2,1,0:T(8,128)(2,1)S(1)}, u32[]{:S(2)}, u32[]{:S(2)}) async-start(bf16[8,36,538]{2,1,0:T(8,128)(2,1)} %reshape.90), calls=%async_computation.3 | async-start | bytes 819200 | tf_op jit(solution)/shard_map/all_to_all | solution.py:45
  210.7 26.0 %copy-start.9 = (f32[36]{0:T(128)}, f32[36]{0:T(128)S(1)}, u32[]{:S(2)}) copy-start(f32[36]{0:T(128)S(1)} %multiply_add_fusion) | copy-start | bytes 436
  226.2 10.6 %copy-start.7 = (f32[538]{0:T(1024)}, f32[538]{0:T(1024)S(1)}, u32[]{:S(2)}) copy-start(f32[538]{0:T(1024)S(1)} %get-tuple-element.29) | copy-start | bytes 6460
  227.4 8.5 %all-to-all-start.6 = ((f32[8,1,128]{2,1,0:T(1,128)}), f32[8,1,128]{2,1,0:T(1,128)S(1)}, u32[]{:S(2)}, u32[]{:S(2)}) async-start(f32[8,1,128]{2,1,0:T(1,128)} %broadcast_in_dim_broadcast_in_dim.3), calls=%async_computation.6 | async-start | bytes 8192 | tf_op jit(solution)/shard_map/all_to_all | solution.py:45

commit v4 on v3

--- a/solution.py
+++ b/solution.py
@@ -114,7 +114,7 @@
         loss[...] += jnp.sum(softplus, axis=0, keepdims=True)
         return 0
 
-    lax.fori_loop(0, count, one, 0)
+    lax.fori_loop(0, count, one, 0, unroll=2)
     if not first:
         scaled = scalars[0] * part[...]
         part[...] = scaled
@@ -173,7 +173,9 @@
     up, down = ring_step(up, down, "z")
     ring_pieces += [up, down]
 
-    weight_own = everywhere(weight.astype(BF16), "z").reshape(quarter, slice_ff)
+    scalars = jnp.stack([jnp.exp(log_scale), bias])
+    weight_own = everywhere(after(weight.astype(BF16), hidden_x), "z")
+    weight_own = after(weight_own.reshape(quarter, slice_ff), scalars)
     weight_other = shift(weight_own, k=1)
     weight_x = jnp.concatenate(
         [
@@ -203,19 +205,17 @@
     up, down = ring_step(*after((up, down), partial), "z")
     ring_pieces += [up, down]
     arrived = exchange(partial.reshape(16, tokens, quarter), ("x", "y"))
-    half = texts_y.shape[0] // 2
-    up, down = after((up, down), arrived)
-    ring_pieces += ring_step(up[:half], down[half:], "z")
     projected = jnp.sum(arrived.astype(F32).reshape(4, 4, tokens, quarter), axis=0)
     mixed = pooled.astype(F32) + jnp.moveaxis(projected, 0, 1).reshape(tokens, D)
     length = jnp.sqrt(jnp.sum(mixed * mixed, axis=1, keepdims=True) + EPSILON)
     unit = mixed / length
     images = unit.astype(BF16)
-    logit_scale = jnp.exp(log_scale)
+    half = texts_y.shape[0] // 2
+    up, down = after((up, down), images)
+    ring_pieces += ring_step(up[:half], down[half:], "z")
     image_rows = joined([images] + [shift(images, x=s) for s in (1, 2, 3)])
     texts_own = jnp.concatenate(ring_pieces[:-2] + after(ring_pieces[-2:], image_rows))
     texts_other = shift(texts_own, k=1)
-    scalars = jnp.stack([logit_scale, bias])
     part_a, loss_a = pair_tiles(scalars, image_rows, texts_own, None, tokens, batch_total)
     part, part_sent, loss_b = pair_tiles(
         scalars, image_rows, texts_other, part_a, tokens, batch_total

time: 241 us -> 245 us (1.017)
  waiting for transfers between devices: 79.9 us -> 89.3 us
    ppermute x26, waiting for transfers between devices: 37.1 us -> 45 us  [shift(): return lax.ppermute(value, names, pairs)]
  transfers between devices with their start and end apart: 31 -> 31, of which waited for: 15 -> 18; matrix products, arithmetic and copies ran while one was open for 11% -> 10% of each run, Pallas kernels for 4% -> 3%
where the time goes in v4:
time: 245 us; the launch traced here: 242 us
  waiting for transfers between devices  89.3 us (36%)
  starting transfers between devices  64.7 us (26%)
  blocking collectives  22.6 us (9%)
  local copies, waits for them, and re-layouts  22 us (9%)
  Pallas kernels  16.4 us (7%)
  other arithmetic  11.4 us (5%)
  matrix products  11 us (4%)
  between operations  4.36 us (2%)
    ppermute x26, waiting for transfers between devices, shift(): return lax.ppermute(value, names, pairs)  45 us
    all_to_all x5, waiting for transfers between devices, exchange(): return lax.all_to_all(pieces, axes, split_axis=0, concat_axis=0, tiled=True)  44.3 us
    ppermute x26, starting transfers between devices, shift(): return lax.ppermute(value, names, pairs)  34.8 us
    all_to_all x5, starting transfers between devices, exchange(): return lax.all_to_all(pieces, axes, split_axis=0, concat_axis=0, tiled=True)  30 us
    all_to_all x2, blocking collectives, exchange(): return lax.all_to_all(pieces, axes, split_axis=0, concat_axis=0, tiled=True)  22.6 us
    pallas_call x2, Pallas kernels, pair_tiles(): pl.pallas_call(functools.partial(pair_kernel, first=first, tokens=tokens,...  16.4 us
    unnamed x37, local copies, waits for them, and re-layouts  9.39 us
    dot_general x4, matrix products, step(): lax.dot_general(piece, weight_x, (((1,), (1,)), ((), ())), preferred_elem...  5.96 us
  transfers between devices with their start and end apart: 31, of which 18 were waited for; matrix products, arithmetic and copies ran while one was open for 10% of the time, Pallas kernels for 3%

profile of v4, /device:TPU:2, one launch (start us, length us, event | category | flops | bytes accessed | tf_op | source)
XLA Modules:
  0.0 241.8 jit_solution(389632579125698498)
XLA Ops:
  0.6 1.0 fusion.2
  1.7 1.0 fusion.3
  2.7 1.1 collective-permute-start.10
  3.8 3.2 %collective-permute-start.11 = (bf16[64,1152]{1,0:T(8,128)(2,1)S(1)}, bf16[64,1152]{1,0:T(8,128)(2,1)S(1)}, u32[]{:S(2)}, u32[]{:S(2)}) collective-permute-start(bf16[64,1152]{1,0:T(8,128)(2,1)S(1)} %fusion.3), channel_id=1, source_target_pairs={{0,48},{8,56},{16,32},{24,40},{32,16},{40,24},{48,0},{56,8},{1,49}... | collective-permute-start | bytes 442376 | tf_op jit(solution)/shard_map/ppermute | solution.py:41
  7.8 1.5 reshape.79
  9.3 1.2 constant_dynamic-slice_fusion
  10.5 1.6 collective-permute-start
  12.1 1.2 collective-permute-start.1
  13.5 3.8 %collective-permute-done = bf16[1,64,1076]{2,1,0:T(8,128)(2,1)S(1)} collective-permute-done((bf16[1,64,1076]{2,1,0:T(8,128)(2,1)S(1)}, bf16[1,64,1076]{2,1,0:T(8,128)(2,1)S(1)}, u32[]{:S(2)}, u32[]{:S(2)}) %collective-permute-start) | collective-permute-done | bytes 137760 | tf_op jit(solution)/shard_map/ppermute | solution.py:41
  17.3 1.5 collective-permute-start.2
  18.8 1.1 collective-permute-done.1
  19.9 3.1 %collective-permute-done.2 = bf16[1,64,1076]{2,1,0:T(8,128)(2,1)S(1)} collective-permute-done((bf16[1,64,1076]{2,1,0:T(8,128)(2,1)S(1)}, bf16[1,64,1076]{2,1,0:T(8,128)(2,1)S(1)}, u32[]{:S(2)}, u32[]{:S(2)}) %collective-permute-start.2) | collective-permute-done | bytes 137760 | tf_op jit(solution)/shard_map/ppermute | solution.py:41
  23.8 8.5 %all-to-all-start = ((bf16[8,36,538]{2,1,0:T(8,128)(2,1)}), bf16[8,36,538]{2,1,0:T(8,128)(2,1)S(1)}, u32[]{:S(2)}, u32[]{:S(2)}) async-start(bf16[8,36,538]{2,1,0:T(8,128)(2,1)} %broadcast_in_dim.11), calls=%async_computation | async-start | bytes 819200 | tf_op jit(solution)/shard_map/all_to_all | solution.py:45
  32.4 2.1 collective-permute-start.13
  34.5 1.3 collective-permute-start.14
  37.8 9.8 %all-to-all-done = bf16[8,36,538]{2,1,0:T(8,128)(2,1)S(1)} async-done(((bf16[8,36,538]{2,1,0:T(8,128)(2,1)}), bf16[8,36,538]{2,1,0:T(8,128)(2,1)S(1)}, u32[]{:S(2)}, u32[]{:S(2)}) %all-to-all-start) | async-done | bytes 309920 | tf_op jit(solution)/shard_map/all_to_all | solution.py:45
  49.5 0.9 constant_dynamic-update-slice_fusion.8
  50.3 6.2 %collective-permute-done.13 = bf16[256,1152]{1,0:T(8,128)(2,1)S(1)} collective-permute-done((bf16[256,1152]{1,0:T(8,128)(2,1)S(1)}, bf16[256,1152]{1,0:T(8,128)(2,1)S(1)}, u32[]{:S(2)}, u32[]{:S(2)}) %collective-permute-start.13) | collective-permute-done | bytes 589856 | tf_op jit(solution)/shard_map/ppermute | solution.py:41
  56.8 3.0 %collective-permute-start.16 = (bf16[256,1152]{1,0:T(8,128)(2,1)S(1)}, bf16[256,1152]{1,0:T(8,128)(2,1)}, u32[]{:S(2)}, u32[]{:S(2)}) collective-permute-start(bf16[256,1152]{1,0:T(8,128)(2,1)S(1)} %collective-permute-done.14), channel_id=1, source_target_pairs={{0,7},{1,0},{2,1},{3,2},{4,3},{5,4},{6,5},{7,6},{8,15},{9,8},{10,9... | collective-permute-start | bytes 1769480 | tf_op jit(solution)/shard_map/ppermute | solution.py:41
  59.8 1.1 broadcast_select_fusion.1
  60.9 15.4 %collective-permute-done.6 = bf16[256,1076]{0,1:T(8,128)(2,1)} collective-permute-done((bf16[256,1076]{0,1:T(8,128)(2,1)S(1)}, bf16[256,1076]{0,1:T(8,128)(2,1)}, u32[]{:S(2)}, u32[]{:S(2)}) %collective-permute-start.6) | collective-permute-done | bytes 550944 | tf_op jit(solution)/shard_map/ppermute | solution.py:41
  76.2 1.4 convolution_convert_fusion
  77.9 1.5 convolution_convert_fusion.1
  79.6 1.6 convolution_convert_fusion.3
  81.2 1.4 convolution_convert_fusion.2
  83.3 1.1 pad_maximum_fusion.1
  84.4 5.4 %all-to-all-start.1 = ((bf16[16,64,288]{2,1,0:T(8,128)(2,1)}), bf16[16,64,288]{2,1,0:T(8,128)(2,1)S(1)}, u32[]{:S(2)}, u32[]{:S(2)}) async-start(bf16[16,64,288]{2,1,0:T(8,128)(2,1)} %bitcast.11), calls=%async_computation.1 | async-start | bytes 1572864 | tf_op jit(solution)/shard_map/all_to_all | solution.py:45
  89.8 0.9 constant_dynamic-update-slice_fusion.7
  90.6 0.9 constant_dynamic-update-slice_fusion.6
  92.2 2.6 %collective-permute-start.18 = (bf16[256,1152]{1,0:T(8,128)(2,1)}, bf16[256,1152]{1,0:T(8,128)(2,1)S(1)}, u32[]{:S(2)}, u32[]{:S(2)}) collective-permute-start(bf16[256,1152]{1,0:T(8,128)(2,1)} %collective-permute-done.16), channel_id=1, source_target_pairs={{0,7},{1,0},{2,1},{3,2},{4,3},{5,4},{6,5},{7,6},{8,15},{9,8},{10,9... | collective-permute-start | bytes 1769480 | tf_op jit(solution)/shard_map/ppermute | solution.py:41
  94.8 1.9 constant_dynamic-update-slice_fusion.5
  96.7 5.0 %all-to-all-done.1 = bf16[16,64,288]{2,1,0:T(8,128)(2,1)S(1)} async-done(((bf16[16,64,288]{2,1,0:T(8,128)(2,1)}), bf16[16,64,288]{2,1,0:T(8,128)(2,1)S(1)}, u32[]{:S(2)}, u32[]{:S(2)}) %all-to-all-start.1) | async-done | bytes 589856 | tf_op jit(solution)/shard_map/all_to_all | solution.py:45
  102.9 1.3 collective-permute-start.7
  104.2 1.9 constant_dynamic-update-slice_fusion.4
  106.2 3.2 %collective-permute-start.8 = (bf16[64,1152]{1,0:T(8,128)(2,1)S(1)}, bf16[64,1152]{1,0:T(8,128)(2,1)S(1)}, u32[]{:S(2)}, u32[]{:S(2)}) collective-permute-start(bf16[64,1152]{1,0:T(8,128)(2,1)S(1)} %fusion.22), channel_id=1, source_target_pairs={{0,128},{64,192},{128,0},{192,64},{1,129},{65,193},{129,1},{193,65... | collective-permute-start | bytes 442376 | tf_op jit(solution)/shard_map/ppermute | solution.py:41
  109.9 3.2 %collective-permute-done.8 = bf16[64,1152]{1,0:T(8,128)(2,1)S(1)} collective-permute-done((bf16[64,1152]{1,0:T(8,128)(2,1)S(1)}, bf16[64,1152]{1,0:T(8,128)(2,1)S(1)}, u32[]{:S(2)}, u32[]{:S(2)}) %collective-permute-start.8) | collective-permute-done | bytes 147488 | tf_op jit(solution)/shard_map/ppermute | solution.py:41
  113.1 1.5 collective-permute-done.9
  115.5 2.6 %collective-permute-start.20 = (bf16[128,1152]{1,0:T(8,128)(2,1)S(1)}, bf16[128,1152]{1,0:T(8,128)(2,1)S(1)}, u32[]{:S(2)}, u32[]{:S(2)}) collective-permute-start(bf16[128,1152]{1,0:T(8,128)(2,1)S(1)} %slice.43), channel_id=1, source_target_pairs={{0,7},{1,0},{2,1},{3,2},{4,3},{5,4},{6,5},{7,6},{8,15},{9,8},{10,9... | collective-permute-start | bytes 884744 | tf_op jit(solution)/shard_map/ppermute | solution.py:41
  118.1 0.9 constant_dynamic-update-slice_fusion.3
  119.0 0.9 constant_dynamic-update-slice_fusion.2
  119.9 2.9 %collective-permute-done.19 = bf16[128,1152]{1,0:T(8,128)(2,1)S(1)} collective-permute-done((bf16[128,1152]{1,0:T(8,128)(2,1)S(1)}, bf16[128,1152]{1,0:T(8,128)(2,1)S(1)}, u32[]{:S(2)}, u32[]{:S(2)}) %collective-permute-start.19) | collective-permute-done | bytes 294944 | tf_op jit(solution)/shard_map/ppermute | solution.py:41
  124.2 7.9 %shard_map.111 = (f32[256,1152]{1,0:T(8,128)}, f32[1,512]{1,0:T(1,128)}) custom-call(f32[2]{0:T(128)} %pad_maximum_fusion.3.scalars, bf16[256,1152]{1,0:T(8,128)(2,1)} %copy-done.1, bf16[2048,1152]{1,0:T(8,128)(2,1)} %constant_dynamic-update-slice_fusion.texts), custom_call_target="tpu_custom_call" | custom-call | flops 2415919104 | bytes 4718592 | tf_op jit(solution)/shard_map/pallas_call | solution.py:133
  132.5 8.5 %shard_map.112 = (f32[256,1152]{1,0:T(8,128)}, bf16[256,1152]{1,0:T(8,128)(2,1)}, f32[1,512]{1,0:T(1,128)}) custom-call(f32[2]{0:T(128)} %pad_maximum_fusion.3.scalars, bf16[256,1152]{1,0:T(8,128)(2,1)} %copy-done.1, bf16[2048,1152]{1,0:T(8,128)(2,1)} %collective-permute-done.21.texts, f32[256,1152]{1,0:T(8,128)} %get-tuple-element.25.refs_0_), custom_call_target="tpu_custom_call" | custom-call | flops 2415919104 | bytes 4718592 | tf_op jit(solution)/shard_map/pallas_call | solution.py:133
  141.0 1.1 fusion.24
  142.7 2.9 %collective-permute-start.23 = (bf16[64,1152]{1,0:T(8,128)(2,1)S(1)}, bf16[64,1152]{1,0:T(8,128)(2,1)S(1)}, u32[]{:S(2)}, u32[]{:S(2)}) collective-permute-start(bf16[64,1152]{1,0:T(8,128)(2,1)S(1)} %get-tuple-element.42), channel_id=1, source_target_pairs={{0,128},{64,192},{128,0},{192,64},{1,129},{65,193},{129,1},{193,65... | collective-permute-start | bytes 442376 | tf_op jit(solution)/shard_map/ppermute | solution.py:41
  145.7 2.1 collective-permute-start.22
  148.0 2.9 %collective-permute-done.23 = bf16[64,1152]{1,0:T(8,128)(2,1)S(1)} collective-permute-done((bf16[64,1152]{1,0:T(8,128)(2,1)S(1)}, bf16[64,1152]{1,0:T(8,128)(2,1)S(1)}, u32[]{:S(2)}, u32[]{:S(2)}) %collective-permute-start.23) | collective-permute-done | bytes 147488 | tf_op jit(solution)/shard_map/ppermute | solution.py:41
  150.9 2.0 collective-permute-done.22
  153.0 1.2 multiply_reduce_fusion
  154.2 1.1 divide_convert_fusion
  155.5 1.0 broadcast_in_dim.12
  156.5 7.1 %all-to-all-start.2 = ((bf16[16,64,288]{2,1,0:T(8,128)(2,1)}), bf16[16,64,288]{2,1,0:T(8,128)(2,1)S(1)}, u32[]{:S(2)}, u32[]{:S(2)}) async-start(bf16[16,64,288]{2,1,0:T(8,128)(2,1)} %bitcast.15), calls=%async_computation.2 | async-start | bytes 1572864 | tf_op jit(solution)/shard_map/all_to_all | solution.py:45
  163.6 12.2 %all-to-all-done.2 = bf16[16,64,288]{2,1,0:T(8,128)(2,1)S(1)} async-done(((bf16[16,64,288]{2,1,0:T(8,128)(2,1)}), bf16[16,64,288]{2,1,0:T(8,128)(2,1)S(1)}, u32[]{:S(2)}, u32[]{:S(2)}) %all-to-all-start.2) | async-done | bytes 589856 | tf_op jit(solution)/shard_map/all_to_all | solution.py:45
  175.9 1.5 fusion.5
  177.5 1.5 fusion.7
  179.0 1.5 fusion.9
  181.3 2.2 collective-permute-done.25
  184.7 4.3 %all-to-all-start.3 = ((bf16[8,36,538]{2,1,0:T(8,128)(2,1)}), bf16[8,36,538]{2,1,0:T(8,128)(2,1)S(1)}, u32[]{:S(2)}, u32[]{:S(2)}) async-start(bf16[8,36,538]{2,1,0:T(8,128)(2,1)} %reshape.90), calls=%async_computation.3 | async-start | bytes 819200 | tf_op jit(solution)/shard_map/all_to_all | solution.py:45
  189.6 14.7 %all-to-all-done.3 = bf16[8,36,538]{2,1,0:T(8,128)(2,1)S(1)} async-done(((bf16[8,36,538]{2,1,0:T(8,128)(2,1)}), bf16[8,36,538]{2,1,0:T(8,128)(2,1)S(1)}, u32[]{:S(2)}, u32[]{:S(2)}) %all-to-all-start.3) | async-done | bytes 309920 | tf_op jit(solution)/shard_map/all_to_all | solution.py:45
  205.3 8.8 %all_to_all.35 = f32[8,1,37]{2,1,0:T(1,128)S(1)} all-to-all(f32[8,1,37]{2,1,0:T(1,128)S(1)} %broadcast_in_dim.13), channel_id=1, replica_groups=mesh['x'=4,'k'=2,'y'=4,'z'=8] {'x','k'}, dimensions={0} | all-to-all | bytes 2368 | tf_op jit(solution)/shard_map/all_to_all | solution.py:45
  215.6 13.8 %all_to_all.36 = f32[32,1,1077]{2,1,0:T(1,128)S(1)} all-to-all(f32[32,1,1077]{2,1,0:T(1,128)S(1)} %broadcast_in_dim.14), channel_id=1, replica_groups=mesh['x'=4,'k'=2,'y'=4,'z'=8] {'y','z'}, dimensions={0} | all-to-all | bytes 275712 | tf_op jit(solution)/shard_map/all_to_all | solution.py:45
  230.1 1.2 broadcast_in_dim_broadcast_in_dim.3
  231.4 4.7 %all-to-all-start.6 = ((f32[8,1,128]{2,1,0:T(1,128)}), f32[8,1,128]{2,1,0:T(1,128)S(1)}, u32[]{:S(2)}, u32[]{:S(2)}) async-start(f32[8,1,128]{2,1,0:T(1,128)} %broadcast_in_dim_broadcast_in_dim.3), calls=%async_computation.6 | async-start | bytes 8192 | tf_op jit(solution)/shard_map/all_to_all | solution.py:45
  237.3 2.6 %all-to-all-done.6 = f32[8,1,128]{2,1,0:T(1,128)S(1)} async-done(((f32[8,1,128]{2,1,0:T(1,128)}), f32[8,1,128]{2,1,0:T(1,128)S(1)}, u32[]{:S(2)}, u32[]{:S(2)}) %all-to-all-start.6) | async-done | bytes 4128 | tf_op jit(solution)/shard_map/all_to_all | solution.py:45
  (114 shorter events, 19.0 us)
Async XLA Ops:
  2.7 29.6 %collective-permute-start.10 = (bf16[64,1152]{1,0:T(8,128)(2,1)S(1)}, bf16[64,1152]{1,0:T(8,128)(2,1)S(1)}, u32[]{:S(2)}, u32[]{:S(2)}) collective-permute-start(bf16[64,1152]{1,0:T(8,128)(2,1)S(1)} %fusion.3), channel_id=1, source_target_pairs={{0,40},{8,48},{16,56},{24,32},{32,8},{40,16},{48,24},{56,0},{1,41}... | collective-permute-start | bytes 442376 | tf_op jit(solution)/shard_map/ppermute | solution.py:41
  3.8 28.5 %collective-permute-start.11 = (bf16[64,1152]{1,0:T(8,128)(2,1)S(1)}, bf16[64,1152]{1,0:T(8,128)(2,1)S(1)}, u32[]{:S(2)}, u32[]{:S(2)}) collective-permute-start(bf16[64,1152]{1,0:T(8,128)(2,1)S(1)} %fusion.3), channel_id=1, source_target_pairs={{0,48},{8,56},{16,32},{24,40},{32,16},{40,24},{48,0},{56,8},{1,49}... | collective-permute-start | bytes 442376 | tf_op jit(solution)/shard_map/ppermute | solution.py:41
  7.0 25.4 %collective-permute-start.12 = (bf16[64,1152]{1,0:T(8,128)(2,1)S(1)}, bf16[64,1152]{1,0:T(8,128)(2,1)S(1)}, u32[]{:S(2)}, u32[]{:S(2)}) collective-permute-start(bf16[64,1152]{1,0:T(8,128)(2,1)S(1)} %fusion.3), channel_id=1, source_target_pairs={{0,56},{8,32},{16,40},{24,48},{32,24},{40,0},{48,8},{56,16},{1,57}... | collective-permute-start | bytes 442376 | tf_op jit(solution)/shard_map/ppermute | solution.py:41
  10.5 6.8 %collective-permute-start = (bf16[1,64,1076]{2,1,0:T(8,128)(2,1)S(1)}, bf16[1,64,1076]{2,1,0:T(8,128)(2,1)S(1)}, u32[]{:S(2)}, u32[]{:S(2)}) collective-permute-start(bf16[1,64,1076]{2,1,0:T(8,128)(2,1)S(1)} %bitcast.79), channel_id=1, source_target_pairs={{0,64},{64,128},{128,192},{192,0},{1,65},{65,129},{129,193},{193,1... | collective-permute-start | bytes 413192 | tf_op jit(solution)/shard_map/ppermute | solution.py:41
  12.1 1.4 copy-start.6
  12.1 7.8 %collective-permute-start.1 = (bf16[1,64,1076]{2,1,0:T(8,128)(2,1)S(1)}, bf16[1,64,1076]{2,1,0:T(8,128)(2,1)S(1)}, u32[]{:S(2)}, u32[]{:S(2)}) collective-permute-start(bf16[1,64,1076]{2,1,0:T(8,128)(2,1)S(1)} %bitcast.78), channel_id=1, source_target_pairs={{0,128},{64,192},{128,0},{192,64},{1,129},{65,193},{129,1},{193,65... | collective-permute-start | bytes 413192 | tf_op jit(solution)/shard_map/ppermute | solution.py:41
  17.3 5.7 %collective-permute-start.2 = (bf16[1,64,1076]{2,1,0:T(8,128)(2,1)S(1)}, bf16[1,64,1076]{2,1,0:T(8,128)(2,1)S(1)}, u32[]{:S(2)}, u32[]{:S(2)}) collective-permute-start(bf16[1,64,1076]{2,1,0:T(8,128)(2,1)S(1)} %bitcast.80), channel_id=1, source_target_pairs={{0,192},{64,0},{128,64},{192,128},{1,193},{65,1},{129,65},{193,129... | collective-permute-start | bytes 413192 | tf_op jit(solution)/shard_map/ppermute | solution.py:41
  23.8 23.8 %all-to-all-start = ((bf16[8,36,538]{2,1,0:T(8,128)(2,1)}), bf16[8,36,538]{2,1,0:T(8,128)(2,1)S(1)}, u32[]{:S(2)}, u32[]{:S(2)}) async-start(bf16[8,36,538]{2,1,0:T(8,128)(2,1)} %broadcast_in_dim.11), calls=%async_computation | async-start | bytes 819200 | tf_op jit(solution)/shard_map/all_to_all | solution.py:45
  32.4 24.1 %collective-permute-start.13 = (bf16[256,1152]{1,0:T(8,128)(2,1)S(1)}, bf16[256,1152]{1,0:T(8,128)(2,1)S(1)}, u32[]{:S(2)}, u32[]{:S(2)}) collective-permute-start(bf16[256,1152]{1,0:T(8,128)(2,1)S(1)} %constant_dynamic-update-slice_fusion.9), channel_id=1, source_target_pairs={{0,1},{1,2},{2,3},{3,4},{4,5},{5,6},{6,7},{7,0},{8,9},{9,10},{10,1... | collective-permute-start | bytes 1769480 | tf_op jit(solution)/shard_map/ppermute | solution.py:41
  34.5 22.0 %collective-permute-start.14 = (bf16[256,1152]{1,0:T(8,128)(2,1)S(1)}, bf16[256,1152]{1,0:T(8,128)(2,1)S(1)}, u32[]{:S(2)}, u32[]{:S(2)}) collective-permute-start(bf16[256,1152]{1,0:T(8,128)(2,1)S(1)} %constant_dynamic-update-slice_fusion.9), channel_id=1, source_target_pairs={{0,7},{1,0},{2,1},{3,2},{4,3},{5,4},{6,5},{7,6},{8,15},{9,8},{10,9... | collective-permute-start | bytes 1769480 | tf_op jit(solution)/shard_map/ppermute | solution.py:41
  47.7 9.1 %collective-permute-start.3 = (bf16[288,538]{1,0:T(8,128)(2,1)S(1)}, bf16[288,538]{1,0:T(8,128)(2,1)}, u32[]{:S(2)}, u32[]{:S(2)}) collective-permute-start(bf16[288,538]{1,0:T(8,128)(2,1)S(1)} %reshape.81), channel_id=1, source_target_pairs={{0,32},{32,0},{1,33},{33,1},{2,34},{34,2},{3,35},{35,3},{4,36},{36... | collective-permute-start | bytes 929672 | tf_op jit(solution)/shard_map/ppermute | solution.py:41
  48.0 28.2 %collective-permute-start.6 = (bf16[256,1076]{0,1:T(8,128)(2,1)S(1)}, bf16[256,1076]{0,1:T(8,128)(2,1)}, u32[]{:S(2)}, u32[]{:S(2)}) collective-permute-start(bf16[256,1076]{0,1:T(8,128)(2,1)S(1)} %copy.56), channel_id=1, source_target_pairs={{0,8},{8,16},{16,24},{24,0},{1,9},{9,17},{17,25},{25,1},{2,10},{10... | collective-permute-start | bytes 1652744 | tf_op jit(solution)/shard_map/ppermute | solution.py:41
  48.8 29.0 %collective-permute-start.5 = (bf16[256,1076]{0,1:T(8,128)(2,1)S(1)}, bf16[256,1076]{0,1:T(8,128)(2,1)}, u32[]{:S(2)}, u32[]{:S(2)}) collective-permute-start(bf16[256,1076]{0,1:T(8,128)(2,1)S(1)} %copy.56), channel_id=1, source_target_pairs={{0,16},{8,24},{16,0},{24,8},{1,17},{9,25},{17,1},{25,9},{2,18},{10... | collective-permute-start | bytes 1652744 | tf_op jit(solution)/shard_map/ppermute | solution.py:41
  56.5 24.6 %collective-permute-start.4 = (bf16[256,1076]{0,1:T(8,128)(2,1)S(1)}, bf16[256,1076]{0,1:T(8,128)(2,1)}, u32[]{:S(2)}, u32[]{:S(2)}) collective-permute-start(bf16[256,1076]{0,1:T(8,128)(2,1)S(1)} %copy.56), channel_id=1, source_target_pairs={{0,24},{8,0},{16,8},{24,16},{1,25},{9,1},{17,9},{25,17},{2,26},{10... | collective-permute-start | bytes 1652744 | tf_op jit(solution)/shard_map/ppermute | solution.py:41
  56.5 35.0 %collective-permute-start.15 = (bf16[256,1152]{1,0:T(8,128)(2,1)S(1)}, bf16[256,1152]{1,0:T(8,128)(2,1)}, u32[]{:S(2)}, u32[]{:S(2)}) collective-permute-start(bf16[256,1152]{1,0:T(8,128)(2,1)S(1)} %collective-permute-done.13), channel_id=1, source_target_pairs={{0,1},{1,2},{2,3},{3,4},{4,5},{5,6},{6,7},{7,0},{8,9},{9,10},{10,1... | collective-permute-start | bytes 1769480 | tf_op jit(solution)/shard_map/ppermute | solution.py:41
  56.8 34.7 %collective-permute-start.16 = (bf16[256,1152]{1,0:T(8,128)(2,1)S(1)}, bf16[256,1152]{1,0:T(8,128)(2,1)}, u32[]{:S(2)}, u32[]{:S(2)}) collective-permute-start(bf16[256,1152]{1,0:T(8,128)(2,1)S(1)} %collective-permute-done.14), channel_id=1, source_target_pairs={{0,7},{1,0},{2,1},{3,2},{4,3},{5,4},{6,5},{7,6},{8,15},{9,8},{10,9... | collective-permute-start | bytes 1769480 | tf_op jit(solution)/shard_map/ppermute | solution.py:41
  60.8 15.4 %copy-start.4 = (bf16[288,538]{1,0:T(8,128)(2,1)}, bf16[288,538]{1,0:T(8,128)(2,1)S(1)}, u32[]{:S(2)}) copy-start(bf16[288,538]{1,0:T(8,128)(2,1)S(1)} %get-tuple-element.39) | copy-start | bytes 929668
  60.9 17.0 %copy-start.2 = (bf16[288,538]{1,0:T(8,128)(2,1)}, bf16[288,538]{1,0:T(8,128)(2,1)S(1)}, u32[]{:S(2)}) copy-start(bf16[288,538]{1,0:T(8,128)(2,1)S(1)} %get-tuple-element.38) | copy-start | bytes 929668
  79.4 1.8 copy-start.3
  79.6 1.6 copy-start.5
  84.4 17.4 %all-to-all-start.1 = ((bf16[16,64,288]{2,1,0:T(8,128)(2,1)}), bf16[16,64,288]{2,1,0:T(8,128)(2,1)S(1)}, u32[]{:S(2)}, u32[]{:S(2)}) async-start(bf16[16,64,288]{2,1,0:T(8,128)(2,1)} %bitcast.11), calls=%async_computation.1 | async-start | bytes 1572864 | tf_op jit(solution)/shard_map/all_to_all | solution.py:45
  91.5 23.1 %collective-permute-start.17 = (bf16[256,1152]{1,0:T(8,128)(2,1)}, bf16[256,1152]{1,0:T(8,128)(2,1)S(1)}, u32[]{:S(2)}, u32[]{:S(2)}) collective-permute-start(bf16[256,1152]{1,0:T(8,128)(2,1)} %collective-permute-done.15), channel_id=1, source_target_pairs={{0,1},{1,2},{2,3},{3,4},{4,5},{5,6},{6,7},{7,0},{8,9},{9,10},{10,1... | collective-permute-start | bytes 1769480 | tf_op jit(solution)/shard_map/ppermute | solution.py:41
  92.2 22.5 %collective-permute-start.18 = (bf16[256,1152]{1,0:T(8,128)(2,1)}, bf16[256,1152]{1,0:T(8,128)(2,1)S(1)}, u32[]{:S(2)}, u32[]{:S(2)}) collective-permute-start(bf16[256,1152]{1,0:T(8,128)(2,1)} %collective-permute-done.16), channel_id=1, source_target_pairs={{0,7},{1,0},{2,1},{3,2},{4,3},{5,4},{6,5},{7,6},{8,15},{9,8},{10,9... | collective-permute-start | bytes 1769480 | tf_op jit(solution)/shard_map/ppermute | solution.py:41
  101.7 0.9 copy-start
  102.9 6.9 %collective-permute-start.7 = (bf16[64,1152]{1,0:T(8,128)(2,1)S(1)}, bf16[64,1152]{1,0:T(8,128)(2,1)S(1)}, u32[]{:S(2)}, u32[]{:S(2)}) collective-permute-start(bf16[64,1152]{1,0:T(8,128)(2,1)S(1)} %fusion.22), channel_id=1, source_target_pairs={{0,64},{64,128},{128,192},{192,0},{1,65},{65,129},{129,193},{193,1... | collective-permute-start | bytes 442376 | tf_op jit(solution)/shard_map/ppermute | solution.py:41
  106.2 6.9 %collective-permute-start.8 = (bf16[64,1152]{1,0:T(8,128)(2,1)S(1)}, bf16[64,1152]{1,0:T(8,128)(2,1)S(1)}, u32[]{:S(2)}, u32[]{:S(2)}) collective-permute-start(bf16[64,1152]{1,0:T(8,128)(2,1)S(1)} %fusion.22), channel_id=1, source_target_pairs={{0,128},{64,192},{128,0},{192,64},{1,129},{65,193},{129,1},{193,65... | collective-permute-start | bytes 442376 | tf_op jit(solution)/shard_map/ppermute | solution.py:41
  109.4 5.3 %collective-permute-start.9 = (bf16[64,1152]{1,0:T(8,128)(2,1)S(1)}, bf16[64,1152]{1,0:T(8,128)(2,1)S(1)}, u32[]{:S(2)}, u32[]{:S(2)}) collective-permute-start(bf16[64,1152]{1,0:T(8,128)(2,1)S(1)} %fusion.22), channel_id=1, source_target_pairs={{0,192},{64,0},{128,64},{192,128},{1,193},{65,1},{129,65},{193,129... | collective-permute-start | bytes 442376 | tf_op jit(solution)/shard_map/ppermute | solution.py:41
  114.7 5.2 %copy-start.1 = (bf16[256,1152]{1,0:T(8,128)(2,1)}, bf16[256,1152]{1,0:T(8,128)(2,1)S(1)}, u32[]{:S(2)}) copy-start(bf16[256,1152]{1,0:T(8,128)(2,1)S(1)} %constant_dynamic-update-slice_fusion.12.images) | copy-start | bytes 1769476
  114.7 8.0 %collective-permute-start.19 = (bf16[128,1152]{1,0:T(8,128)(2,1)S(1)}, bf16[128,1152]{1,0:T(8,128)(2,1)S(1)}, u32[]{:S(2)}, u32[]{:S(2)}) collective-permute-start(bf16[128,1152]{1,0:T(8,128)(2,1)S(1)} %slice.42), channel_id=1, source_target_pairs={{0,1},{1,2},{2,3},{3,4},{4,5},{5,6},{6,7},{7,0},{8,9},{9,10},{10,1... | collective-permute-start | bytes 884744 | tf_op jit(solution)/shard_map/ppermute | solution.py:41
  115.5 7.2 %collective-permute-start.20 = (bf16[128,1152]{1,0:T(8,128)(2,1)S(1)}, bf16[128,1152]{1,0:T(8,128)(2,1)S(1)}, u32[]{:S(2)}, u32[]{:S(2)}) collective-permute-start(bf16[128,1152]{1,0:T(8,128)(2,1)S(1)} %slice.43), channel_id=1, source_target_pairs={{0,7},{1,0},{2,1},{3,2},{4,3},{5,4},{6,5},{7,6},{8,15},{9,8},{10,9... | collective-permute-start | bytes 884744 | tf_op jit(solution)/shard_map/ppermute | solution.py:41
  124.2 8.3 %collective-permute-start.21 = (bf16[2048,1152]{1,0:T(8,128)(2,1)}, bf16[2048,1152]{1,0:T(8,128)(2,1)}, u32[]{:S(2)}, u32[]{:S(2)}) collective-permute-start(bf16[2048,1152]{1,0:T(8,128)(2,1)} %constant_dynamic-update-slice_fusion.texts), channel_id=1, source_target_pairs={{0,32},{32,0},{1,33},{33,1},{2,34},{34,2},{3,35},{35,3},{4,36},{36... | collective-permute-start | bytes 14155784 | tf_op jit(solution)/shard_map/ppermute | solution.py:41
  142.1 6.0 %collective-permute-start.24 = (bf16[64,1152]{1,0:T(8,128)(2,1)S(1)}, bf16[64,1152]{1,0:T(8,128)(2,1)S(1)}, u32[]{:S(2)}, u32[]{:S(2)}) collective-permute-start(bf16[64,1152]{1,0:T(8,128)(2,1)S(1)} %get-tuple-element.41), channel_id=1, source_target_pairs={{0,64},{64,128},{128,192},{192,0},{1,65},{65,129},{129,193},{193,1... | collective-permute-start | bytes 442376 | tf_op jit(solution)/shard_map/ppermute | solution.py:41
  142.7 8.2 %collective-permute-start.23 = (bf16[64,1152]{1,0:T(8,128)(2,1)S(1)}, bf16[64,1152]{1,0:T(8,128)(2,1)S(1)}, u32[]{:S(2)}, u32[]{:S(2)}) collective-permute-start(bf16[64,1152]{1,0:T(8,128)(2,1)S(1)} %get-tuple-element.42), channel_id=1, source_target_pairs={{0,128},{64,192},{128,0},{192,64},{1,129},{65,193},{129,1},{193,65... | collective-permute-start | bytes 442376 | tf_op jit(solution)/shard_map/ppermute | solution.py:41
  145.7 7.3 %collective-permute-start.22 = (bf16[64,1152]{1,0:T(8,128)(2,1)S(1)}, bf16[64,1152]{1,0:T(8,128)(2,1)S(1)}, u32[]{:S(2)}, u32[]{:S(2)}) collective-permute-start(bf16[64,1152]{1,0:T(8,128)(2,1)S(1)} %get-tuple-element.40), channel_id=1, source_target_pairs={{0,192},{64,0},{128,64},{192,128},{1,193},{65,1},{129,65},{193,129... | collective-permute-start | bytes 442376 | tf_op jit(solution)/shard_map/ppermute | solution.py:41
  156.5 19.3 %all-to-all-start.2 = ((bf16[16,64,288]{2,1,0:T(8,128)(2,1)}), bf16[16,64,288]{2,1,0:T(8,128)(2,1)S(1)}, u32[]{:S(2)}, u32[]{:S(2)}) async-start(bf16[16,64,288]{2,1,0:T(8,128)(2,1)} %bitcast.15), calls=%async_computation.2 | async-start | bytes 1572864 | tf_op jit(solution)/shard_map/all_to_all | solution.py:45
  181.2 2.3 collective-permute-start.25
  183.8 5.2 %copy-start.10 = (f32[1,512]{1,0:T(1,128)S(1)}, f32[1,512]{1,0:T(1,128)}, u32[]{:S(2)}) copy-start(f32[1,512]{1,0:T(1,128)} %get-tuple-element.28) | copy-start | bytes 6148
  183.8 5.2 %copy-start.11 = (f32[1,512]{1,0:T(1,128)S(1)}, f32[1,512]{1,0:T(1,128)}, u32[]{:S(2)}) copy-start(f32[1,512]{1,0:T(1,128)} %get-tuple-element.29) | copy-start | bytes 6148
  183.8 30.8 %copy-start.12 = (f32[36]{0:T(128)S(1)}, f32[36]{0:T(128)}, u32[]{:S(2)}) copy-start(f32[36]{0:T(128)} %param.12) | copy-start | bytes 436
  183.8 45.6 %copy-start.8 = (f32[538]{0:T(1024)S(1)}, f32[538]{0:T(1024)}, u32[]{:S(2)}) copy-start(f32[538]{0:T(1024)} %param.13) | copy-start | bytes 6460
  184.7 19.7 %all-to-all-start.3 = ((bf16[8,36,538]{2,1,0:T(8,128)(2,1)}), bf16[8,36,538]{2,1,0:T(8,128)(2,1)S(1)}, u32[]{:S(2)}, u32[]{:S(2)}) async-start(bf16[8,36,538]{2,1,0:T(8,128)(2,1)} %reshape.90), calls=%async_computation.3 | async-start | bytes 819200 | tf_op jit(solution)/shard_map/all_to_all | solution.py:45
  214.7 26.0 %copy-start.9 = (f32[36]{0:T(128)}, f32[36]{0:T(128)S(1)}, u32[]{:S(2)}) copy-start(f32[36]{0:T(128)S(1)} %multiply_add_fusion) | copy-start | bytes 436
  230.1 10.6 %copy-start.7 = (f32[538]{0:T(1024)}, f32[538]{0:T(1024)S(1)}, u32[]{:S(2)}) copy-start(f32[538]{0:T(1024)S(1)} %get-tuple-element.33) | copy-start | bytes 6460
  231.4 8.5 %all-to-all-start.6 = ((f32[8,1,128]{2,1,0:T(1,128)}), f32[8,1,128]{2,1,0:T(1,128)S(1)}, u32[]{:S(2)}, u32[]{:S(2)}) async-start(f32[8,1,128]{2,1,0:T(1,128)} %broadcast_in_dim_broadcast_in_dim.3), calls=%async_computation.6 | async-start | bytes 8192 | tf_op jit(solution)/shard_map/all_to_all | solution.py:45

commit v5 on v4

--- a/solution.py
+++ b/solution.py
@@ -170,13 +170,12 @@
     texts_y = joined([text_units] + [shift(text_units, k=1, y=s) for s in (1, 2, 3)])
     up, down = ring_step(texts_y, texts_y, "z")
     ring_pieces = [texts_y, up, down]
-    up, down = ring_step(up, down, "z")
-    ring_pieces += [up, down]
-
     scalars = jnp.stack([jnp.exp(log_scale), bias])
     weight_own = everywhere(after(weight.astype(BF16), hidden_x), "z")
     weight_own = after(weight_own.reshape(quarter, slice_ff), scalars)
-    weight_other = shift(weight_own, k=1)
+    weight_other = after(shift(weight_own, k=1), up, down)
+    up, down = ring_step(up, down, "z")
+    ring_pieces += [up, down]
     weight_x = jnp.concatenate(
         [
             jnp.where(first_core, weight_own, weight_other),
@@ -184,24 +183,15 @@
         ],
         axis=1,
     )
-    partial = jnp.stack(
-        [
-            lax.dot_general(
-                piece, weight_x, (((1,), (1,)), ((), ())), preferred_element_type=F32
-            )
-            .astype(BF16)
-            .reshape(4, tokens, quarter)
-            for piece in hid_y
-        ]
-    )
     y_place = lax.axis_index("y")
-    partial = jnp.stack(
-        [
-            lax.dynamic_index_in_dim(partial, (c - y_place) & 3, 0, keepdims=False)
-            for c in range(4)
-        ],
-        axis=1,
-    )
+    partial = jnp.zeros((4, 4, tokens, quarter), BF16)
+    for s, piece in enumerate(hid_y):
+        product = lax.dot_general(
+            piece, weight_x, (((1,), (1,)), ((), ())), preferred_element_type=F32
+        ).astype(BF16)
+        partial = lax.dynamic_update_slice_in_dim(
+            partial, product.reshape(4, 1, tokens, quarter), (y_place + s) & 3, 1
+        )
     up, down = ring_step(*after((up, down), partial), "z")
     ring_pieces += [up, down]
     arrived = exchange(partial.reshape(16, tokens, quarter), ("x", "y"))

time: 245 us -> 245 us (level)
  blocking collectives: 22.6 us -> 40.2 us
  waiting for transfers between devices: 89.3 us -> 72.6 us
  local copies, waits for them, and re-layouts: 22 us -> 25.6 us
    all_to_all x2 -> x3, blocking collectives: 22.6 us -> 40.2 us  [exchange(): return lax.all_to_all(pieces, axes, split_axis=0, concat_axis=0, tiled=True)]
    all_to_all x5 -> x4, waiting for transfers between devices: 44.3 us -> 31.8 us  [exchange(): return lax.all_to_all(pieces, axes, split_axis=0, concat_axis=0, tiled=True)]
    ppermute x26, waiting for transfers between devices: 45 us -> 40.7 us  [shift(): return lax.ppermute(value, names, pairs)]
    all_to_all x5 -> x4, starting transfers between devices: 30 us -> 26.4 us  [exchange(): return lax.all_to_all(pieces, axes, split_axis=0, concat_axis=0, tiled=True)]
    dynamic_update_slice x0 -> x4, local copies, waits for them, and re-layouts: none -> 2.89 us  [step(): lax.dynamic_update_slice_in_dim(partial, product.reshape(4, 1, tokens, qu...]
    unnamed x37 -> x35, local copies, waits for them, and re-layouts: 9.39 us -> 10.1 us
  transfers between devices with their start and end apart: 31 -> 30, of which waited for: 18 -> 17; matrix products, arithmetic and copies ran while one was open for 10% -> 11% of each run, Pallas kernels for 3% -> 3%
where the time goes in v5:
time: 245 us; the launch traced here: 243 us
  waiting for transfers between devices  72.6 us (30%)
  starting transfers between devices  63.3 us (26%)
  blocking collectives  40.2 us (16%)
  local copies, waits for them, and re-layouts  25.6 us (10%)
  Pallas kernels  16.3 us (7%)
  other arithmetic  10.1 us (4%)
  matrix products  10.1 us (4%)
  between operations  4.35 us (2%)
    ppermute x26, waiting for transfers between devices, shift(): return lax.ppermute(value, names, pairs)  40.7 us
    all_to_all x3, blocking collectives, exchange(): return lax.all_to_all(pieces, axes, split_axis=0, concat_axis=0, tiled=True)  40.2 us
    ppermute x26, starting transfers between devices, shift(): return lax.ppermute(value, names, pairs)  36.9 us
    all_to_all x4, waiting for transfers between devices, exchange(): return lax.all_to_all(pieces, axes, split_axis=0, concat_axis=0, tiled=True)  31.8 us
    all_to_all x4, starting transfers between devices, exchange(): return lax.all_to_all(pieces, axes, split_axis=0, concat_axis=0, tiled=True)  26.4 us
    pallas_call x2, Pallas kernels, pair_tiles(): pl.pallas_call(functools.partial(pair_kernel, first=first, tokens=tokens,...  16.3 us
    unnamed x35, local copies, waits for them, and re-layouts  10.1 us
    dot_general x4, matrix products, step(): lax.dot_general(piece, weight_x, (((1,), (1,)), ((), ())), preferred_elem...  5.12 us
  transfers between devices with their start and end apart: 30, of which 17 were waited for; matrix products, arithmetic and copies ran while one was open for 11% of the time, Pallas kernels for 3%

profile of v5, /device:TPU:2, one launch (start us, length us, event | category | flops | bytes accessed | tf_op | source)
XLA Modules:
  0.0 242.6 jit_solution(1343675982630824044)
XLA Ops:
  0.6 1.0 fusion.2
  1.7 1.0 fusion.3
  2.7 1.1 collective-permute-start.4
  3.8 3.2 %collective-permute-start.5 = (bf16[64,1152]{1,0:T(8,128)(2,1)S(1)}, bf16[64,1152]{1,0:T(8,128)(2,1)S(1)}, u32[]{:S(2)}, u32[]{:S(2)}) collective-permute-start(bf16[64,1152]{1,0:T(8,128)(2,1)S(1)} %fusion.3), channel_id=1, source_target_pairs={{0,48},{8,56},{16,32},{24,40},{32,16},{40,24},{48,0},{56,8},{1,49}... | collective-permute-start | bytes 442376 | tf_op jit(solution)/shard_map/ppermute | solution.py:41
  7.0 0.8 collective-permute-start.6
  7.8 1.5 reshape.87
  9.3 1.2 constant_dynamic-slice_fusion
  10.5 1.6 collective-permute-start
  12.1 1.2 collective-permute-start.1
  13.5 3.8 %collective-permute-done = bf16[1,64,1076]{2,1,0:T(8,128)(2,1)S(1)} collective-permute-done((bf16[1,64,1076]{2,1,0:T(8,128)(2,1)S(1)}, bf16[1,64,1076]{2,1,0:T(8,128)(2,1)S(1)}, u32[]{:S(2)}, u32[]{:S(2)}) %collective-permute-start) | collective-permute-done | bytes 137760 | tf_op jit(solution)/shard_map/ppermute | solution.py:41
  17.3 1.5 collective-permute-start.2
  18.8 1.1 collective-permute-done.1
  19.9 3.1 %collective-permute-done.2 = bf16[1,64,1076]{2,1,0:T(8,128)(2,1)S(1)} collective-permute-done((bf16[1,64,1076]{2,1,0:T(8,128)(2,1)S(1)}, bf16[1,64,1076]{2,1,0:T(8,128)(2,1)S(1)}, u32[]{:S(2)}, u32[]{:S(2)}) %collective-permute-start.2) | collective-permute-done | bytes 137760 | tf_op jit(solution)/shard_map/ppermute | solution.py:41
  23.8 8.5 %all-to-all-start = ((bf16[8,36,538]{2,1,0:T(8,128)(2,1)}), bf16[8,36,538]{2,1,0:T(8,128)(2,1)S(1)}, u32[]{:S(2)}, u32[]{:S(2)}) async-start(bf16[8,36,538]{2,1,0:T(8,128)(2,1)} %broadcast_in_dim.14), calls=%async_computation | async-start | bytes 819200 | tf_op jit(solution)/shard_map/all_to_all | solution.py:45
  32.4 2.1 collective-permute-start.7
  34.5 1.3 collective-permute-start.8
  37.7 9.9 %all-to-all-done = bf16[8,36,538]{2,1,0:T(8,128)(2,1)S(1)} async-done(((bf16[8,36,538]{2,1,0:T(8,128)(2,1)}), bf16[8,36,538]{2,1,0:T(8,128)(2,1)S(1)}, u32[]{:S(2)}, u32[]{:S(2)}) %all-to-all-start) | async-done | bytes 309920 | tf_op jit(solution)/shard_map/all_to_all | solution.py:45
  48.8 2.6 %collective-permute-start.9 = (bf16[256,1076]{0,1:T(8,128)(2,1)S(1)}, bf16[256,1076]{0,1:T(8,128)(2,1)}, u32[]{:S(2)}, u32[]{:S(2)}) collective-permute-start(bf16[256,1076]{0,1:T(8,128)(2,1)S(1)} %copy.77), channel_id=1, source_target_pairs={{0,24},{8,0},{16,8},{24,16},{1,25},{9,1},{17,9},{25,17},{2,26},{10... | collective-permute-start | bytes 1652744 | tf_op jit(solution)/shard_map/ppermute | solution.py:41
  51.4 0.9 constant_dynamic-update-slice_fusion.8
  52.2 4.3 %collective-permute-done.7 = bf16[256,1152]{1,0:T(8,128)(2,1)S(1)} collective-permute-done((bf16[256,1152]{1,0:T(8,128)(2,1)S(1)}, bf16[256,1152]{1,0:T(8,128)(2,1)S(1)}, u32[]{:S(2)}, u32[]{:S(2)}) %collective-permute-start.7) | collective-permute-done | bytes 589856 | tf_op jit(solution)/shard_map/ppermute | solution.py:41
  56.8 3.0 %collective-permute-start.16 = (bf16[256,1152]{1,0:T(8,128)(2,1)S(1)}, bf16[256,1152]{1,0:T(8,128)(2,1)}, u32[]{:S(2)}, u32[]{:S(2)}) collective-permute-start(bf16[256,1152]{1,0:T(8,128)(2,1)S(1)} %collective-permute-done.8), channel_id=1, source_target_pairs={{0,7},{1,0},{2,1},{3,2},{4,3},{5,4},{6,5},{7,6},{8,15},{9,8},{10,9... | collective-permute-start | bytes 1769480 | tf_op jit(solution)/shard_map/ppermute | solution.py:41
  59.8 1.1 broadcast_select_fusion.1
  62.2 13.2 %collective-permute-done.9 = bf16[256,1076]{0,1:T(8,128)(2,1)} collective-permute-done((bf16[256,1076]{0,1:T(8,128)(2,1)S(1)}, bf16[256,1076]{0,1:T(8,128)(2,1)}, u32[]{:S(2)}, u32[]{:S(2)}) %collective-permute-start.9) | collective-permute-done | bytes 550944 | tf_op jit(solution)/shard_map/ppermute | solution.py:41
  75.4 1.5 convolution_convert_fusion.2
  77.1 1.6 convolution_convert_fusion.1
  79.0 1.5 convolution_convert_fusion
  80.7 1.0 broadcast_in_dim.12
  84.6 8.6 %all-to-all-start.1 = ((bf16[16,64,288]{2,1,0:T(8,128)(2,1)}), bf16[16,64,288]{2,1,0:T(8,128)(2,1)S(1)}, u32[]{:S(2)}, u32[]{:S(2)}) async-start(bf16[16,64,288]{2,1,0:T(8,128)(2,1)} %bitcast.11), calls=%async_computation.1 | async-start | bytes 1572864 | tf_op jit(solution)/shard_map/all_to_all | solution.py:45
  93.2 0.9 constant_dynamic-update-slice_fusion.7
  94.1 0.9 constant_dynamic-update-slice_fusion.6
  95.7 2.5 %collective-permute-start.18 = (bf16[256,1152]{1,0:T(8,128)(2,1)}, bf16[256,1152]{1,0:T(8,128)(2,1)S(1)}, u32[]{:S(2)}, u32[]{:S(2)}) collective-permute-start(bf16[256,1152]{1,0:T(8,128)(2,1)} %collective-permute-done.16), channel_id=1, source_target_pairs={{0,7},{1,0},{2,1},{3,2},{4,3},{5,4},{6,5},{7,6},{8,15},{9,8},{10,9... | collective-permute-start | bytes 1769480 | tf_op jit(solution)/shard_map/ppermute | solution.py:41
  98.2 1.9 constant_dynamic-update-slice_fusion.5
  100.1 4.7 %all-to-all-done.1 = bf16[16,64,288]{2,1,0:T(8,128)(2,1)S(1)} async-done(((bf16[16,64,288]{2,1,0:T(8,128)(2,1)}), bf16[16,64,288]{2,1,0:T(8,128)(2,1)S(1)}, u32[]{:S(2)}, u32[]{:S(2)}) %all-to-all-start.1) | async-done | bytes 589856 | tf_op jit(solution)/shard_map/all_to_all | solution.py:45
  106.0 1.4 collective-permute-start.12
  107.4 1.9 constant_dynamic-update-slice_fusion.4
  109.3 3.1 %collective-permute-start.13 = (bf16[64,1152]{1,0:T(8,128)(2,1)S(1)}, bf16[64,1152]{1,0:T(8,128)(2,1)S(1)}, u32[]{:S(2)}, u32[]{:S(2)}) collective-permute-start(bf16[64,1152]{1,0:T(8,128)(2,1)S(1)} %fusion.22), channel_id=1, source_target_pairs={{0,128},{64,192},{128,0},{192,64},{1,129},{65,193},{129,1},{193,65... | collective-permute-start | bytes 442376 | tf_op jit(solution)/shard_map/ppermute | solution.py:41
  113.0 3.1 %collective-permute-done.13 = bf16[64,1152]{1,0:T(8,128)(2,1)S(1)} collective-permute-done((bf16[64,1152]{1,0:T(8,128)(2,1)S(1)}, bf16[64,1152]{1,0:T(8,128)(2,1)S(1)}, u32[]{:S(2)}, u32[]{:S(2)}) %collective-permute-start.13) | collective-permute-done | bytes 147488 | tf_op jit(solution)/shard_map/ppermute | solution.py:41
  116.1 1.6 collective-permute-done.14
  118.5 2.6 %collective-permute-start.20 = (bf16[128,1152]{1,0:T(8,128)(2,1)S(1)}, bf16[128,1152]{1,0:T(8,128)(2,1)S(1)}, u32[]{:S(2)}, u32[]{:S(2)}) collective-permute-start(bf16[128,1152]{1,0:T(8,128)(2,1)S(1)} %slice.43), channel_id=1, source_target_pairs={{0,7},{1,0},{2,1},{3,2},{4,3},{5,4},{6,5},{7,6},{8,15},{9,8},{10,9... | collective-permute-start | bytes 884744 | tf_op jit(solution)/shard_map/ppermute | solution.py:41
  121.1 0.9 constant_dynamic-update-slice_fusion.3
  122.0 0.9 constant_dynamic-update-slice_fusion.2
  122.9 2.9 %collective-permute-done.19 = bf16[128,1152]{1,0:T(8,128)(2,1)S(1)} collective-permute-done((bf16[128,1152]{1,0:T(8,128)(2,1)S(1)}, bf16[128,1152]{1,0:T(8,128)(2,1)S(1)}, u32[]{:S(2)}, u32[]{:S(2)}) %collective-permute-start.19) | collective-permute-done | bytes 294944 | tf_op jit(solution)/shard_map/ppermute | solution.py:41
  127.2 7.8 %shard_map.111 = (f32[256,1152]{1,0:T(8,128)}, f32[1,512]{1,0:T(1,128)}) custom-call(f32[2]{0:T(128)} %pad_maximum_fusion.1.scalars, bf16[256,1152]{1,0:T(8,128)(2,1)} %copy-done.1, bf16[2048,1152]{1,0:T(8,128)(2,1)} %constant_dynamic-update-slice_fusion.texts), custom_call_target="tpu_custom_call" | custom-call | flops 2415919104 | bytes 4718592 | tf_op jit(solution)/shard_map/pallas_call | solution.py:133
  135.5 8.5 %shard_map.112 = (f32[256,1152]{1,0:T(8,128)}, bf16[256,1152]{1,0:T(8,128)(2,1)}, f32[1,512]{1,0:T(1,128)}) custom-call(f32[2]{0:T(128)} %pad_maximum_fusion.1.scalars, bf16[256,1152]{1,0:T(8,128)(2,1)} %copy-done.1, bf16[2048,1152]{1,0:T(8,128)(2,1)} %collective-permute-done.21.texts, f32[256,1152]{1,0:T(8,128)} %get-tuple-element.27.refs_0_), custom_call_target="tpu_custom_call" | custom-call | flops 2415919104 | bytes 4718592 | tf_op jit(solution)/shard_map/pallas_call | solution.py:133
  144.0 1.1 fusion.24
  145.7 3.1 %collective-permute-start.23 = (bf16[64,1152]{1,0:T(8,128)(2,1)S(1)}, bf16[64,1152]{1,0:T(8,128)(2,1)S(1)}, u32[]{:S(2)}, u32[]{:S(2)}) collective-permute-start(bf16[64,1152]{1,0:T(8,128)(2,1)S(1)} %get-tuple-element.40), channel_id=1, source_target_pairs={{0,128},{64,192},{128,0},{192,64},{1,129},{65,193},{129,1},{193,65... | collective-permute-start | bytes 442376 | tf_op jit(solution)/shard_map/ppermute | solution.py:41
  148.8 2.1 collective-permute-start.22
  151.0 2.9 %collective-permute-done.23 = bf16[64,1152]{1,0:T(8,128)(2,1)S(1)} collective-permute-done((bf16[64,1152]{1,0:T(8,128)(2,1)S(1)}, bf16[64,1152]{1,0:T(8,128)(2,1)S(1)}, u32[]{:S(2)}, u32[]{:S(2)}) %collective-permute-start.23) | collective-permute-done | bytes 147488 | tf_op jit(solution)/shard_map/ppermute | solution.py:41
  153.9 2.1 collective-permute-done.22
  156.0 1.2 multiply_reduce_fusion
  157.2 1.1 divide_convert_fusion
  158.6 18.5 %all_to_all.35 = bf16[16,64,288]{2,1,0:T(8,128)(2,1)S(1)} all-to-all(bf16[16,64,288]{2,1,0:T(8,128)(2,1)S(1)} %bitcast.72), channel_id=1, replica_groups=mesh['x'=4,'k'=2,'y'=4,'z'=8] {'x','y'}, dimensions={0} | all-to-all | bytes 1179648 | tf_op jit(solution)/shard_map/all_to_all | solution.py:45
  177.2 1.5 fusion.5
  178.7 1.5 fusion.7
  180.3 1.5 fusion.9
  182.6 2.2 collective-permute-done.25
  185.1 0.8 reshape.102
  186.0 4.6 %all-to-all-start.3 = ((bf16[8,36,538]{2,1,0:T(8,128)(2,1)}), bf16[8,36,538]{2,1,0:T(8,128)(2,1)S(1)}, u32[]{:S(2)}, u32[]{:S(2)}) async-start(bf16[8,36,538]{2,1,0:T(8,128)(2,1)} %reshape.102), calls=%async_computation.3 | async-start | bytes 819200 | tf_op jit(solution)/shard_map/all_to_all | solution.py:45
  191.2 14.7 %all-to-all-done.3 = bf16[8,36,538]{2,1,0:T(8,128)(2,1)S(1)} async-done(((bf16[8,36,538]{2,1,0:T(8,128)(2,1)}), bf16[8,36,538]{2,1,0:T(8,128)(2,1)S(1)}, u32[]{:S(2)}, u32[]{:S(2)}) %all-to-all-start.3) | async-done | bytes 309920 | tf_op jit(solution)/shard_map/all_to_all | solution.py:45
  206.8 8.0 %all_to_all.36 = f32[8,1,37]{2,1,0:T(1,128)S(1)} all-to-all(f32[8,1,37]{2,1,0:T(1,128)S(1)} %broadcast_in_dim.32), channel_id=1, replica_groups=mesh['x'=4,'k'=2,'y'=4,'z'=8] {'x','k'}, dimensions={0} | all-to-all | bytes 2368 | tf_op jit(solution)/shard_map/all_to_all | solution.py:45
  216.3 13.8 %all_to_all.37 = f32[32,1,1077]{2,1,0:T(1,128)S(1)} all-to-all(f32[32,1,1077]{2,1,0:T(1,128)S(1)} %broadcast_in_dim.33), channel_id=1, replica_groups=mesh['x'=4,'k'=2,'y'=4,'z'=8] {'y','z'}, dimensions={0} | all-to-all | bytes 275712 | tf_op jit(solution)/shard_map/all_to_all | solution.py:45
  230.9 1.2 broadcast_in_dim_broadcast_in_dim.3
  232.2 4.7 %all-to-all-start.6 = ((f32[8,1,128]{2,1,0:T(1,128)}), f32[8,1,128]{2,1,0:T(1,128)S(1)}, u32[]{:S(2)}, u32[]{:S(2)}) async-start(f32[8,1,128]{2,1,0:T(1,128)} %broadcast_in_dim_broadcast_in_dim.3), calls=%async_computation.6 | async-start | bytes 8192 | tf_op jit(solution)/shard_map/all_to_all | solution.py:45
  238.1 2.6 %all-to-all-done.6 = f32[8,1,128]{2,1,0:T(1,128)S(1)} async-done(((f32[8,1,128]{2,1,0:T(1,128)}), f32[8,1,128]{2,1,0:T(1,128)S(1)}, u32[]{:S(2)}, u32[]{:S(2)}) %all-to-all-start.6) | async-done | bytes 4128 | tf_op jit(solution)/shard_map/all_to_all | solution.py:45
  (113 shorter events, 20.4 us)
Async XLA Ops:
  2.7 29.6 %collective-permute-start.4 = (bf16[64,1152]{1,0:T(8,128)(2,1)S(1)}, bf16[64,1152]{1,0:T(8,128)(2,1)S(1)}, u32[]{:S(2)}, u32[]{:S(2)}) collective-permute-start(bf16[64,1152]{1,0:T(8,128)(2,1)S(1)} %fusion.3), channel_id=1, source_target_pairs={{0,40},{8,48},{16,56},{24,32},{32,8},{40,16},{48,24},{56,0},{1,41}... | collective-permute-start | bytes 442376 | tf_op jit(solution)/shard_map/ppermute | solution.py:41
  3.8 28.5 %collective-permute-start.5 = (bf16[64,1152]{1,0:T(8,128)(2,1)S(1)}, bf16[64,1152]{1,0:T(8,128)(2,1)S(1)}, u32[]{:S(2)}, u32[]{:S(2)}) collective-permute-start(bf16[64,1152]{1,0:T(8,128)(2,1)S(1)} %fusion.3), channel_id=1, source_target_pairs={{0,48},{8,56},{16,32},{24,40},{32,16},{40,24},{48,0},{56,8},{1,49}... | collective-permute-start | bytes 442376 | tf_op jit(solution)/shard_map/ppermute | solution.py:41
  7.0 25.4 %collective-permute-start.6 = (bf16[64,1152]{1,0:T(8,128)(2,1)S(1)}, bf16[64,1152]{1,0:T(8,128)(2,1)S(1)}, u32[]{:S(2)}, u32[]{:S(2)}) collective-permute-start(bf16[64,1152]{1,0:T(8,128)(2,1)S(1)} %fusion.3), channel_id=1, source_target_pairs={{0,56},{8,32},{16,40},{24,48},{32,24},{40,0},{48,8},{56,16},{1,57}... | collective-permute-start | bytes 442376 | tf_op jit(solution)/shard_map/ppermute | solution.py:41
  10.5 6.8 %collective-permute-start = (bf16[1,64,1076]{2,1,0:T(8,128)(2,1)S(1)}, bf16[1,64,1076]{2,1,0:T(8,128)(2,1)S(1)}, u32[]{:S(2)}, u32[]{:S(2)}) collective-permute-start(bf16[1,64,1076]{2,1,0:T(8,128)(2,1)S(1)} %bitcast.80), channel_id=1, source_target_pairs={{0,64},{64,128},{128,192},{192,0},{1,65},{65,129},{129,193},{193,1... | collective-permute-start | bytes 413192 | tf_op jit(solution)/shard_map/ppermute | solution.py:41
  12.1 1.4 copy-start.5
  12.1 7.8 %collective-permute-start.1 = (bf16[1,64,1076]{2,1,0:T(8,128)(2,1)S(1)}, bf16[1,64,1076]{2,1,0:T(8,128)(2,1)S(1)}, u32[]{:S(2)}, u32[]{:S(2)}) collective-permute-start(bf16[1,64,1076]{2,1,0:T(8,128)(2,1)S(1)} %bitcast.79), channel_id=1, source_target_pairs={{0,128},{64,192},{128,0},{192,64},{1,129},{65,193},{129,1},{193,65... | collective-permute-start | bytes 413192 | tf_op jit(solution)/shard_map/ppermute | solution.py:41
  17.3 5.7 %collective-permute-start.2 = (bf16[1,64,1076]{2,1,0:T(8,128)(2,1)S(1)}, bf16[1,64,1076]{2,1,0:T(8,128)(2,1)S(1)}, u32[]{:S(2)}, u32[]{:S(2)}) collective-permute-start(bf16[1,64,1076]{2,1,0:T(8,128)(2,1)S(1)} %bitcast.81), channel_id=1, source_target_pairs={{0,192},{64,0},{128,64},{192,128},{1,193},{65,1},{129,65},{193,129... | collective-permute-start | bytes 413192 | tf_op jit(solution)/shard_map/ppermute | solution.py:41
  23.8 23.8 %all-to-all-start = ((bf16[8,36,538]{2,1,0:T(8,128)(2,1)}), bf16[8,36,538]{2,1,0:T(8,128)(2,1)S(1)}, u32[]{:S(2)}, u32[]{:S(2)}) async-start(bf16[8,36,538]{2,1,0:T(8,128)(2,1)} %broadcast_in_dim.14), calls=%async_computation | async-start | bytes 819200 | tf_op jit(solution)/shard_map/all_to_all | solution.py:45
  32.4 24.1 %collective-permute-start.7 = (bf16[256,1152]{1,0:T(8,128)(2,1)S(1)}, bf16[256,1152]{1,0:T(8,128)(2,1)S(1)}, u32[]{:S(2)}, u32[]{:S(2)}) collective-permute-start(bf16[256,1152]{1,0:T(8,128)(2,1)S(1)} %constant_dynamic-update-slice_fusion.16), channel_id=1, source_target_pairs={{0,1},{1,2},{2,3},{3,4},{4,5},{5,6},{6,7},{7,0},{8,9},{9,10},{10,1... | collective-permute-start | bytes 1769480 | tf_op jit(solution)/shard_map/ppermute | solution.py:41
  34.5 22.1 %collective-permute-start.8 = (bf16[256,1152]{1,0:T(8,128)(2,1)S(1)}, bf16[256,1152]{1,0:T(8,128)(2,1)S(1)}, u32[]{:S(2)}, u32[]{:S(2)}) collective-permute-start(bf16[256,1152]{1,0:T(8,128)(2,1)S(1)} %constant_dynamic-update-slice_fusion.16), channel_id=1, source_target_pairs={{0,7},{1,0},{2,1},{3,2},{4,3},{5,4},{6,5},{7,6},{8,15},{9,8},{10,9... | collective-permute-start | bytes 1769480 | tf_op jit(solution)/shard_map/ppermute | solution.py:41
  47.7 9.1 %collective-permute-start.3 = (bf16[288,538]{1,0:T(8,128)(2,1)S(1)}, bf16[288,538]{1,0:T(8,128)(2,1)}, u32[]{:S(2)}, u32[]{:S(2)}) collective-permute-start(bf16[288,538]{1,0:T(8,128)(2,1)S(1)} %reshape.89), channel_id=1, source_target_pairs={{0,32},{32,0},{1,33},{33,1},{2,34},{34,2},{3,35},{35,3},{4,36},{36... | collective-permute-start | bytes 929672 | tf_op jit(solution)/shard_map/ppermute | solution.py:41
  48.1 30.9 %collective-permute-start.11 = (bf16[256,1076]{0,1:T(8,128)(2,1)S(1)}, bf16[256,1076]{0,1:T(8,128)(2,1)}, u32[]{:S(2)}, u32[]{:S(2)}) collective-permute-start(bf16[256,1076]{0,1:T(8,128)(2,1)S(1)} %copy.77), channel_id=1, source_target_pairs={{0,8},{8,16},{16,24},{24,0},{1,9},{9,17},{17,25},{25,1},{2,10},{10... | collective-permute-start | bytes 1652744 | tf_op jit(solution)/shard_map/ppermute | solution.py:41
  48.8 26.6 %collective-permute-start.9 = (bf16[256,1076]{0,1:T(8,128)(2,1)S(1)}, bf16[256,1076]{0,1:T(8,128)(2,1)}, u32[]{:S(2)}, u32[]{:S(2)}) collective-permute-start(bf16[256,1076]{0,1:T(8,128)(2,1)S(1)} %copy.77), channel_id=1, source_target_pairs={{0,24},{8,0},{16,8},{24,16},{1,25},{9,1},{17,9},{25,17},{2,26},{10... | collective-permute-start | bytes 1652744 | tf_op jit(solution)/shard_map/ppermute | solution.py:41
  56.5 20.6 %collective-permute-start.10 = (bf16[256,1076]{0,1:T(8,128)(2,1)S(1)}, bf16[256,1076]{0,1:T(8,128)(2,1)}, u32[]{:S(2)}, u32[]{:S(2)}) collective-permute-start(bf16[256,1076]{0,1:T(8,128)(2,1)S(1)} %copy.77), channel_id=1, source_target_pairs={{0,16},{8,24},{16,0},{24,8},{1,17},{9,25},{17,1},{25,9},{2,18},{10... | collective-permute-start | bytes 1652744 | tf_op jit(solution)/shard_map/ppermute | solution.py:41
  56.6 38.4 %collective-permute-start.15 = (bf16[256,1152]{1,0:T(8,128)(2,1)S(1)}, bf16[256,1152]{1,0:T(8,128)(2,1)}, u32[]{:S(2)}, u32[]{:S(2)}) collective-permute-start(bf16[256,1152]{1,0:T(8,128)(2,1)S(1)} %collective-permute-done.7), channel_id=1, source_target_pairs={{0,1},{1,2},{2,3},{3,4},{4,5},{5,6},{6,7},{7,0},{8,9},{9,10},{10,1... | collective-permute-start | bytes 1769480 | tf_op jit(solution)/shard_map/ppermute | solution.py:41
  56.8 38.1 %collective-permute-start.16 = (bf16[256,1152]{1,0:T(8,128)(2,1)S(1)}, bf16[256,1152]{1,0:T(8,128)(2,1)}, u32[]{:S(2)}, u32[]{:S(2)}) collective-permute-start(bf16[256,1152]{1,0:T(8,128)(2,1)S(1)} %collective-permute-done.8), channel_id=1, source_target_pairs={{0,7},{1,0},{2,1},{3,2},{4,3},{5,4},{6,5},{7,6},{8,15},{9,8},{10,9... | collective-permute-start | bytes 1769480 | tf_op jit(solution)/shard_map/ppermute | solution.py:41
  60.9 0.8 copy-start.4
  60.9 14.5 %copy-start.2 = (bf16[288,538]{1,0:T(8,128)(2,1)}, bf16[288,538]{1,0:T(8,128)(2,1)S(1)}, u32[]{:S(2)}) copy-start(bf16[288,538]{1,0:T(8,128)(2,1)S(1)} %get-tuple-element.36) | copy-start | bytes 929668
  77.0 2.0 copy-start.3
  84.6 20.2 %all-to-all-start.1 = ((bf16[16,64,288]{2,1,0:T(8,128)(2,1)}), bf16[16,64,288]{2,1,0:T(8,128)(2,1)S(1)}, u32[]{:S(2)}, u32[]{:S(2)}) async-start(bf16[16,64,288]{2,1,0:T(8,128)(2,1)} %bitcast.11), calls=%async_computation.1 | async-start | bytes 1572864 | tf_op jit(solution)/shard_map/all_to_all | solution.py:45
  95.0 22.7 %collective-permute-start.17 = (bf16[256,1152]{1,0:T(8,128)(2,1)}, bf16[256,1152]{1,0:T(8,128)(2,1)S(1)}, u32[]{:S(2)}, u32[]{:S(2)}) collective-permute-start(bf16[256,1152]{1,0:T(8,128)(2,1)} %collective-permute-done.15), channel_id=1, source_target_pairs={{0,1},{1,2},{2,3},{3,4},{4,5},{5,6},{6,7},{7,0},{8,9},{9,10},{10,1... | collective-permute-start | bytes 1769480 | tf_op jit(solution)/shard_map/ppermute | solution.py:41
  95.7 22.0 %collective-permute-start.18 = (bf16[256,1152]{1,0:T(8,128)(2,1)}, bf16[256,1152]{1,0:T(8,128)(2,1)S(1)}, u32[]{:S(2)}, u32[]{:S(2)}) collective-permute-start(bf16[256,1152]{1,0:T(8,128)(2,1)} %collective-permute-done.16), channel_id=1, source_target_pairs={{0,7},{1,0},{2,1},{3,2},{4,3},{5,4},{6,5},{7,6},{8,15},{9,8},{10,9... | collective-permute-start | bytes 1769480 | tf_op jit(solution)/shard_map/ppermute | solution.py:41
  104.8 0.9 copy-start
  106.0 7.0 %collective-permute-start.12 = (bf16[64,1152]{1,0:T(8,128)(2,1)S(1)}, bf16[64,1152]{1,0:T(8,128)(2,1)S(1)}, u32[]{:S(2)}, u32[]{:S(2)}) collective-permute-start(bf16[64,1152]{1,0:T(8,128)(2,1)S(1)} %fusion.22), channel_id=1, source_target_pairs={{0,64},{64,128},{128,192},{192,0},{1,65},{65,129},{129,193},{193,1... | collective-permute-start | bytes 442376 | tf_op jit(solution)/shard_map/ppermute | solution.py:41
  109.3 6.7 %collective-permute-start.13 = (bf16[64,1152]{1,0:T(8,128)(2,1)S(1)}, bf16[64,1152]{1,0:T(8,128)(2,1)S(1)}, u32[]{:S(2)}, u32[]{:S(2)}) collective-permute-start(bf16[64,1152]{1,0:T(8,128)(2,1)S(1)} %fusion.22), channel_id=1, source_target_pairs={{0,128},{64,192},{128,0},{192,64},{1,129},{65,193},{129,1},{193,65... | collective-permute-start | bytes 442376 | tf_op jit(solution)/shard_map/ppermute | solution.py:41
  112.5 5.2 %collective-permute-start.14 = (bf16[64,1152]{1,0:T(8,128)(2,1)S(1)}, bf16[64,1152]{1,0:T(8,128)(2,1)S(1)}, u32[]{:S(2)}, u32[]{:S(2)}) collective-permute-start(bf16[64,1152]{1,0:T(8,128)(2,1)S(1)} %fusion.22), channel_id=1, source_target_pairs={{0,192},{64,0},{128,64},{192,128},{1,193},{65,1},{129,65},{193,129... | collective-permute-start | bytes 442376 | tf_op jit(solution)/shard_map/ppermute | solution.py:41
  117.7 5.2 %copy-start.1 = (bf16[256,1152]{1,0:T(8,128)(2,1)}, bf16[256,1152]{1,0:T(8,128)(2,1)S(1)}, u32[]{:S(2)}) copy-start(bf16[256,1152]{1,0:T(8,128)(2,1)S(1)} %constant_dynamic-update-slice_fusion.9.images) | copy-start | bytes 1769476
  117.7 8.0 %collective-permute-start.19 = (bf16[128,1152]{1,0:T(8,128)(2,1)S(1)}, bf16[128,1152]{1,0:T(8,128)(2,1)S(1)}, u32[]{:S(2)}, u32[]{:S(2)}) collective-permute-start(bf16[128,1152]{1,0:T(8,128)(2,1)S(1)} %slice.42), channel_id=1, source_target_pairs={{0,1},{1,2},{2,3},{3,4},{4,5},{5,6},{6,7},{7,0},{8,9},{9,10},{10,1... | collective-permute-start | bytes 884744 | tf_op jit(solution)/shard_map/ppermute | solution.py:41
  118.5 7.2 %collective-permute-start.20 = (bf16[128,1152]{1,0:T(8,128)(2,1)S(1)}, bf16[128,1152]{1,0:T(8,128)(2,1)S(1)}, u32[]{:S(2)}, u32[]{:S(2)}) collective-permute-start(bf16[128,1152]{1,0:T(8,128)(2,1)S(1)} %slice.43), channel_id=1, source_target_pairs={{0,7},{1,0},{2,1},{3,2},{4,3},{5,4},{6,5},{7,6},{8,15},{9,8},{10,9... | collective-permute-start | bytes 884744 | tf_op jit(solution)/shard_map/ppermute | solution.py:41
  127.2 8.3 %collective-permute-start.21 = (bf16[2048,1152]{1,0:T(8,128)(2,1)}, bf16[2048,1152]{1,0:T(8,128)(2,1)}, u32[]{:S(2)}, u32[]{:S(2)}) collective-permute-start(bf16[2048,1152]{1,0:T(8,128)(2,1)} %constant_dynamic-update-slice_fusion.texts), channel_id=1, source_target_pairs={{0,32},{32,0},{1,33},{33,1},{2,34},{34,2},{3,35},{35,3},{4,36},{36... | collective-permute-start | bytes 14155784 | tf_op jit(solution)/shard_map/ppermute | solution.py:41
  145.1 6.0 %collective-permute-start.24 = (bf16[64,1152]{1,0:T(8,128)(2,1)S(1)}, bf16[64,1152]{1,0:T(8,128)(2,1)S(1)}, u32[]{:S(2)}, u32[]{:S(2)}) collective-permute-start(bf16[64,1152]{1,0:T(8,128)(2,1)S(1)} %get-tuple-element.39), channel_id=1, source_target_pairs={{0,64},{64,128},{128,192},{192,0},{1,65},{65,129},{129,193},{193,1... | collective-permute-start | bytes 442376 | tf_op jit(solution)/shard_map/ppermute | solution.py:41
  145.7 8.2 %collective-permute-start.23 = (bf16[64,1152]{1,0:T(8,128)(2,1)S(1)}, bf16[64,1152]{1,0:T(8,128)(2,1)S(1)}, u32[]{:S(2)}, u32[]{:S(2)}) collective-permute-start(bf16[64,1152]{1,0:T(8,128)(2,1)S(1)} %get-tuple-element.40), channel_id=1, source_target_pairs={{0,128},{64,192},{128,0},{192,64},{1,129},{65,193},{129,1},{193,65... | collective-permute-start | bytes 442376 | tf_op jit(solution)/shard_map/ppermute | solution.py:41
  148.8 7.2 %collective-permute-start.22 = (bf16[64,1152]{1,0:T(8,128)(2,1)S(1)}, bf16[64,1152]{1,0:T(8,128)(2,1)S(1)}, u32[]{:S(2)}, u32[]{:S(2)}) collective-permute-start(bf16[64,1152]{1,0:T(8,128)(2,1)S(1)} %get-tuple-element.38), channel_id=1, source_target_pairs={{0,192},{64,0},{128,64},{192,128},{1,193},{65,1},{129,65},{193,129... | collective-permute-start | bytes 442376 | tf_op jit(solution)/shard_map/ppermute | solution.py:41
  182.5 2.3 collective-permute-start.25
  185.1 5.5 %copy-start.9 = (f32[1,512]{1,0:T(1,128)S(1)}, f32[1,512]{1,0:T(1,128)}, u32[]{:S(2)}) copy-start(f32[1,512]{1,0:T(1,128)} %get-tuple-element.30) | copy-start | bytes 6148
  185.1 5.5 %copy-start.10 = (f32[1,512]{1,0:T(1,128)S(1)}, f32[1,512]{1,0:T(1,128)}, u32[]{:S(2)}) copy-start(f32[1,512]{1,0:T(1,128)} %get-tuple-element.31) | copy-start | bytes 6148
  185.1 30.3 %copy-start.11 = (f32[36]{0:T(128)S(1)}, f32[36]{0:T(128)}, u32[]{:S(2)}) copy-start(f32[36]{0:T(128)} %param.12) | copy-start | bytes 436
  185.1 45.1 %copy-start.7 = (f32[538]{0:T(1024)S(1)}, f32[538]{0:T(1024)}, u32[]{:S(2)}) copy-start(f32[538]{0:T(1024)} %param.13) | copy-start | bytes 6460
  186.0 20.0 %all-to-all-start.3 = ((bf16[8,36,538]{2,1,0:T(8,128)(2,1)}), bf16[8,36,538]{2,1,0:T(8,128)(2,1)S(1)}, u32[]{:S(2)}, u32[]{:S(2)}) async-start(bf16[8,36,538]{2,1,0:T(8,128)(2,1)} %reshape.102), calls=%async_computation.3 | async-start | bytes 819200 | tf_op jit(solution)/shard_map/all_to_all | solution.py:45
  215.4 26.0 %copy-start.8 = (f32[36]{0:T(128)}, f32[36]{0:T(128)S(1)}, u32[]{:S(2)}) copy-start(f32[36]{0:T(128)S(1)} %multiply_add_fusion) | copy-start | bytes 436
  230.9 10.6 %copy-start.6 = (f32[538]{0:T(1024)}, f32[538]{0:T(1024)S(1)}, u32[]{:S(2)}) copy-start(f32[538]{0:T(1024)S(1)} %get-tuple-element.35) | copy-start | bytes 6460
  232.2 8.5 %all-to-all-start.6 = ((f32[8,1,128]{2,1,0:T(1,128)}), f32[8,1,128]{2,1,0:T(1,128)S(1)}, u32[]{:S(2)}, u32[]{:S(2)}) async-start(f32[8,1,128]{2,1,0:T(1,128)} %broadcast_in_dim_broadcast_in_dim.3), calls=%async_computation.6 | async-start | bytes 8192 | tf_op jit(solution)/shard_map/all_to_all | solution.py:45

commit v6 on v5

--- a/solution.py
+++ b/solution.py
@@ -172,10 +172,9 @@
     ring_pieces = [texts_y, up, down]
     scalars = jnp.stack([jnp.exp(log_scale), bias])
     weight_own = everywhere(after(weight.astype(BF16), hidden_x), "z")
-    weight_own = after(weight_own.reshape(quarter, slice_ff), scalars)
-    weight_other = after(shift(weight_own, k=1), up, down)
-    up, down = ring_step(up, down, "z")
-    ring_pieces += [up, down]
+    weight_own = weight_own.reshape(quarter, slice_ff)
+    weight_own = after(weight_own, scalars)
+    weight_other = shift(weight_own, k=1)
     weight_x = jnp.concatenate(
         [
             jnp.where(first_core, weight_own, weight_other),
@@ -183,6 +182,8 @@
         ],
         axis=1,
     )
+    up, down = ring_step(up, down, "z")
+    ring_pieces += [up, down]
     y_place = lax.axis_index("y")
     partial = jnp.zeros((4, 4, tokens, quarter), BF16)
     for s, piece in enumerate(hid_y):

time: 245 us -> 245 us (level)
  no operation moved by 1% of the time
where the time goes in v6:
time: 245 us; the launch traced here: 243 us
  waiting for transfers between devices  72.6 us (30%)
  starting transfers between devices  63.3 us (26%)
  blocking collectives  40.2 us (16%)
  local copies, waits for them, and re-layouts  25.6 us (10%)
  Pallas kernels  16.3 us (7%)
  other arithmetic  10.1 us (4%)
  matrix products  10.1 us (4%)
  between operations  4.35 us (2%)
    ppermute x26, waiting for transfers between devices, shift(): return lax.ppermute(value, names, pairs)  40.7 us
    all_to_all x3, blocking collectives, exchange(): return lax.all_to_all(pieces, axes, split_axis=0, concat_axis=0, tiled=True)  40.2 us
    ppermute x26, starting transfers between devices, shift(): return lax.ppermute(value, names, pairs)  36.9 us
    all_to_all x4, waiting for transfers between devices, exchange(): return lax.all_to_all(pieces, axes, split_axis=0, concat_axis=0, tiled=True)  31.8 us
    all_to_all x4, starting transfers between devices, exchange(): return lax.all_to_all(pieces, axes, split_axis=0, concat_axis=0, tiled=True)  26.4 us
    pallas_call x2, Pallas kernels, pair_tiles(): pl.pallas_call(functools.partial(pair_kernel, first=first, tokens=tokens,...  16.3 us
    unnamed x35, local copies, waits for them, and re-layouts  10.1 us
    dot_general x4, matrix products, step(): lax.dot_general(piece, weight_x, (((1,), (1,)), ((), ())), preferred_elem...  5.12 us
  transfers between devices with their start and end apart: 30, of which 17 were waited for; matrix products, arithmetic and copies ran while one was open for 11% of the time, Pallas kernels for 3%

profile of v6, /device:TPU:2, one launch (start us, length us, event | category | flops | bytes accessed | tf_op | source)
XLA Modules:
  0.0 242.6 jit_solution(1343675982630824044)
XLA Ops:
  0.6 1.0 fusion.2
  1.7 1.0 fusion.3
  2.7 1.1 collective-permute-start.10
  3.8 3.2 %collective-permute-start.11 = (bf16[64,1152]{1,0:T(8,128)(2,1)S(1)}, bf16[64,1152]{1,0:T(8,128)(2,1)S(1)}, u32[]{:S(2)}, u32[]{:S(2)}) collective-permute-start(bf16[64,1152]{1,0:T(8,128)(2,1)S(1)} %fusion.3), channel_id=1, source_target_pairs={{0,48},{8,56},{16,32},{24,40},{32,16},{40,24},{48,0},{56,8},{1,49}... | collective-permute-start | bytes 442376 | tf_op jit(solution)/shard_map/ppermute | solution.py:41
  7.0 0.8 collective-permute-start.12
  7.8 1.5 reshape.87
  9.3 1.2 constant_dynamic-slice_fusion
  10.5 1.6 collective-permute-start
  12.1 1.2 collective-permute-start.1
  13.5 3.8 %collective-permute-done = bf16[1,64,1076]{2,1,0:T(8,128)(2,1)S(1)} collective-permute-done((bf16[1,64,1076]{2,1,0:T(8,128)(2,1)S(1)}, bf16[1,64,1076]{2,1,0:T(8,128)(2,1)S(1)}, u32[]{:S(2)}, u32[]{:S(2)}) %collective-permute-start) | collective-permute-done | bytes 137760 | tf_op jit(solution)/shard_map/ppermute | solution.py:41
  17.3 1.5 collective-permute-start.2
  18.8 1.1 collective-permute-done.1
  19.9 3.1 %collective-permute-done.2 = bf16[1,64,1076]{2,1,0:T(8,128)(2,1)S(1)} collective-permute-done((bf16[1,64,1076]{2,1,0:T(8,128)(2,1)S(1)}, bf16[1,64,1076]{2,1,0:T(8,128)(2,1)S(1)}, u32[]{:S(2)}, u32[]{:S(2)}) %collective-permute-start.2) | collective-permute-done | bytes 137760 | tf_op jit(solution)/shard_map/ppermute | solution.py:41
  23.8 8.5 %all-to-all-start = ((bf16[8,36,538]{2,1,0:T(8,128)(2,1)}), bf16[8,36,538]{2,1,0:T(8,128)(2,1)S(1)}, u32[]{:S(2)}, u32[]{:S(2)}) async-start(bf16[8,36,538]{2,1,0:T(8,128)(2,1)} %broadcast_in_dim.14), calls=%async_computation | async-start | bytes 819200 | tf_op jit(solution)/shard_map/all_to_all | solution.py:45
  32.4 2.1 collective-permute-start.13
  34.5 1.3 collective-permute-start.14
  37.7 9.9 %all-to-all-done = bf16[8,36,538]{2,1,0:T(8,128)(2,1)S(1)} async-done(((bf16[8,36,538]{2,1,0:T(8,128)(2,1)}), bf16[8,36,538]{2,1,0:T(8,128)(2,1)S(1)}, u32[]{:S(2)}, u32[]{:S(2)}) %all-to-all-start) | async-done | bytes 309920 | tf_op jit(solution)/shard_map/all_to_all | solution.py:45
  48.8 2.6 %collective-permute-start.4 = (bf16[256,1076]{0,1:T(8,128)(2,1)S(1)}, bf16[256,1076]{0,1:T(8,128)(2,1)}, u32[]{:S(2)}, u32[]{:S(2)}) collective-permute-start(bf16[256,1076]{0,1:T(8,128)(2,1)S(1)} %copy.77), channel_id=1, source_target_pairs={{0,24},{8,0},{16,8},{24,16},{1,25},{9,1},{17,9},{25,17},{2,26},{10... | collective-permute-start | bytes 1652744 | tf_op jit(solution)/shard_map/ppermute | solution.py:41
  51.4 0.9 constant_dynamic-update-slice_fusion.8
  52.2 4.3 %collective-permute-done.13 = bf16[256,1152]{1,0:T(8,128)(2,1)S(1)} collective-permute-done((bf16[256,1152]{1,0:T(8,128)(2,1)S(1)}, bf16[256,1152]{1,0:T(8,128)(2,1)S(1)}, u32[]{:S(2)}, u32[]{:S(2)}) %collective-permute-start.13) | collective-permute-done | bytes 589856 | tf_op jit(solution)/shard_map/ppermute | solution.py:41
  56.8 3.0 %collective-permute-start.16 = (bf16[256,1152]{1,0:T(8,128)(2,1)S(1)}, bf16[256,1152]{1,0:T(8,128)(2,1)}, u32[]{:S(2)}, u32[]{:S(2)}) collective-permute-start(bf16[256,1152]{1,0:T(8,128)(2,1)S(1)} %collective-permute-done.14), channel_id=1, source_target_pairs={{0,7},{1,0},{2,1},{3,2},{4,3},{5,4},{6,5},{7,6},{8,15},{9,8},{10,9... | collective-permute-start | bytes 1769480 | tf_op jit(solution)/shard_map/ppermute | solution.py:41
  59.8 1.1 broadcast_select_fusion.1
  62.2 13.2 %collective-permute-done.4 = bf16[256,1076]{0,1:T(8,128)(2,1)} collective-permute-done((bf16[256,1076]{0,1:T(8,128)(2,1)S(1)}, bf16[256,1076]{0,1:T(8,128)(2,1)}, u32[]{:S(2)}, u32[]{:S(2)}) %collective-permute-start.4) | collective-permute-done | bytes 550944 | tf_op jit(solution)/shard_map/ppermute | solution.py:41
  75.4 1.5 convolution_convert_fusion.2
  77.1 1.6 convolution_convert_fusion.1
  79.0 1.5 convolution_convert_fusion
  80.7 1.0 broadcast_in_dim.12
  84.6 8.6 %all-to-all-start.1 = ((bf16[16,64,288]{2,1,0:T(8,128)(2,1)}), bf16[16,64,288]{2,1,0:T(8,128)(2,1)S(1)}, u32[]{:S(2)}, u32[]{:S(2)}) async-start(bf16[16,64,288]{2,1,0:T(8,128)(2,1)} %bitcast.11), calls=%async_computation.1 | async-start | bytes 1572864 | tf_op jit(solution)/shard_map/all_to_all | solution.py:45
  93.2 0.9 constant_dynamic-update-slice_fusion.7
  94.1 0.9 constant_dynamic-update-slice_fusion.6
  95.7 2.5 %collective-permute-start.18 = (bf16[256,1152]{1,0:T(8,128)(2,1)}, bf16[256,1152]{1,0:T(8,128)(2,1)S(1)}, u32[]{:S(2)}, u32[]{:S(2)}) collective-permute-start(bf16[256,1152]{1,0:T(8,128)(2,1)} %collective-permute-done.16), channel_id=1, source_target_pairs={{0,7},{1,0},{2,1},{3,2},{4,3},{5,4},{6,5},{7,6},{8,15},{9,8},{10,9... | collective-permute-start | bytes 1769480 | tf_op jit(solution)/shard_map/ppermute | solution.py:41
  98.2 1.9 constant_dynamic-update-slice_fusion.5
  100.1 4.7 %all-to-all-done.1 = bf16[16,64,288]{2,1,0:T(8,128)(2,1)S(1)} async-done(((bf16[16,64,288]{2,1,0:T(8,128)(2,1)}), bf16[16,64,288]{2,1,0:T(8,128)(2,1)S(1)}, u32[]{:S(2)}, u32[]{:S(2)}) %all-to-all-start.1) | async-done | bytes 589856 | tf_op jit(solution)/shard_map/all_to_all | solution.py:45
  106.0 1.4 collective-permute-start.7
  107.4 1.9 constant_dynamic-update-slice_fusion.4
  109.3 3.1 %collective-permute-start.8 = (bf16[64,1152]{1,0:T(8,128)(2,1)S(1)}, bf16[64,1152]{1,0:T(8,128)(2,1)S(1)}, u32[]{:S(2)}, u32[]{:S(2)}) collective-permute-start(bf16[64,1152]{1,0:T(8,128)(2,1)S(1)} %fusion.22), channel_id=1, source_target_pairs={{0,128},{64,192},{128,0},{192,64},{1,129},{65,193},{129,1},{193,65... | collective-permute-start | bytes 442376 | tf_op jit(solution)/shard_map/ppermute | solution.py:41
  113.0 3.1 %collective-permute-done.8 = bf16[64,1152]{1,0:T(8,128)(2,1)S(1)} collective-permute-done((bf16[64,1152]{1,0:T(8,128)(2,1)S(1)}, bf16[64,1152]{1,0:T(8,128)(2,1)S(1)}, u32[]{:S(2)}, u32[]{:S(2)}) %collective-permute-start.8) | collective-permute-done | bytes 147488 | tf_op jit(solution)/shard_map/ppermute | solution.py:41
  116.1 1.6 collective-permute-done.9
  118.5 2.6 %collective-permute-start.20 = (bf16[128,1152]{1,0:T(8,128)(2,1)S(1)}, bf16[128,1152]{1,0:T(8,128)(2,1)S(1)}, u32[]{:S(2)}, u32[]{:S(2)}) collective-permute-start(bf16[128,1152]{1,0:T(8,128)(2,1)S(1)} %slice.43), channel_id=1, source_target_pairs={{0,7},{1,0},{2,1},{3,2},{4,3},{5,4},{6,5},{7,6},{8,15},{9,8},{10,9... | collective-permute-start | bytes 884744 | tf_op jit(solution)/shard_map/ppermute | solution.py:41
  121.1 0.9 constant_dynamic-update-slice_fusion.3
  122.0 0.9 constant_dynamic-update-slice_fusion.2
  122.9 2.9 %collective-permute-done.19 = bf16[128,1152]{1,0:T(8,128)(2,1)S(1)} collective-permute-done((bf16[128,1152]{1,0:T(8,128)(2,1)S(1)}, bf16[128,1152]{1,0:T(8,128)(2,1)S(1)}, u32[]{:S(2)}, u32[]{:S(2)}) %collective-permute-start.19) | collective-permute-done | bytes 294944 | tf_op jit(solution)/shard_map/ppermute | solution.py:41
  127.2 7.8 %shard_map.111 = (f32[256,1152]{1,0:T(8,128)}, f32[1,512]{1,0:T(1,128)}) custom-call(f32[2]{0:T(128)} %pad_maximum_fusion.1.scalars, bf16[256,1152]{1,0:T(8,128)(2,1)} %copy-done.1, bf16[2048,1152]{1,0:T(8,128)(2,1)} %constant_dynamic-update-slice_fusion.texts), custom_call_target="tpu_custom_call" | custom-call | flops 2415919104 | bytes 4718592 | tf_op jit(solution)/shard_map/pallas_call | solution.py:133
  135.5 8.5 %shard_map.112 = (f32[256,1152]{1,0:T(8,128)}, bf16[256,1152]{1,0:T(8,128)(2,1)}, f32[1,512]{1,0:T(1,128)}) custom-call(f32[2]{0:T(128)} %pad_maximum_fusion.1.scalars, bf16[256,1152]{1,0:T(8,128)(2,1)} %copy-done.1, bf16[2048,1152]{1,0:T(8,128)(2,1)} %collective-permute-done.21.texts, f32[256,1152]{1,0:T(8,128)} %get-tuple-element.25.refs_0_), custom_call_target="tpu_custom_call" | custom-call | flops 2415919104 | bytes 4718592 | tf_op jit(solution)/shard_map/pallas_call | solution.py:133
  144.0 1.1 fusion.24
  145.7 3.1 %collective-permute-start.23 = (bf16[64,1152]{1,0:T(8,128)(2,1)S(1)}, bf16[64,1152]{1,0:T(8,128)(2,1)S(1)}, u32[]{:S(2)}, u32[]{:S(2)}) collective-permute-start(bf16[64,1152]{1,0:T(8,128)(2,1)S(1)} %get-tuple-element.38), channel_id=1, source_target_pairs={{0,128},{64,192},{128,0},{192,64},{1,129},{65,193},{129,1},{193,65... | collective-permute-start | bytes 442376 | tf_op jit(solution)/shard_map/ppermute | solution.py:41
  148.8 2.1 collective-permute-start.22
  151.0 2.9 %collective-permute-done.23 = bf16[64,1152]{1,0:T(8,128)(2,1)S(1)} collective-permute-done((bf16[64,1152]{1,0:T(8,128)(2,1)S(1)}, bf16[64,1152]{1,0:T(8,128)(2,1)S(1)}, u32[]{:S(2)}, u32[]{:S(2)}) %collective-permute-start.23) | collective-permute-done | bytes 147488 | tf_op jit(solution)/shard_map/ppermute | solution.py:41
  153.9 2.1 collective-permute-done.22
  156.0 1.2 multiply_reduce_fusion
  157.2 1.1 divide_convert_fusion
  158.6 18.5 %all_to_all.35 = bf16[16,64,288]{2,1,0:T(8,128)(2,1)S(1)} all-to-all(bf16[16,64,288]{2,1,0:T(8,128)(2,1)S(1)} %bitcast.72), channel_id=1, replica_groups=mesh['x'=4,'k'=2,'y'=4,'z'=8] {'x','y'}, dimensions={0} | all-to-all | bytes 1179648 | tf_op jit(solution)/shard_map/all_to_all | solution.py:45
  177.2 1.5 fusion.5
  178.7 1.5 fusion.7
  180.3 1.5 fusion.9
  182.6 2.2 collective-permute-done.25
  185.1 0.8 reshape.102
  186.0 4.6 %all-to-all-start.3 = ((bf16[8,36,538]{2,1,0:T(8,128)(2,1)}), bf16[8,36,538]{2,1,0:T(8,128)(2,1)S(1)}, u32[]{:S(2)}, u32[]{:S(2)}) async-start(bf16[8,36,538]{2,1,0:T(8,128)(2,1)} %reshape.102), calls=%async_computation.3 | async-start | bytes 819200 | tf_op jit(solution)/shard_map/all_to_all | solution.py:45
  191.2 14.7 %all-to-all-done.3 = bf16[8,36,538]{2,1,0:T(8,128)(2,1)S(1)} async-done(((bf16[8,36,538]{2,1,0:T(8,128)(2,1)}), bf16[8,36,538]{2,1,0:T(8,128)(2,1)S(1)}, u32[]{:S(2)}, u32[]{:S(2)}) %all-to-all-start.3) | async-done | bytes 309920 | tf_op jit(solution)/shard_map/all_to_all | solution.py:45
  206.8 8.0 %all_to_all.36 = f32[8,1,37]{2,1,0:T(1,128)S(1)} all-to-all(f32[8,1,37]{2,1,0:T(1,128)S(1)} %broadcast_in_dim.32), channel_id=1, replica_groups=mesh['x'=4,'k'=2,'y'=4,'z'=8] {'x','k'}, dimensions={0} | all-to-all | bytes 2368 | tf_op jit(solution)/shard_map/all_to_all | solution.py:45
  216.3 13.8 %all_to_all.37 = f32[32,1,1077]{2,1,0:T(1,128)S(1)} all-to-all(f32[32,1,1077]{2,1,0:T(1,128)S(1)} %broadcast_in_dim.33), channel_id=1, replica_groups=mesh['x'=4,'k'=2,'y'=4,'z'=8] {'y','z'}, dimensions={0} | all-to-all | bytes 275712 | tf_op jit(solution)/shard_map/all_to_all | solution.py:45
  230.9 1.2 broadcast_in_dim_broadcast_in_dim.3
  232.2 4.7 %all-to-all-start.6 = ((f32[8,1,128]{2,1,0:T(1,128)}), f32[8,1,128]{2,1,0:T(1,128)S(1)}, u32[]{:S(2)}, u32[]{:S(2)}) async-start(f32[8,1,128]{2,1,0:T(1,128)} %broadcast_in_dim_broadcast_in_dim.3), calls=%async_computation.6 | async-start | bytes 8192 | tf_op jit(solution)/shard_map/all_to_all | solution.py:45
  238.1 2.6 %all-to-all-done.6 = f32[8,1,128]{2,1,0:T(1,128)S(1)} async-done(((f32[8,1,128]{2,1,0:T(1,128)}), f32[8,1,128]{2,1,0:T(1,128)S(1)}, u32[]{:S(2)}, u32[]{:S(2)}) %all-to-all-start.6) | async-done | bytes 4128 | tf_op jit(solution)/shard_map/all_to_all | solution.py:45
  (113 shorter events, 20.4 us)
Async XLA Ops:
  2.7 29.6 %collective-permute-start.10 = (bf16[64,1152]{1,0:T(8,128)(2,1)S(1)}, bf16[64,1152]{1,0:T(8,128)(2,1)S(1)}, u32[]{:S(2)}, u32[]{:S(2)}) collective-permute-start(bf16[64,1152]{1,0:T(8,128)(2,1)S(1)} %fusion.3), channel_id=1, source_target_pairs={{0,40},{8,48},{16,56},{24,32},{32,8},{40,16},{48,24},{56,0},{1,41}... | collective-permute-start | bytes 442376 | tf_op jit(solution)/shard_map/ppermute | solution.py:41
  3.8 28.5 %collective-permute-start.11 = (bf16[64,1152]{1,0:T(8,128)(2,1)S(1)}, bf16[64,1152]{1,0:T(8,128)(2,1)S(1)}, u32[]{:S(2)}, u32[]{:S(2)}) collective-permute-start(bf16[64,1152]{1,0:T(8,128)(2,1)S(1)} %fusion.3), channel_id=1, source_target_pairs={{0,48},{8,56},{16,32},{24,40},{32,16},{40,24},{48,0},{56,8},{1,49}... | collective-permute-start | bytes 442376 | tf_op jit(solution)/shard_map/ppermute | solution.py:41
  7.0 25.4 %collective-permute-start.12 = (bf16[64,1152]{1,0:T(8,128)(2,1)S(1)}, bf16[64,1152]{1,0:T(8,128)(2,1)S(1)}, u32[]{:S(2)}, u32[]{:S(2)}) collective-permute-start(bf16[64,1152]{1,0:T(8,128)(2,1)S(1)} %fusion.3), channel_id=1, source_target_pairs={{0,56},{8,32},{16,40},{24,48},{32,24},{40,0},{48,8},{56,16},{1,57}... | collective-permute-start | bytes 442376 | tf_op jit(solution)/shard_map/ppermute | solution.py:41
  10.5 6.8 %collective-permute-start = (bf16[1,64,1076]{2,1,0:T(8,128)(2,1)S(1)}, bf16[1,64,1076]{2,1,0:T(8,128)(2,1)S(1)}, u32[]{:S(2)}, u32[]{:S(2)}) collective-permute-start(bf16[1,64,1076]{2,1,0:T(8,128)(2,1)S(1)} %bitcast.80), channel_id=1, source_target_pairs={{0,64},{64,128},{128,192},{192,0},{1,65},{65,129},{129,193},{193,1... | collective-permute-start | bytes 413192 | tf_op jit(solution)/shard_map/ppermute | solution.py:41
  12.1 1.4 copy-start.5
  12.1 7.8 %collective-permute-start.1 = (bf16[1,64,1076]{2,1,0:T(8,128)(2,1)S(1)}, bf16[1,64,1076]{2,1,0:T(8,128)(2,1)S(1)}, u32[]{:S(2)}, u32[]{:S(2)}) collective-permute-start(bf16[1,64,1076]{2,1,0:T(8,128)(2,1)S(1)} %bitcast.79), channel_id=1, source_target_pairs={{0,128},{64,192},{128,0},{192,64},{1,129},{65,193},{129,1},{193,65... | collective-permute-start | bytes 413192 | tf_op jit(solution)/shard_map/ppermute | solution.py:41
  17.3 5.7 %collective-permute-start.2 = (bf16[1,64,1076]{2,1,0:T(8,128)(2,1)S(1)}, bf16[1,64,1076]{2,1,0:T(8,128)(2,1)S(1)}, u32[]{:S(2)}, u32[]{:S(2)}) collective-permute-start(bf16[1,64,1076]{2,1,0:T(8,128)(2,1)S(1)} %bitcast.81), channel_id=1, source_target_pairs={{0,192},{64,0},{128,64},{192,128},{1,193},{65,1},{129,65},{193,129... | collective-permute-start | bytes 413192 | tf_op jit(solution)/shard_map/ppermute | solution.py:41
  23.8 23.8 %all-to-all-start = ((bf16[8,36,538]{2,1,0:T(8,128)(2,1)}), bf16[8,36,538]{2,1,0:T(8,128)(2,1)S(1)}, u32[]{:S(2)}, u32[]{:S(2)}) async-start(bf16[8,36,538]{2,1,0:T(8,128)(2,1)} %broadcast_in_dim.14), calls=%async_computation | async-start | bytes 819200 | tf_op jit(solution)/shard_map/all_to_all | solution.py:45
  32.4 24.1 %collective-permute-start.13 = (bf16[256,1152]{1,0:T(8,128)(2,1)S(1)}, bf16[256,1152]{1,0:T(8,128)(2,1)S(1)}, u32[]{:S(2)}, u32[]{:S(2)}) collective-permute-start(bf16[256,1152]{1,0:T(8,128)(2,1)S(1)} %constant_dynamic-update-slice_fusion.9), channel_id=1, source_target_pairs={{0,1},{1,2},{2,3},{3,4},{4,5},{5,6},{6,7},{7,0},{8,9},{9,10},{10,1... | collective-permute-start | bytes 1769480 | tf_op jit(solution)/shard_map/ppermute | solution.py:41
  34.5 22.1 %collective-permute-start.14 = (bf16[256,1152]{1,0:T(8,128)(2,1)S(1)}, bf16[256,1152]{1,0:T(8,128)(2,1)S(1)}, u32[]{:S(2)}, u32[]{:S(2)}) collective-permute-start(bf16[256,1152]{1,0:T(8,128)(2,1)S(1)} %constant_dynamic-update-slice_fusion.9), channel_id=1, source_target_pairs={{0,7},{1,0},{2,1},{3,2},{4,3},{5,4},{6,5},{7,6},{8,15},{9,8},{10,9... | collective-permute-start | bytes 1769480 | tf_op jit(solution)/shard_map/ppermute | solution.py:41
  47.7 9.1 %collective-permute-start.3 = (bf16[288,538]{1,0:T(8,128)(2,1)S(1)}, bf16[288,538]{1,0:T(8,128)(2,1)}, u32[]{:S(2)}, u32[]{:S(2)}) collective-permute-start(bf16[288,538]{1,0:T(8,128)(2,1)S(1)} %reshape.89), channel_id=1, source_target_pairs={{0,32},{32,0},{1,33},{33,1},{2,34},{34,2},{3,35},{35,3},{4,36},{36... | collective-permute-start | bytes 929672 | tf_op jit(solution)/shard_map/ppermute | solution.py:41
  48.1 30.9 %collective-permute-start.6 = (bf16[256,1076]{0,1:T(8,128)(2,1)S(1)}, bf16[256,1076]{0,1:T(8,128)(2,1)}, u32[]{:S(2)}, u32[]{:S(2)}) collective-permute-start(bf16[256,1076]{0,1:T(8,128)(2,1)S(1)} %copy.77), channel_id=1, source_target_pairs={{0,8},{8,16},{16,24},{24,0},{1,9},{9,17},{17,25},{25,1},{2,10},{10... | collective-permute-start | bytes 1652744 | tf_op jit(solution)/shard_map/ppermute | solution.py:41
  48.8 26.6 %collective-permute-start.4 = (bf16[256,1076]{0,1:T(8,128)(2,1)S(1)}, bf16[256,1076]{0,1:T(8,128)(2,1)}, u32[]{:S(2)}, u32[]{:S(2)}) collective-permute-start(bf16[256,1076]{0,1:T(8,128)(2,1)S(1)} %copy.77), channel_id=1, source_target_pairs={{0,24},{8,0},{16,8},{24,16},{1,25},{9,1},{17,9},{25,17},{2,26},{10... | collective-permute-start | bytes 1652744 | tf_op jit(solution)/shard_map/ppermute | solution.py:41
  56.5 20.6 %collective-permute-start.5 = (bf16[256,1076]{0,1:T(8,128)(2,1)S(1)}, bf16[256,1076]{0,1:T(8,128)(2,1)}, u32[]{:S(2)}, u32[]{:S(2)}) collective-permute-start(bf16[256,1076]{0,1:T(8,128)(2,1)S(1)} %copy.77), channel_id=1, source_target_pairs={{0,16},{8,24},{16,0},{24,8},{1,17},{9,25},{17,1},{25,9},{2,18},{10... | collective-permute-start | bytes 1652744 | tf_op jit(solution)/shard_map/ppermute | solution.py:41
  56.6 38.4 %collective-permute-start.15 = (bf16[256,1152]{1,0:T(8,128)(2,1)S(1)}, bf16[256,1152]{1,0:T(8,128)(2,1)}, u32[]{:S(2)}, u32[]{:S(2)}) collective-permute-start(bf16[256,1152]{1,0:T(8,128)(2,1)S(1)} %collective-permute-done.13), channel_id=1, source_target_pairs={{0,1},{1,2},{2,3},{3,4},{4,5},{5,6},{6,7},{7,0},{8,9},{9,10},{10,1... | collective-permute-start | bytes 1769480 | tf_op jit(solution)/shard_map/ppermute | solution.py:41
  56.8 38.1 %collective-permute-start.16 = (bf16[256,1152]{1,0:T(8,128)(2,1)S(1)}, bf16[256,1152]{1,0:T(8,128)(2,1)}, u32[]{:S(2)}, u32[]{:S(2)}) collective-permute-start(bf16[256,1152]{1,0:T(8,128)(2,1)S(1)} %collective-permute-done.14), channel_id=1, source_target_pairs={{0,7},{1,0},{2,1},{3,2},{4,3},{5,4},{6,5},{7,6},{8,15},{9,8},{10,9... | collective-permute-start | bytes 1769480 | tf_op jit(solution)/shard_map/ppermute | solution.py:41
  60.9 0.8 copy-start.4
  60.9 14.5 %copy-start.2 = (bf16[288,538]{1,0:T(8,128)(2,1)}, bf16[288,538]{1,0:T(8,128)(2,1)S(1)}, u32[]{:S(2)}) copy-start(bf16[288,538]{1,0:T(8,128)(2,1)S(1)} %get-tuple-element.34) | copy-start | bytes 929668
  77.0 2.0 copy-start.3
  84.6 20.2 %all-to-all-start.1 = ((bf16[16,64,288]{2,1,0:T(8,128)(2,1)}), bf16[16,64,288]{2,1,0:T(8,128)(2,1)S(1)}, u32[]{:S(2)}, u32[]{:S(2)}) async-start(bf16[16,64,288]{2,1,0:T(8,128)(2,1)} %bitcast.11), calls=%async_computation.1 | async-start | bytes 1572864 | tf_op jit(solution)/shard_map/all_to_all | solution.py:45
  95.0 22.7 %collective-permute-start.17 = (bf16[256,1152]{1,0:T(8,128)(2,1)}, bf16[256,1152]{1,0:T(8,128)(2,1)S(1)}, u32[]{:S(2)}, u32[]{:S(2)}) collective-permute-start(bf16[256,1152]{1,0:T(8,128)(2,1)} %collective-permute-done.15), channel_id=1, source_target_pairs={{0,1},{1,2},{2,3},{3,4},{4,5},{5,6},{6,7},{7,0},{8,9},{9,10},{10,1... | collective-permute-start | bytes 1769480 | tf_op jit(solution)/shard_map/ppermute | solution.py:41
  95.7 22.0 %collective-permute-start.18 = (bf16[256,1152]{1,0:T(8,128)(2,1)}, bf16[256,1152]{1,0:T(8,128)(2,1)S(1)}, u32[]{:S(2)}, u32[]{:S(2)}) collective-permute-start(bf16[256,1152]{1,0:T(8,128)(2,1)} %collective-permute-done.16), channel_id=1, source_target_pairs={{0,7},{1,0},{2,1},{3,2},{4,3},{5,4},{6,5},{7,6},{8,15},{9,8},{10,9... | collective-permute-start | bytes 1769480 | tf_op jit(solution)/shard_map/ppermute | solution.py:41
  104.8 0.9 copy-start
  106.0 7.0 %collective-permute-start.7 = (bf16[64,1152]{1,0:T(8,128)(2,1)S(1)}, bf16[64,1152]{1,0:T(8,128)(2,1)S(1)}, u32[]{:S(2)}, u32[]{:S(2)}) collective-permute-start(bf16[64,1152]{1,0:T(8,128)(2,1)S(1)} %fusion.22), channel_id=1, source_target_pairs={{0,64},{64,128},{128,192},{192,0},{1,65},{65,129},{129,193},{193,1... | collective-permute-start | bytes 442376 | tf_op jit(solution)/shard_map/ppermute | solution.py:41
  109.3 6.7 %collective-permute-start.8 = (bf16[64,1152]{1,0:T(8,128)(2,1)S(1)}, bf16[64,1152]{1,0:T(8,128)(2,1)S(1)}, u32[]{:S(2)}, u32[]{:S(2)}) collective-permute-start(bf16[64,1152]{1,0:T(8,128)(2,1)S(1)} %fusion.22), channel_id=1, source_target_pairs={{0,128},{64,192},{128,0},{192,64},{1,129},{65,193},{129,1},{193,65... | collective-permute-start | bytes 442376 | tf_op jit(solution)/shard_map/ppermute | solution.py:41
  112.5 5.2 %collective-permute-start.9 = (bf16[64,1152]{1,0:T(8,128)(2,1)S(1)}, bf16[64,1152]{1,0:T(8,128)(2,1)S(1)}, u32[]{:S(2)}, u32[]{:S(2)}) collective-permute-start(bf16[64,1152]{1,0:T(8,128)(2,1)S(1)} %fusion.22), channel_id=1, source_target_pairs={{0,192},{64,0},{128,64},{192,128},{1,193},{65,1},{129,65},{193,129... | collective-permute-start | bytes 442376 | tf_op jit(solution)/shard_map/ppermute | solution.py:41
  117.7 5.2 %copy-start.1 = (bf16[256,1152]{1,0:T(8,128)(2,1)}, bf16[256,1152]{1,0:T(8,128)(2,1)S(1)}, u32[]{:S(2)}) copy-start(bf16[256,1152]{1,0:T(8,128)(2,1)S(1)} %constant_dynamic-update-slice_fusion.12.images) | copy-start | bytes 1769476
  117.7 8.0 %collective-permute-start.19 = (bf16[128,1152]{1,0:T(8,128)(2,1)S(1)}, bf16[128,1152]{1,0:T(8,128)(2,1)S(1)}, u32[]{:S(2)}, u32[]{:S(2)}) collective-permute-start(bf16[128,1152]{1,0:T(8,128)(2,1)S(1)} %slice.42), channel_id=1, source_target_pairs={{0,1},{1,2},{2,3},{3,4},{4,5},{5,6},{6,7},{7,0},{8,9},{9,10},{10,1... | collective-permute-start | bytes 884744 | tf_op jit(solution)/shard_map/ppermute | solution.py:41
  118.5 7.2 %collective-permute-start.20 = (bf16[128,1152]{1,0:T(8,128)(2,1)S(1)}, bf16[128,1152]{1,0:T(8,128)(2,1)S(1)}, u32[]{:S(2)}, u32[]{:S(2)}) collective-permute-start(bf16[128,1152]{1,0:T(8,128)(2,1)S(1)} %slice.43), channel_id=1, source_target_pairs={{0,7},{1,0},{2,1},{3,2},{4,3},{5,4},{6,5},{7,6},{8,15},{9,8},{10,9... | collective-permute-start | bytes 884744 | tf_op jit(solution)/shard_map/ppermute | solution.py:41
  127.2 8.3 %collective-permute-start.21 = (bf16[2048,1152]{1,0:T(8,128)(2,1)}, bf16[2048,1152]{1,0:T(8,128)(2,1)}, u32[]{:S(2)}, u32[]{:S(2)}) collective-permute-start(bf16[2048,1152]{1,0:T(8,128)(2,1)} %constant_dynamic-update-slice_fusion.texts), channel_id=1, source_target_pairs={{0,32},{32,0},{1,33},{33,1},{2,34},{34,2},{3,35},{35,3},{4,36},{36... | collective-permute-start | bytes 14155784 | tf_op jit(solution)/shard_map/ppermute | solution.py:41
  145.1 6.0 %collective-permute-start.24 = (bf16[64,1152]{1,0:T(8,128)(2,1)S(1)}, bf16[64,1152]{1,0:T(8,128)(2,1)S(1)}, u32[]{:S(2)}, u32[]{:S(2)}) collective-permute-start(bf16[64,1152]{1,0:T(8,128)(2,1)S(1)} %get-tuple-element.37), channel_id=1, source_target_pairs={{0,64},{64,128},{128,192},{192,0},{1,65},{65,129},{129,193},{193,1... | collective-permute-start | bytes 442376 | tf_op jit(solution)/shard_map/ppermute | solution.py:41
  145.7 8.2 %collective-permute-start.23 = (bf16[64,1152]{1,0:T(8,128)(2,1)S(1)}, bf16[64,1152]{1,0:T(8,128)(2,1)S(1)}, u32[]{:S(2)}, u32[]{:S(2)}) collective-permute-start(bf16[64,1152]{1,0:T(8,128)(2,1)S(1)} %get-tuple-element.38), channel_id=1, source_target_pairs={{0,128},{64,192},{128,0},{192,64},{1,129},{65,193},{129,1},{193,65... | collective-permute-start | bytes 442376 | tf_op jit(solution)/shard_map/ppermute | solution.py:41
  148.8 7.2 %collective-permute-start.22 = (bf16[64,1152]{1,0:T(8,128)(2,1)S(1)}, bf16[64,1152]{1,0:T(8,128)(2,1)S(1)}, u32[]{:S(2)}, u32[]{:S(2)}) collective-permute-start(bf16[64,1152]{1,0:T(8,128)(2,1)S(1)} %get-tuple-element.36), channel_id=1, source_target_pairs={{0,192},{64,0},{128,64},{192,128},{1,193},{65,1},{129,65},{193,129... | collective-permute-start | bytes 442376 | tf_op jit(solution)/shard_map/ppermute | solution.py:41
  182.5 2.3 collective-permute-start.25
  185.1 5.5 %copy-start.9 = (f32[1,512]{1,0:T(1,128)S(1)}, f32[1,512]{1,0:T(1,128)}, u32[]{:S(2)}) copy-start(f32[1,512]{1,0:T(1,128)} %get-tuple-element.28) | copy-start | bytes 6148
  185.1 5.5 %copy-start.10 = (f32[1,512]{1,0:T(1,128)S(1)}, f32[1,512]{1,0:T(1,128)}, u32[]{:S(2)}) copy-start(f32[1,512]{1,0:T(1,128)} %get-tuple-element.29) | copy-start | bytes 6148
  185.1 30.3 %copy-start.11 = (f32[36]{0:T(128)S(1)}, f32[36]{0:T(128)}, u32[]{:S(2)}) copy-start(f32[36]{0:T(128)} %param.12) | copy-start | bytes 436
  185.1 45.1 %copy-start.7 = (f32[538]{0:T(1024)S(1)}, f32[538]{0:T(1024)}, u32[]{:S(2)}) copy-start(f32[538]{0:T(1024)} %param.13) | copy-start | bytes 6460
  186.0 20.0 %all-to-all-start.3 = ((bf16[8,36,538]{2,1,0:T(8,128)(2,1)}), bf16[8,36,538]{2,1,0:T(8,128)(2,1)S(1)}, u32[]{:S(2)}, u32[]{:S(2)}) async-start(bf16[8,36,538]{2,1,0:T(8,128)(2,1)} %reshape.102), calls=%async_computation.3 | async-start | bytes 819200 | tf_op jit(solution)/shard_map/all_to_all | solution.py:45
  215.4 26.0 %copy-start.8 = (f32[36]{0:T(128)}, f32[36]{0:T(128)S(1)}, u32[]{:S(2)}) copy-start(f32[36]{0:T(128)S(1)} %multiply_add_fusion) | copy-start | bytes 436
  230.9 10.6 %copy-start.6 = (f32[538]{0:T(1024)}, f32[538]{0:T(1024)S(1)}, u32[]{:S(2)}) copy-start(f32[538]{0:T(1024)S(1)} %get-tuple-element.33) | copy-start | bytes 6460
  232.2 8.5 %all-to-all-start.6 = ((f32[8,1,128]{2,1,0:T(1,128)}), f32[8,1,128]{2,1,0:T(1,128)S(1)}, u32[]{:S(2)}, u32[]{:S(2)}) async-start(f32[8,1,128]{2,1,0:T(1,128)} %broadcast_in_dim_broadcast_in_dim.3), calls=%async_computation.6 | async-start | bytes 8192 | tf_op jit(solution)/shard_map/all_to_all | solution.py:45
